TPU v7x, 256 devices: a whole 4x4x8 slice. The times are simulated.
256 devices in a mesh: tm: 4 (over y), sx: 8 (over x, core), sy: 8 (over z).
Axes of the slice: x: 4, y: 4, z: 8, core: 2. Of those that a mesh axis runs over, the one named last changes fastest.
Arguments:
- iterate: float32 [32, 2048, 2048], P('tm', 'sx', 'sy'), may hold values from -6 to 6
- source: float32 [32, 2048, 2048], P('tm', 'sx', 'sy'), may hold values from -6 to 6
- start_field: float32 [2048, 2048], P('sx', 'sy'), may hold values from -6 to 6
- conduct: float32 [2048, 2048], P('sx', 'sy'), may hold values from 0.2 to 5
Outputs:
- updated: float32 [32, 2048, 2048], P('tm', 'sx', 'sy')
- coarse_residual: float32 [8, 2048, 2048], P('tm', 'sx', 'sy')
All inputs are finite; a program needn't handle non-finite values.
Results may differ from a plain program's by a relative error of at most 0.00002.
Values sent between devices are 32-bit elements; how exact they have to be, the bound alone decides.
No kernel may reach another device: no remote copies, remote signals or barrier semaphores. Data moves between devices by JAX's collectives and lax.ppermute only.
A program may use at most 128 MiB of HBM per device.

v0:
```python
import jax
import jax.numpy as jnp
from jax import lax
from jax.sharding import PartitionSpec as P

FACTOR = 4
SWEEPS = 2


def extended(cells, sides, width):
    for axis, dim in sides:
        count = lax.axis_size(axis)
        ends = count - 1
        head = lax.slice_in_dim(cells, 0, width, axis=dim)
        tail = lax.slice_in_dim(cells, cells.shape[dim] - width, cells.shape[dim], axis=dim)
        cells = jnp.concatenate(
            [
                lax.ppermute(tail, axis, [(i, (i + 1) % count) for i in range(ends)]),
                cells,
                lax.ppermute(head, axis, [((i + 1) % count, i) for i in range(ends)]),
            ],
            axis=dim,
        )
    return cells


def extended_2(shard, sides, width):
    edges = {}
    for axis, dim in sides:
        count, length = (lax.axis_size(axis), shard.shape[dim])
        up = [(i, (i + 1) % count) for i in range(count - 1)]
        last = lax.slice_in_dim(shard, length - width, length, axis=dim)
        initial = lax.slice_in_dim(shard, 0, width, axis=dim)
        edges[dim] = (
            lax.ppermute(last, axis, up),
            lax.ppermute(initial, axis, [(b, a) for a, b in up]),
        )
    done = []
    for _, dim in sides:
        low, high = edges[dim]
        around = [(width, width) if d in done else (0, 0) for d in range(shard.ndim)]
        shard = jnp.concatenate([jnp.pad(low, around), shard, jnp.pad(high, around)], axis=dim)
        done.append(dim)
    return shard


def shifted(shard, axis, by):
    count = lax.axis_size(axis)
    pairs = [(i, i + by) for i in range(count) if 0 <= i + by < count]
    return lax.ppermute(shard, axis, pairs)


def neighbours(padded):
    total = padded[:, 2:, 1:-1] + padded[:, :-2, 1:-1]
    return total + padded[:, 1:-1, 2:] + padded[:, 1:-1, :-2]


def loop_sweeps(rhs_wide, coeff_wide):
    field = rhs_wide
    for sweep in range(SWEEPS):
        trim = sweep + 1
        rhs_part = rhs_wide[:, trim : rhs_wide.shape[1] - trim, trim : rhs_wide.shape[2] - trim]
        coeff_part = coeff_wide[
            :, trim : coeff_wide.shape[1] - trim, trim : coeff_wide.shape[2] - trim
        ]
        field = (rhs_part + coeff_part * neighbours(field)) / (1.0 + 4.0 * coeff_part)
    return field


def fine_step(rhs, coeff):
    rhs_wide, coeff_wide = (
        extended(rhs, (("sx", 1), ("sy", 2)), SWEEPS),
        extended(coeff[None], (("sx", 1), ("sy", 2)), SWEEPS),
    )
    return loop_sweeps(rhs_wide, coeff_wide)


def block_step(rhs, coeff):
    denom = 1.0 + 4.0 * coeff
    field = rhs
    for sweep in range(SWEEPS):
        padded = extended_2(field, (("sx", 1), ("sy", 2)), 1)
        field = (rhs + coeff * neighbours(padded)) / denom
    return field


def restrict(field):
    shape = field.shape
    blocks = field.reshape(shape[0], shape[1] // 2, 2, shape[2] // 2, 2)
    return 0.25 * jnp.sum(blocks, axis=(2, 4))


def prolong(field):
    return jnp.repeat(jnp.repeat(field, 2, axis=1), 2, axis=2)


def shards(iterate, source, start_field, conduct):
    local_steps, rows, cols = iterate.shape
    count = local_steps // FACTOR
    state = iterate.reshape(count, FACTOR, rows, cols)
    forcing = source.reshape(count, FACTOR, rows, cols)
    first_block = lax.axis_index("tm") == 0

    def relax_fine(state):
        earlier = shifted(state[count - 1, FACTOR - 1], "tm", 1)
        opening = jnp.where(first_block, start_field, earlier)
        field = jnp.concatenate([opening[None], state[:-1, FACTOR - 1]], axis=0)
        columns = []
        for place in range(FACTOR - 1):
            field = fine_step(field + forcing[:, place], conduct)
            columns.append(field)
        columns.append(state[:, FACTOR - 1])
        return jnp.stack(columns, axis=1)

    state = relax_fine(state)
    point = fine_step(state[:, FACTOR - 2] + forcing[:, FACTOR - 1], conduct)
    state = state.at[:, FACTOR - 1].set(point)
    state = relax_fine(state)
    resid = fine_step(state[:, FACTOR - 2] + forcing[:, FACTOR - 1], conduct) - state[:, FACTOR - 1]
    coarse_rhs = restrict(resid)
    coarse_coeff = restrict(conduct[None])
    blocks_tm = lax.axis_size("tm")
    half_rows = rows // 2
    incoming = jnp.zeros((1, half_rows, cols // 2), jnp.float32)
    errors = []
    for round_index in range(blocks_tm):
        error = incoming
        errors = []
        for level in range(count):
            error = block_step(error, coarse_coeff[0]) + coarse_rhs[level][None]
            errors.append(error[0])
        if round_index + 1 < blocks_tm:
            incoming = shifted(error, "tm", 1)
    own_errors = jnp.stack(errors, axis=0)
    state = state.at[:, FACTOR - 1].add(prolong(own_errors))
    state = relax_fine(state)
    return (state.reshape(local_steps, rows, cols), resid)


def solution(mesh):
    in_specs = (P("tm", "sx", "sy"), P("tm", "sx", "sy"), P("sx", "sy"), P("sx", "sy"))
    out_specs = (P("tm", "sx", "sy"), P("tm", "sx", "sy"))
    return jax.shard_map(shards, mesh=mesh, in_specs=in_specs, out_specs=out_specs, check_vma=False)
```

profile of v0, /device:TPU:9, one launch (start us, length us, event | category | flops | bytes accessed | tf_op | source)
XLA Modules:
  0.0 609.7 jit_solution(10922590088033074429)
XLA Ops:
  5.8 3.9 collective-permute-start.5
  26.3 4.2 collective-permute-start.3
  32.6 3.9 collective-permute-done.3
  36.5 4.2 collective-permute-done.4
  49.2 4.9 collective-permute-start.11
  55.4 4.8 collective-permute-done.11
  60.2 5.2 collective-permute-done.12
  75.7 4.6 collective-permute-start.15
  81.6 3.6 collective-permute-done.15
  85.2 4.1 collective-permute-done.16
  91.2 4.1 collective-permute-start.17
  105.1 3.6 collective-permute-done.19
  108.6 4.1 collective-permute-done.20
  117.6 7.3 %collective-permute-done.29 = f32[256,256]{1,0:T(8,128)S(1)} collective-permute-done((f32[256,256]{1,0:T(8,128)S(1)}, f32[256,256]{1,0:T(8,128)S(1)}, u32[]{:S(2)}, u32[]{:S(2)}) %collective-permute-start.29) | collective-permute-done | bytes 262176 | tf_op jit(solution)/shard_map/ppermute | solution.py:50
  140.6 4.1 collective-permute-done.33
  158.0 4.1 collective-permute-done.36
  162.1 4.1 collective-permute-done.37
  175.1 4.6 collective-permute-start.24
  181.7 18.1 %reshape_broadcast_in_dim.3 = f32[128,2,128,2]{3,2,1,0:T(8,128)} reshape(f32[256,256]{1,0:T(8,128)S(1)} %copy-done) | data formatting | bytes 524288 | tf_op jit(solution)/shard_map/reshape;broadcast_in_dim | solution.py:89
  199.8 8.0 %reduce_sum.18 = f32[128,128]{1,0:T(8,128)S(1)} reduce(f32[128,2,128,2]{3,2,1,0:T(8,128)} %reshape_broadcast_in_dim.3, f32[]{:T(128)} %constant.71.clone.1), dimensions={1,3}, to_apply=%region_0.1 | reduce | flops 49152 | bytes 327684 | tf_op jit(solution)/shard_map/reduce_sum | solution.py:90
  207.9 3.9 collective-permute-start.22
  221.1 4.1 collective-permute-done.41
  241.6 5.2 collective-permute-start.28
  248.7 3.9 collective-permute-start.26
  255.3 35.6 %reshape.126 = f32[2,128,2,128,2]{4,3,2,1,0:T(8,128)} reshape(f32[2,256,256]{2,1,0:T(8,128)} %fusion.68) | data formatting | bytes 1048576 | tf_op jit(solution)/shard_map/reshape | solution.py:89
  291.0 13.9 %reduce_sum.19 = f32[2,128,128]{2,1,0:T(8,128)} reduce(f32[2,128,2,128,2]{4,3,2,1,0:T(8,128)} %reshape.126, f32[]{:T(128)} %constant.71.clone.1), dimensions={2,4}, to_apply=%region_1.2 | reduce | flops 98304 | bytes 655364 | tf_op jit(solution)/shard_map/reduce_sum | solution.py:90
  308.4 4.0 collective-permute-start.49
  314.3 3.6 collective-permute-start.47
  320.2 4.0 collective-permute-start.53
  326.1 4.7 collective-permute-start.51
  338.0 4.1 collective-permute-start.58
  344.1 5.8 collective-permute-start.56
  352.1 5.0 collective-permute-start.62
  359.1 4.5 collective-permute-start.60
  365.8 5.5 collective-permute-start.66
  373.2 4.5 collective-permute-start.64
  379.9 5.5 collective-permute-start.70
  387.3 4.5 collective-permute-start.68
  399.0 5.5 collective-permute-start.75
  406.4 5.6 collective-permute-start.73
  414.2 5.5 collective-permute-start.79
  421.7 4.5 collective-permute-start.77
  428.3 5.5 collective-permute-start.83
  435.8 4.5 collective-permute-start.81
  442.5 5.5 collective-permute-start.87
  449.9 4.5 collective-permute-start.85
  461.6 5.5 collective-permute-start.92
  469.0 5.6 collective-permute-start.90
  476.8 5.5 collective-permute-start.96
  484.2 4.5 collective-permute-start.94
  489.6 4.9 collective-permute-start.100
  497.7 4.5 collective-permute-start.98
  504.4 6.1 %collective-permute-start.104 = (f32[1,128,1]{2,1,0:T(8,128)S(1)}, f32[1,128,1]{2,1,0:T(8,128)S(1)}, u32[]{:S(2)}, u32[]{:S(2)}) collective-permute-start(f32[1,128,1]{2,1,0:T(8,128)S(1)} %get-tuple-element.87), channel_id=1, source_target_pairs={{0,1},{1,2},{2,3},{3,4},{4,5},{5,6},{6,7},{8,9},{9,10},{10,11},{11... | collective-permute-start | bytes 1544 | tf_op jit(solution)/shard_map/ppermute | solution.py:35
  512.5 4.5 collective-permute-start.102
  528.6 5.5 collective-permute-done.105
  534.2 4.5 collective-permute-start.106
  543.9 4.9 collective-permute-start.108
  553.6 4.1 collective-permute-done.109
  559.6 4.0 collective-permute-start.110
  568.7 4.9 collective-permute-start.112
  574.9 3.6 collective-permute-done.112
  578.5 4.1 collective-permute-done.113
  584.5 3.7 collective-permute-start.114
  601.5 4.1 collective-permute-done.117
  (338 shorter events, 253.3 us)
Async XLA Ops:
  1.9 13.8 %collective-permute-start = (f32[256,256]{1,0:T(8,128)S(1)}, f32[256,256]{1,0:T(8,128)}, u32[]{:S(2)}, u32[]{:S(2)}) collective-permute-start(f32[256,256]{1,0:T(8,128)S(1)} %get-tuple-element.30), channel_id=1, source_target_pairs={{0,64},{64,128},{128,192},{1,65},{65,129},{129,193},{2,66},{66,130... | collective-permute-start | bytes 786440 | tf_op jit(solution)/shard_map/ppermute | solution.py:50
  16.8 9.3 %collective-permute-start.1 = (f32[2,2,256]{2,1,0:T(2,128)S(1)}, f32[2,2,256]{2,1,0:T(2,128)S(1)}, u32[]{:S(2)}, u32[]{:S(2)}) collective-permute-start(f32[2,2,256]{2,1,0:T(2,128)S(1)} %get-tuple-element.80), channel_id=1, source_target_pairs={{0,8},{8,16},{16,24},{24,32},{32,40},{40,48},{48,56},{1,9},{9,17},... | collective-permute-start | bytes 12296 | tf_op jit(solution)/shard_map/ppermute | solution.py:18
  21.2 10.6 %collective-permute-start.7 = (f32[1,260,2]{2,1,0:T(8,128)S(1)}, f32[1,260,2]{2,1,0:T(8,128)S(1)}, u32[]{:S(2)}, u32[]{:S(2)}) collective-permute-start(f32[1,260,2]{2,1,0:T(8,128)S(1)} %get-tuple-element.82), channel_id=1, source_target_pairs={{0,1},{1,2},{2,3},{3,4},{4,5},{5,6},{6,7},{8,9},{9,10},{10,11},{11... | collective-permute-start | bytes 6248 | tf_op jit(solution)/shard_map/ppermute | solution.py:18
  26.3 10.2 %collective-permute-start.3 = (f32[2,260,2]{2,1,0:T(8,128)S(1)}, f32[2,260,2]{2,1,0:T(8,128)S(1)}, u32[]{:S(2)}, u32[]{:S(2)}) collective-permute-start(f32[2,260,2]{2,1,0:T(8,128)S(1)} %get-tuple-element.53), channel_id=1, source_target_pairs={{0,1},{1,2},{2,3},{3,4},{4,5},{5,6},{6,7},{8,9},{9,10},{10,11},{11... | collective-permute-start | bytes 12488 | tf_op jit(solution)/shard_map/ppermute | solution.py:18
  30.5 10.2 %collective-permute-start.4 = (f32[2,260,2]{2,1,0:T(8,128)S(1)}, f32[2,260,2]{2,1,0:T(8,128)S(1)}, u32[]{:S(2)}, u32[]{:S(2)}) collective-permute-start(f32[2,260,2]{2,1,0:T(8,128)S(1)} %get-tuple-element.52), channel_id=1, source_target_pairs={{1,0},{2,1},{3,2},{4,3},{5,4},{6,5},{7,6},{9,8},{10,9},{11,10},{12... | collective-permute-start | bytes 12488 | tf_op jit(solution)/shard_map/ppermute | solution.py:20
  49.2 11.0 %collective-permute-start.11 = (f32[2,260,2]{2,1,0:T(8,128)S(1)}, f32[2,260,2]{2,1,0:T(8,128)S(1)}, u32[]{:S(2)}, u32[]{:S(2)}) collective-permute-start(f32[2,260,2]{2,1,0:T(8,128)S(1)} %get-tuple-element.51), channel_id=1, source_target_pairs={{0,1},{1,2},{2,3},{3,4},{4,5},{5,6},{6,7},{8,9},{9,10},{10,11},{11... | collective-permute-start | bytes 12488 | tf_op jit(solution)/shard_map/ppermute | solution.py:18
  54.1 11.3 %collective-permute-start.12 = (f32[2,260,2]{2,1,0:T(8,128)S(1)}, f32[2,260,2]{2,1,0:T(8,128)S(1)}, u32[]{:S(2)}, u32[]{:S(2)}) collective-permute-start(f32[2,260,2]{2,1,0:T(8,128)S(1)} %get-tuple-element.50), channel_id=1, source_target_pairs={{1,0},{2,1},{3,2},{4,3},{5,4},{6,5},{7,6},{9,8},{10,9},{11,10},{12... | collective-permute-start | bytes 12488 | tf_op jit(solution)/shard_map/ppermute | solution.py:20
  75.7 9.5 %collective-permute-start.15 = (f32[2,260,2]{2,1,0:T(8,128)S(1)}, f32[2,260,2]{2,1,0:T(8,128)S(1)}, u32[]{:S(2)}, u32[]{:S(2)}) collective-permute-start(f32[2,260,2]{2,1,0:T(8,128)S(1)} %get-tuple-element.49), channel_id=1, source_target_pairs={{0,1},{1,2},{2,3},{3,4},{4,5},{5,6},{6,7},{8,9},{9,10},{10,11},{11... | collective-permute-start | bytes 12488 | tf_op jit(solution)/shard_map/ppermute | solution.py:18
  80.3 9.0 %collective-permute-start.16 = (f32[2,260,2]{2,1,0:T(8,128)S(1)}, f32[2,260,2]{2,1,0:T(8,128)S(1)}, u32[]{:S(2)}, u32[]{:S(2)}) collective-permute-start(f32[2,260,2]{2,1,0:T(8,128)S(1)} %get-tuple-element.48), channel_id=1, source_target_pairs={{1,0},{2,1},{3,2},{4,3},{5,4},{6,5},{7,6},{9,8},{10,9},{11,10},{12... | collective-permute-start | bytes 12488 | tf_op jit(solution)/shard_map/ppermute | solution.py:20
  100.4 8.2 %collective-permute-start.19 = (f32[2,260,2]{2,1,0:T(8,128)S(1)}, f32[2,260,2]{2,1,0:T(8,128)S(1)}, u32[]{:S(2)}, u32[]{:S(2)}) collective-permute-start(f32[2,260,2]{2,1,0:T(8,128)S(1)} %get-tuple-element.47), channel_id=1, source_target_pairs={{0,1},{1,2},{2,3},{3,4},{4,5},{5,6},{6,7},{8,9},{9,10},{10,11},{11... | collective-permute-start | bytes 12488 | tf_op jit(solution)/shard_map/ppermute | solution.py:18
  103.8 9.0 %collective-permute-start.20 = (f32[2,260,2]{2,1,0:T(8,128)S(1)}, f32[2,260,2]{2,1,0:T(8,128)S(1)}, u32[]{:S(2)}, u32[]{:S(2)}) collective-permute-start(f32[2,260,2]{2,1,0:T(8,128)S(1)} %get-tuple-element.46), channel_id=1, source_target_pairs={{1,0},{2,1},{3,2},{4,3},{5,4},{6,5},{7,6},{9,8},{10,9},{11,10},{12... | collective-permute-start | bytes 12488 | tf_op jit(solution)/shard_map/ppermute | solution.py:20
  114.7 10.2 %collective-permute-start.29 = (f32[256,256]{1,0:T(8,128)S(1)}, f32[256,256]{1,0:T(8,128)S(1)}, u32[]{:S(2)}, u32[]{:S(2)}) collective-permute-start(f32[256,256]{1,0:T(8,128)S(1)} %get-tuple-element.72), channel_id=1, source_target_pairs={{0,64},{64,128},{128,192},{1,65},{65,129},{129,193},{2,66},{66,130... | collective-permute-start | bytes 786440 | tf_op jit(solution)/shard_map/ppermute | solution.py:50
  132.5 8.0 %collective-permute-start.32 = (f32[2,260,2]{2,1,0:T(8,128)S(1)}, f32[2,260,2]{2,1,0:T(8,128)S(1)}, u32[]{:S(2)}, u32[]{:S(2)}) collective-permute-start(f32[2,260,2]{2,1,0:T(8,128)S(1)} %get-tuple-element.45), channel_id=1, source_target_pairs={{0,1},{1,2},{2,3},{3,4},{4,5},{5,6},{6,7},{8,9},{9,10},{10,11},{11... | collective-permute-start | bytes 12488 | tf_op jit(solution)/shard_map/ppermute | solution.py:18
  135.6 9.1 %collective-permute-start.33 = (f32[2,260,2]{2,1,0:T(8,128)S(1)}, f32[2,260,2]{2,1,0:T(8,128)S(1)}, u32[]{:S(2)}, u32[]{:S(2)}) collective-permute-start(f32[2,260,2]{2,1,0:T(8,128)S(1)} %get-tuple-element.44), channel_id=1, source_target_pairs={{1,0},{2,1},{3,2},{4,3},{5,4},{6,5},{7,6},{9,8},{10,9},{11,10},{12... | collective-permute-start | bytes 12488 | tf_op jit(solution)/shard_map/ppermute | solution.py:20
  153.6 8.5 %collective-permute-start.36 = (f32[2,260,2]{2,1,0:T(8,128)S(1)}, f32[2,260,2]{2,1,0:T(8,128)S(1)}, u32[]{:S(2)}, u32[]{:S(2)}) collective-permute-start(f32[2,260,2]{2,1,0:T(8,128)S(1)} %get-tuple-element.43), channel_id=1, source_target_pairs={{0,1},{1,2},{2,3},{3,4},{4,5},{5,6},{6,7},{8,9},{9,10},{10,11},{11... | collective-permute-start | bytes 12488 | tf_op jit(solution)/shard_map/ppermute | solution.py:18
  156.7 9.5 %collective-permute-start.37 = (f32[2,260,2]{2,1,0:T(8,128)S(1)}, f32[2,260,2]{2,1,0:T(8,128)S(1)}, u32[]{:S(2)}, u32[]{:S(2)}) collective-permute-start(f32[2,260,2]{2,1,0:T(8,128)S(1)} %get-tuple-element.42), channel_id=1, source_target_pairs={{1,0},{2,1},{3,2},{4,3},{5,4},{6,5},{7,6},{9,8},{10,9},{11,10},{12... | collective-permute-start | bytes 12488 | tf_op jit(solution)/shard_map/ppermute | solution.py:20
  168.9 39.0 %collective-permute-start.38 = (f32[2,2,256]{2,1,0:T(2,128)S(1)}, f32[2,2,256]{2,1,0:T(2,128)S(1)}, u32[]{:S(2)}, u32[]{:S(2)}) collective-permute-start(f32[2,2,256]{2,1,0:T(2,128)S(1)} %get-tuple-element.66), channel_id=1, source_target_pairs={{0,8},{8,16},{16,24},{24,32},{32,40},{40,48},{48,56},{1,9},{9,17},... | collective-permute-start | bytes 12296 | tf_op jit(solution)/shard_map/ppermute | solution.py:18
  170.8 40.9 %collective-permute-start.39 = (f32[2,2,256]{2,1,0:T(2,128)S(1)}, f32[2,2,256]{2,1,0:T(2,128)S(1)}, u32[]{:S(2)}, u32[]{:S(2)}) collective-permute-start(f32[2,2,256]{2,1,0:T(2,128)S(1)} %get-tuple-element.67), channel_id=1, source_target_pairs={{8,0},{16,8},{24,16},{32,24},{40,32},{48,40},{56,48},{9,1},{17,9},... | collective-permute-start | bytes 12296 | tf_op jit(solution)/shard_map/ppermute | solution.py:20
  173.8 41.8 %collective-permute-start.23 = (f32[1,128,1]{2,1,0:T(8,128)}, f32[1,128,1]{2,1,0:T(8,128)}, u32[]{:S(2)}, u32[]{:S(2)}) collective-permute-start(f32[1,128,1]{2,1,0:T(8,128)} %broadcast.148), channel_id=1, source_target_pairs={{1,0},{2,1},{3,2},{4,3},{5,4},{6,5},{7,6},{9,8},{10,9},{11,10},{12... | collective-permute-start | bytes 1544 | tf_op jit(solution)/shard_map/ppermute | solution.py:36
  175.1 41.9 %collective-permute-start.24 = (f32[1,128,1]{2,1,0:T(8,128)}, f32[1,128,1]{2,1,0:T(8,128)}, u32[]{:S(2)}, u32[]{:S(2)}) collective-permute-start(f32[1,128,1]{2,1,0:T(8,128)} %broadcast.148), channel_id=1, source_target_pairs={{0,1},{1,2},{2,3},{3,4},{4,5},{5,6},{6,7},{8,9},{9,10},{10,11},{11... | collective-permute-start | bytes 1544 | tf_op jit(solution)/shard_map/ppermute | solution.py:35
  179.8 37.2 %collective-permute-start.21 = (f32[1,1,128]{2,1,0:T(1,128)S(1)}, f32[1,1,128]{2,1,0:T(1,128)S(1)}, u32[]{:S(2)}, u32[]{:S(2)}) collective-permute-start(f32[1,1,128]{2,1,0:T(1,128)S(1)} %broadcast.147), channel_id=1, source_target_pairs={{8,0},{16,8},{24,16},{32,24},{40,32},{48,40},{56,48},{9,1},{17,9},... | collective-permute-start | bytes 1544 | tf_op jit(solution)/shard_map/ppermute | solution.py:36
  207.9 9.2 %collective-permute-start.22 = (f32[1,1,128]{2,1,0:T(1,128)S(1)}, f32[1,1,128]{2,1,0:T(1,128)S(1)}, u32[]{:S(2)}, u32[]{:S(2)}) collective-permute-start(f32[1,1,128]{2,1,0:T(1,128)S(1)} %broadcast.147), channel_id=1, source_target_pairs={{0,8},{8,16},{16,24},{24,32},{32,40},{40,48},{48,56},{1,9},{9,17},... | collective-permute-start | bytes 1544 | tf_op jit(solution)/shard_map/ppermute | solution.py:35
  212.9 8.2 %collective-permute-start.40 = (f32[2,260,2]{2,1,0:T(8,128)S(1)}, f32[2,260,2]{2,1,0:T(8,128)S(1)}, u32[]{:S(2)}, u32[]{:S(2)}) collective-permute-start(f32[2,260,2]{2,1,0:T(8,128)S(1)} %get-tuple-element.41), channel_id=1, source_target_pairs={{0,1},{1,2},{2,3},{3,4},{4,5},{5,6},{6,7},{8,9},{9,10},{10,11},{11... | collective-permute-start | bytes 12488 | tf_op jit(solution)/shard_map/ppermute | solution.py:18
  215.7 9.5 %collective-permute-start.41 = (f32[2,260,2]{2,1,0:T(8,128)S(1)}, f32[2,260,2]{2,1,0:T(8,128)S(1)}, u32[]{:S(2)}, u32[]{:S(2)}) collective-permute-start(f32[2,260,2]{2,1,0:T(8,128)S(1)} %get-tuple-element.40), channel_id=1, source_target_pairs={{1,0},{2,1},{3,2},{4,3},{5,4},{6,5},{7,6},{9,8},{10,9},{11,10},{12... | collective-permute-start | bytes 12488 | tf_op jit(solution)/shard_map/ppermute | solution.py:20
  235.4 13.3 %collective-permute-start.44 = (f32[2,260,2]{2,1,0:T(8,128)S(1)}, f32[2,260,2]{2,1,0:T(8,128)S(1)}, u32[]{:S(2)}, u32[]{:S(2)}) collective-permute-start(f32[2,260,2]{2,1,0:T(8,128)S(1)} %get-tuple-element.39), channel_id=1, source_target_pairs={{0,1},{1,2},{2,3},{3,4},{4,5},{5,6},{6,7},{8,9},{9,10},{10,11},{11... | collective-permute-start | bytes 12488 | tf_op jit(solution)/shard_map/ppermute | solution.py:18
  239.0 13.6 %collective-permute-start.45 = (f32[2,260,2]{2,1,0:T(8,128)S(1)}, f32[2,260,2]{2,1,0:T(8,128)S(1)}, u32[]{:S(2)}, u32[]{:S(2)}) collective-permute-start(f32[2,260,2]{2,1,0:T(8,128)S(1)} %get-tuple-element.38), channel_id=1, source_target_pairs={{1,0},{2,1},{3,2},{4,3},{5,4},{6,5},{7,6},{9,8},{10,9},{11,10},{12... | collective-permute-start | bytes 12488 | tf_op jit(solution)/shard_map/ppermute | solution.py:20
  240.3 65.5 %collective-permute-start.27 = (f32[1,128,1]{2,1,0:T(8,128)}, f32[1,128,1]{2,1,0:T(8,128)}, u32[]{:S(2)}, u32[]{:S(2)}) collective-permute-start(f32[1,128,1]{2,1,0:T(8,128)} %get-tuple-element.142), channel_id=1, source_target_pairs={{1,0},{2,1},{3,2},{4,3},{5,4},{6,5},{7,6},{9,8},{10,9},{11,10},{12... | collective-permute-start | bytes 1544 | tf_op jit(solution)/shard_map/ppermute | solution.py:36
  241.6 64.2 %collective-permute-start.28 = (f32[1,128,1]{2,1,0:T(8,128)}, f32[1,128,1]{2,1,0:T(8,128)}, u32[]{:S(2)}, u32[]{:S(2)}) collective-permute-start(f32[1,128,1]{2,1,0:T(8,128)} %get-tuple-element.143), channel_id=1, source_target_pairs={{0,1},{1,2},{2,3},{3,4},{4,5},{5,6},{6,7},{8,9},{9,10},{10,11},{11... | collective-permute-start | bytes 1544 | tf_op jit(solution)/shard_map/ppermute | solution.py:35
  246.8 59.0 %collective-permute-start.25 = (f32[1,1,128]{2,1,0:T(1,128)S(1)}, f32[1,1,128]{2,1,0:T(1,128)S(1)}, u32[]{:S(2)}, u32[]{:S(2)}) collective-permute-start(f32[1,1,128]{2,1,0:T(1,128)S(1)} %get-tuple-element.145), channel_id=1, source_target_pairs={{8,0},{16,8},{24,16},{32,24},{40,32},{48,40},{56,48},{9,1},{17,9},... | collective-permute-start | bytes 1544 | tf_op jit(solution)/shard_map/ppermute | solution.py:36
  248.7 57.1 %collective-permute-start.26 = (f32[1,1,128]{2,1,0:T(1,128)S(1)}, f32[1,1,128]{2,1,0:T(1,128)S(1)}, u32[]{:S(2)}, u32[]{:S(2)}) collective-permute-start(f32[1,1,128]{2,1,0:T(1,128)S(1)} %get-tuple-element.144), channel_id=1, source_target_pairs={{0,8},{8,16},{16,24},{24,32},{32,40},{40,48},{48,56},{1,9},{9,17},... | collective-permute-start | bytes 1544 | tf_op jit(solution)/shard_map/ppermute | solution.py:35
  307.1 10.9 %collective-permute-start.48 = (f32[1,128,1]{2,1,0:T(8,128)S(1)}, f32[1,128,1]{2,1,0:T(8,128)S(1)}, u32[]{:S(2)}, u32[]{:S(2)}) collective-permute-start(f32[1,128,1]{2,1,0:T(8,128)S(1)} %get-tuple-element.138), channel_id=1, source_target_pairs={{1,0},{2,1},{3,2},{4,3},{5,4},{6,5},{7,6},{9,8},{10,9},{11,10},{12... | collective-permute-start | bytes 1544 | tf_op jit(solution)/shard_map/ppermute | solution.py:36
  308.4 9.6 %collective-permute-start.49 = (f32[1,128,1]{2,1,0:T(8,128)S(1)}, f32[1,128,1]{2,1,0:T(8,128)S(1)}, u32[]{:S(2)}, u32[]{:S(2)}) collective-permute-start(f32[1,128,1]{2,1,0:T(8,128)S(1)} %get-tuple-element.139), channel_id=1, source_target_pairs={{0,1},{1,2},{2,3},{3,4},{4,5},{5,6},{6,7},{8,9},{9,10},{10,11},{11... | collective-permute-start | bytes 1544 | tf_op jit(solution)/shard_map/ppermute | solution.py:35
  318.9 12.0 %collective-permute-start.52 = (f32[1,128,1]{2,1,0:T(8,128)S(1)}, f32[1,128,1]{2,1,0:T(8,128)S(1)}, u32[]{:S(2)}, u32[]{:S(2)}) collective-permute-start(f32[1,128,1]{2,1,0:T(8,128)S(1)} %get-tuple-element.134), channel_id=1, source_target_pairs={{1,0},{2,1},{3,2},{4,3},{5,4},{6,5},{7,6},{9,8},{10,9},{11,10},{12... | collective-permute-start | bytes 1544 | tf_op jit(solution)/shard_map/ppermute | solution.py:36
  320.2 10.7 %collective-permute-start.53 = (f32[1,128,1]{2,1,0:T(8,128)S(1)}, f32[1,128,1]{2,1,0:T(8,128)S(1)}, u32[]{:S(2)}, u32[]{:S(2)}) collective-permute-start(f32[1,128,1]{2,1,0:T(8,128)S(1)} %get-tuple-element.135), channel_id=1, source_target_pairs={{0,1},{1,2},{2,3},{3,4},{4,5},{5,6},{6,7},{8,9},{9,10},{10,11},{11... | collective-permute-start | bytes 1544 | tf_op jit(solution)/shard_map/ppermute | solution.py:35
  336.8 13.1 %collective-permute-start.57 = (f32[1,128,1]{2,1,0:T(8,128)S(1)}, f32[1,128,1]{2,1,0:T(8,128)S(1)}, u32[]{:S(2)}, u32[]{:S(2)}) collective-permute-start(f32[1,128,1]{2,1,0:T(8,128)S(1)} %get-tuple-element.130), channel_id=1, source_target_pairs={{1,0},{2,1},{3,2},{4,3},{5,4},{6,5},{7,6},{9,8},{10,9},{11,10},{12... | collective-permute-start | bytes 1544 | tf_op jit(solution)/shard_map/ppermute | solution.py:36
  338.0 11.8 %collective-permute-start.58 = (f32[1,128,1]{2,1,0:T(8,128)S(1)}, f32[1,128,1]{2,1,0:T(8,128)S(1)}, u32[]{:S(2)}, u32[]{:S(2)}) collective-permute-start(f32[1,128,1]{2,1,0:T(8,128)S(1)} %get-tuple-element.131), channel_id=1, source_target_pairs={{0,1},{1,2},{2,3},{3,4},{4,5},{5,6},{6,7},{8,9},{9,10},{10,11},{11... | collective-permute-start | bytes 1544 | tf_op jit(solution)/shard_map/ppermute | solution.py:35
  350.8 12.7 %collective-permute-start.61 = (f32[1,128,1]{2,1,0:T(8,128)S(1)}, f32[1,128,1]{2,1,0:T(8,128)S(1)}, u32[]{:S(2)}, u32[]{:S(2)}) collective-permute-start(f32[1,128,1]{2,1,0:T(8,128)S(1)} %get-tuple-element.126), channel_id=1, source_target_pairs={{1,0},{2,1},{3,2},{4,3},{5,4},{6,5},{7,6},{9,8},{10,9},{11,10},{12... | collective-permute-start | bytes 1544 | tf_op jit(solution)/shard_map/ppermute | solution.py:36
  352.1 11.4 %collective-permute-start.62 = (f32[1,128,1]{2,1,0:T(8,128)S(1)}, f32[1,128,1]{2,1,0:T(8,128)S(1)}, u32[]{:S(2)}, u32[]{:S(2)}) collective-permute-start(f32[1,128,1]{2,1,0:T(8,128)S(1)} %get-tuple-element.127), channel_id=1, source_target_pairs={{0,1},{1,2},{2,3},{3,4},{4,5},{5,6},{6,7},{8,9},{9,10},{10,11},{11... | collective-permute-start | bytes 1544 | tf_op jit(solution)/shard_map/ppermute | solution.py:35
  364.5 13.2 %collective-permute-start.65 = (f32[1,128,1]{2,1,0:T(8,128)S(1)}, f32[1,128,1]{2,1,0:T(8,128)S(1)}, u32[]{:S(2)}, u32[]{:S(2)}) collective-permute-start(f32[1,128,1]{2,1,0:T(8,128)S(1)} %get-tuple-element.122), channel_id=1, source_target_pairs={{1,0},{2,1},{3,2},{4,3},{5,4},{6,5},{7,6},{9,8},{10,9},{11,10},{12... | collective-permute-start | bytes 1544 | tf_op jit(solution)/shard_map/ppermute | solution.py:36
  365.8 11.9 %collective-permute-start.66 = (f32[1,128,1]{2,1,0:T(8,128)S(1)}, f32[1,128,1]{2,1,0:T(8,128)S(1)}, u32[]{:S(2)}, u32[]{:S(2)}) collective-permute-start(f32[1,128,1]{2,1,0:T(8,128)S(1)} %get-tuple-element.123), channel_id=1, source_target_pairs={{0,1},{1,2},{2,3},{3,4},{4,5},{5,6},{6,7},{8,9},{9,10},{10,11},{11... | collective-permute-start | bytes 1544 | tf_op jit(solution)/shard_map/ppermute | solution.py:35
  378.6 13.2 %collective-permute-start.69 = (f32[1,128,1]{2,1,0:T(8,128)S(1)}, f32[1,128,1]{2,1,0:T(8,128)S(1)}, u32[]{:S(2)}, u32[]{:S(2)}) collective-permute-start(f32[1,128,1]{2,1,0:T(8,128)S(1)} %get-tuple-element.118), channel_id=1, source_target_pairs={{1,0},{2,1},{3,2},{4,3},{5,4},{6,5},{7,6},{9,8},{10,9},{11,10},{12... | collective-permute-start | bytes 1544 | tf_op jit(solution)/shard_map/ppermute | solution.py:36
  379.9 11.9 %collective-permute-start.70 = (f32[1,128,1]{2,1,0:T(8,128)S(1)}, f32[1,128,1]{2,1,0:T(8,128)S(1)}, u32[]{:S(2)}, u32[]{:S(2)}) collective-permute-start(f32[1,128,1]{2,1,0:T(8,128)S(1)} %get-tuple-element.119), channel_id=1, source_target_pairs={{0,1},{1,2},{2,3},{3,4},{4,5},{5,6},{6,7},{8,9},{9,10},{10,11},{11... | collective-permute-start | bytes 1544 | tf_op jit(solution)/shard_map/ppermute | solution.py:35
  397.7 14.3 %collective-permute-start.74 = (f32[1,128,1]{2,1,0:T(8,128)S(1)}, f32[1,128,1]{2,1,0:T(8,128)S(1)}, u32[]{:S(2)}, u32[]{:S(2)}) collective-permute-start(f32[1,128,1]{2,1,0:T(8,128)S(1)} %get-tuple-element.114), channel_id=1, source_target_pairs={{1,0},{2,1},{3,2},{4,3},{5,4},{6,5},{7,6},{9,8},{10,9},{11,10},{12... | collective-permute-start | bytes 1544 | tf_op jit(solution)/shard_map/ppermute | solution.py:36
  399.0 13.1 %collective-permute-start.75 = (f32[1,128,1]{2,1,0:T(8,128)S(1)}, f32[1,128,1]{2,1,0:T(8,128)S(1)}, u32[]{:S(2)}, u32[]{:S(2)}) collective-permute-start(f32[1,128,1]{2,1,0:T(8,128)S(1)} %get-tuple-element.115), channel_id=1, source_target_pairs={{0,1},{1,2},{2,3},{3,4},{4,5},{5,6},{6,7},{8,9},{9,10},{10,11},{11... | collective-permute-start | bytes 1544 | tf_op jit(solution)/shard_map/ppermute | solution.py:35
  412.9 13.2 %collective-permute-start.78 = (f32[1,128,1]{2,1,0:T(8,128)S(1)}, f32[1,128,1]{2,1,0:T(8,128)S(1)}, u32[]{:S(2)}, u32[]{:S(2)}) collective-permute-start(f32[1,128,1]{2,1,0:T(8,128)S(1)} %get-tuple-element.110), channel_id=1, source_target_pairs={{1,0},{2,1},{3,2},{4,3},{5,4},{6,5},{7,6},{9,8},{10,9},{11,10},{12... | collective-permute-start | bytes 1544 | tf_op jit(solution)/shard_map/ppermute | solution.py:36
  414.2 11.9 %collective-permute-start.79 = (f32[1,128,1]{2,1,0:T(8,128)S(1)}, f32[1,128,1]{2,1,0:T(8,128)S(1)}, u32[]{:S(2)}, u32[]{:S(2)}) collective-permute-start(f32[1,128,1]{2,1,0:T(8,128)S(1)} %get-tuple-element.111), channel_id=1, source_target_pairs={{0,1},{1,2},{2,3},{3,4},{4,5},{5,6},{6,7},{8,9},{9,10},{10,11},{11... | collective-permute-start | bytes 1544 | tf_op jit(solution)/shard_map/ppermute | solution.py:35
  427.0 13.2 %collective-permute-start.82 = (f32[1,128,1]{2,1,0:T(8,128)S(1)}, f32[1,128,1]{2,1,0:T(8,128)S(1)}, u32[]{:S(2)}, u32[]{:S(2)}) collective-permute-start(f32[1,128,1]{2,1,0:T(8,128)S(1)} %get-tuple-element.106), channel_id=1, source_target_pairs={{1,0},{2,1},{3,2},{4,3},{5,4},{6,5},{7,6},{9,8},{10,9},{11,10},{12... | collective-permute-start | bytes 1544 | tf_op jit(solution)/shard_map/ppermute | solution.py:36
  428.3 11.9 %collective-permute-start.83 = (f32[1,128,1]{2,1,0:T(8,128)S(1)}, f32[1,128,1]{2,1,0:T(8,128)S(1)}, u32[]{:S(2)}, u32[]{:S(2)}) collective-permute-start(f32[1,128,1]{2,1,0:T(8,128)S(1)} %get-tuple-element.107), channel_id=1, source_target_pairs={{0,1},{1,2},{2,3},{3,4},{4,5},{5,6},{6,7},{8,9},{9,10},{10,11},{11... | collective-permute-start | bytes 1544 | tf_op jit(solution)/shard_map/ppermute | solution.py:35
  441.2 13.2 %collective-permute-start.86 = (f32[1,128,1]{2,1,0:T(8,128)S(1)}, f32[1,128,1]{2,1,0:T(8,128)S(1)}, u32[]{:S(2)}, u32[]{:S(2)}) collective-permute-start(f32[1,128,1]{2,1,0:T(8,128)S(1)} %get-tuple-element.102), channel_id=1, source_target_pairs={{1,0},{2,1},{3,2},{4,3},{5,4},{6,5},{7,6},{9,8},{10,9},{11,10},{12... | collective-permute-start | bytes 1544 | tf_op jit(solution)/shard_map/ppermute | solution.py:36
  442.5 11.9 %collective-permute-start.87 = (f32[1,128,1]{2,1,0:T(8,128)S(1)}, f32[1,128,1]{2,1,0:T(8,128)S(1)}, u32[]{:S(2)}, u32[]{:S(2)}) collective-permute-start(f32[1,128,1]{2,1,0:T(8,128)S(1)} %get-tuple-element.103), channel_id=1, source_target_pairs={{0,1},{1,2},{2,3},{3,4},{4,5},{5,6},{6,7},{8,9},{9,10},{10,11},{11... | collective-permute-start | bytes 1544 | tf_op jit(solution)/shard_map/ppermute | solution.py:35
  460.3 14.3 %collective-permute-start.91 = (f32[1,128,1]{2,1,0:T(8,128)S(1)}, f32[1,128,1]{2,1,0:T(8,128)S(1)}, u32[]{:S(2)}, u32[]{:S(2)}) collective-permute-start(f32[1,128,1]{2,1,0:T(8,128)S(1)} %get-tuple-element.98), channel_id=1, source_target_pairs={{1,0},{2,1},{3,2},{4,3},{5,4},{6,5},{7,6},{9,8},{10,9},{11,10},{12... | collective-permute-start | bytes 1544 | tf_op jit(solution)/shard_map/ppermute | solution.py:36
  461.6 13.1 %collective-permute-start.92 = (f32[1,128,1]{2,1,0:T(8,128)S(1)}, f32[1,128,1]{2,1,0:T(8,128)S(1)}, u32[]{:S(2)}, u32[]{:S(2)}) collective-permute-start(f32[1,128,1]{2,1,0:T(8,128)S(1)} %get-tuple-element.99), channel_id=1, source_target_pairs={{0,1},{1,2},{2,3},{3,4},{4,5},{5,6},{6,7},{8,9},{9,10},{10,11},{11... | collective-permute-start | bytes 1544 | tf_op jit(solution)/shard_map/ppermute | solution.py:35
  475.5 13.2 %collective-permute-start.95 = (f32[1,128,1]{2,1,0:T(8,128)S(1)}, f32[1,128,1]{2,1,0:T(8,128)S(1)}, u32[]{:S(2)}, u32[]{:S(2)}) collective-permute-start(f32[1,128,1]{2,1,0:T(8,128)S(1)} %get-tuple-element.94), channel_id=1, source_target_pairs={{1,0},{2,1},{3,2},{4,3},{5,4},{6,5},{7,6},{9,8},{10,9},{11,10},{12... | collective-permute-start | bytes 1544 | tf_op jit(solution)/shard_map/ppermute | solution.py:36
  476.8 11.9 %collective-permute-start.96 = (f32[1,128,1]{2,1,0:T(8,128)S(1)}, f32[1,128,1]{2,1,0:T(8,128)S(1)}, u32[]{:S(2)}, u32[]{:S(2)}) collective-permute-start(f32[1,128,1]{2,1,0:T(8,128)S(1)} %get-tuple-element.95), channel_id=1, source_target_pairs={{0,1},{1,2},{2,3},{3,4},{4,5},{5,6},{6,7},{8,9},{9,10},{10,11},{11... | collective-permute-start | bytes 1544 | tf_op jit(solution)/shard_map/ppermute | solution.py:35
  489.6 12.6 %collective-permute-start.100 = (f32[1,128,1]{2,1,0:T(8,128)S(1)}, f32[1,128,1]{2,1,0:T(8,128)S(1)}, u32[]{:S(2)}, u32[]{:S(2)}) collective-permute-start(f32[1,128,1]{2,1,0:T(8,128)S(1)} %get-tuple-element.91), channel_id=1, source_target_pairs={{0,1},{1,2},{2,3},{3,4},{4,5},{5,6},{6,7},{8,9},{9,10},{10,11},{11... | collective-permute-start | bytes 1544 | tf_op jit(solution)/shard_map/ppermute | solution.py:35
  503.1 13.8 %collective-permute-start.103 = (f32[1,128,1]{2,1,0:T(8,128)S(1)}, f32[1,128,1]{2,1,0:T(8,128)S(1)}, u32[]{:S(2)}, u32[]{:S(2)}) collective-permute-start(f32[1,128,1]{2,1,0:T(8,128)S(1)} %get-tuple-element.86), channel_id=1, source_target_pairs={{1,0},{2,1},{3,2},{4,3},{5,4},{6,5},{7,6},{9,8},{10,9},{11,10},{12... | collective-permute-start | bytes 1544 | tf_op jit(solution)/shard_map/ppermute | solution.py:36
  504.4 12.5 %collective-permute-start.104 = (f32[1,128,1]{2,1,0:T(8,128)S(1)}, f32[1,128,1]{2,1,0:T(8,128)S(1)}, u32[]{:S(2)}, u32[]{:S(2)}) collective-permute-start(f32[1,128,1]{2,1,0:T(8,128)S(1)} %get-tuple-element.87), channel_id=1, source_target_pairs={{0,1},{1,2},{2,3},{3,4},{4,5},{5,6},{6,7},{8,9},{9,10},{10,11},{11... | collective-permute-start | bytes 1544 | tf_op jit(solution)/shard_map/ppermute | solution.py:35
  525.7 8.4 %collective-permute-start.105 = (f32[256,256]{1,0:T(8,128)S(1)}, f32[256,256]{1,0:T(8,128)S(1)}, u32[]{:S(2)}, u32[]{:S(2)}) collective-permute-start(f32[256,256]{1,0:T(8,128)S(1)} %get-tuple-element.62), channel_id=1, source_target_pairs={{0,64},{64,128},{128,192},{1,65},{65,129},{129,193},{2,66},{66,130... | collective-permute-start | bytes 786440 | tf_op jit(solution)/shard_map/ppermute | solution.py:50
  543.9 9.7 %collective-permute-start.108 = (f32[2,260,2]{2,1,0:T(8,128)S(1)}, f32[2,260,2]{2,1,0:T(8,128)S(1)}, u32[]{:S(2)}, u32[]{:S(2)}) collective-permute-start(f32[2,260,2]{2,1,0:T(8,128)S(1)} %get-tuple-element.37), channel_id=1, source_target_pairs={{0,1},{1,2},{2,3},{3,4},{4,5},{5,6},{6,7},{8,9},{9,10},{10,11},{11... | collective-permute-start | bytes 12488 | tf_op jit(solution)/shard_map/ppermute | solution.py:18
  548.7 9.0 %collective-permute-start.109 = (f32[2,260,2]{2,1,0:T(8,128)S(1)}, f32[2,260,2]{2,1,0:T(8,128)S(1)}, u32[]{:S(2)}, u32[]{:S(2)}) collective-permute-start(f32[2,260,2]{2,1,0:T(8,128)S(1)} %get-tuple-element.36), channel_id=1, source_target_pairs={{1,0},{2,1},{3,2},{4,3},{5,4},{6,5},{7,6},{9,8},{10,9},{11,10},{12... | collective-permute-start | bytes 12488 | tf_op jit(solution)/shard_map/ppermute | solution.py:20
  568.7 9.7 %collective-permute-start.112 = (f32[2,260,2]{2,1,0:T(8,128)S(1)}, f32[2,260,2]{2,1,0:T(8,128)S(1)}, u32[]{:S(2)}, u32[]{:S(2)}) collective-permute-start(f32[2,260,2]{2,1,0:T(8,128)S(1)} %get-tuple-element.35), channel_id=1, source_target_pairs={{0,1},{1,2},{2,3},{3,4},{4,5},{5,6},{6,7},{8,9},{9,10},{10,11},{11... | collective-permute-start | bytes 12488 | tf_op jit(solution)/shard_map/ppermute | solution.py:18
  573.6 9.0 %collective-permute-start.113 = (f32[2,260,2]{2,1,0:T(8,128)S(1)}, f32[2,260,2]{2,1,0:T(8,128)S(1)}, u32[]{:S(2)}, u32[]{:S(2)}) collective-permute-start(f32[2,260,2]{2,1,0:T(8,128)S(1)} %get-tuple-element.34), channel_id=1, source_target_pairs={{1,0},{2,1},{3,2},{4,3},{5,4},{6,5},{7,6},{9,8},{10,9},{11,10},{12... | collective-permute-start | bytes 12488 | tf_op jit(solution)/shard_map/ppermute | solution.py:20
  593.3 8.2 %collective-permute-start.116 = (f32[2,260,2]{2,1,0:T(8,128)S(1)}, f32[2,260,2]{2,1,0:T(8,128)S(1)}, u32[]{:S(2)}, u32[]{:S(2)}) collective-permute-start(f32[2,260,2]{2,1,0:T(8,128)S(1)} %get-tuple-element.33), channel_id=1, source_target_pairs={{0,1},{1,2},{2,3},{3,4},{4,5},{5,6},{6,7},{8,9},{9,10},{10,11},{11... | collective-permute-start | bytes 12488 | tf_op jit(solution)/shard_map/ppermute | solution.py:18
  596.7 9.0 %collective-permute-start.117 = (f32[2,260,2]{2,1,0:T(8,128)S(1)}, f32[2,260,2]{2,1,0:T(8,128)S(1)}, u32[]{:S(2)}, u32[]{:S(2)}) collective-permute-start(f32[2,260,2]{2,1,0:T(8,128)S(1)} %get-tuple-element.32), channel_id=1, source_target_pairs={{1,0},{2,1},{3,2},{4,3},{5,4},{6,5},{7,6},{9,8},{10,9},{11,10},{12... | collective-permute-start | bytes 12488 | tf_op jit(solution)/shard_map/ppermute | solution.py:20
  (66 other events, 462.3 us)
where the time goes:
time: 621 us; the launch traced here: 610 us
  starting transfers between devices  349 us (56%)
  waiting for transfers between devices  134 us (22%)
  local copies, waits for them, and re-layouts  68.9 us (11%)
  other arithmetic  54.3 us (9%)
    ppermute x32, starting transfers between devices, extended_2(): lax.ppermute(last, axis, up)  155 us
    ppermute x24, starting transfers between devices, extended(): lax.ppermute(tail, axis, [(i, (i + 1) % count) for i in range(ends)])  84 us
    ppermute x24, waiting for transfers between devices, extended(): lax.ppermute(head, axis, [((i + 1) % count, i) for i in range(ends)])  67.6 us
    ppermute x32, starting transfers between devices, extended_2(): lax.ppermute(initial, axis, [(b, a) for a, b in up])  51.4 us
    ppermute x24, starting transfers between devices, extended(): lax.ppermute(head, axis, [((i + 1) % count, i) for i in range(ends)])  41.1 us
    ppermute x24, waiting for transfers between devices, extended(): lax.ppermute(tail, axis, [(i, (i + 1) % count) for i in range(ends)])  37.7 us
    reshape x1, local copies, waits for them, and re-layouts, restrict(): blocks = field.reshape(shape[0], shape[1] // 2, 2, shape[2] // 2, 2)  35.6 us
    reduce_sum x2, other arithmetic, restrict(): return 0.25 * jnp.sum(blocks, axis=(2, 4))  21.9 us
  transfers between devices with their start and end apart: 118, of which 50 were waited for; matrix products, arithmetic and copies ran while one was open for 14% of the time, Pallas kernels for 0%

commit v1 on v0

v1 whole, which is shorter than its diff:
```python
import functools

import jax
import jax.numpy as jnp
from jax import lax
from jax.experimental import pallas as pl
from jax.experimental.pallas import tpu as pltpu
from jax.sharding import PartitionSpec as P

FACTOR = 4
N = 256
HALO = 16
PAD = 8
EXT = N + 2 * HALO
ROWS = EXT + 2 * PAD
TOP = PAD + HALO
C = N // 2
CEXT = C + 2 * HALO
CROWS = CEXT + 2 * PAD
FIELDS = 11
MID, LAST, COEF = 8, 9, 10
F32 = jnp.float32
LIMIT = 24 * 1024 * 1024

VM = pl.BlockSpec(memory_space=pltpu.VMEM)


def call(body, outs, n_in, scratch=(), aliases=None, name=None, flops=0):
    return pl.pallas_call(
        body,
        out_shape=[jax.ShapeDtypeStruct(s, F32) for s in outs],
        in_specs=[VM] * n_in,
        out_specs=[VM] * len(outs),
        scratch_shapes=list(scratch),
        input_output_aliases=aliases or {},
        name=name,
        compiler_params=pltpu.CompilerParams(vmem_limit_bytes=LIMIT),
        cost_estimate=pl.CostEstimate(flops=flops, bytes_accessed=1000, transcendentals=0),
    )


def lanes(rows):
    return lax.broadcasted_iota(jnp.int32, (rows, 128), 1)


def roll(x, by):
    by %= 128
    return pltpu.roll(x, by, 1) if by else x


def stencil(ref, f, base, rows, cols, first, last):
    mid = [ref[f, j, pl.ds(base, rows), :] for j in range(cols)]
    left = [pltpu.roll(m, 1, 1) for m in mid]
    right = [pltpu.roll(m, 127, 1) for m in mid]
    sums = []
    for j in range(cols):
        total = ref[f, j, pl.ds(base + 1, rows), :] + ref[f, j, pl.ds(base - 1, rows), :]
        side = jnp.where(first, left[j - 1], left[j]) + jnp.where(last, right[(j + 1) % cols], right[j])
        sums.append(total + side)
    return mid, sums


def loop(total, rows, body):
    def step(i, carry):
        body(PAD + pl.multiple_of(i * rows, 8))
        return carry

    lax.fori_loop(0, total // rows, step, 0)


def step(rhs, mid, scaled, inv, cof, fields, cols, total, rows, after):
    def one(base):
        lane = lanes(rows)
        first, last = lane == 0, lane == 127
        for f in fields:
            own, sums = stencil(rhs, f, base, rows, cols, first, last)
            for j in range(cols):
                at = (j, pl.ds(base, rows), slice(None))
                b = own[j] * inv[at]
                scaled[(f, *at)] = b
                mid[(f, *at)] = b + cof[at] * sums[j]

    def two(base):
        lane = lanes(rows)
        first, last = lane == 0, lane == 127
        for f in fields:
            _, sums = stencil(mid, f, base, rows, cols, first, last)
            for j in range(cols):
                at = (j, pl.ds(base, rows), slice(None))
                u = scaled[(f, *at)] + cof[at] * sums[j]
                rhs[(f, *at)] = after(f, j, pl.ds(base, rows), u)

    loop(total, rows, one)
    loop(total, rows, two)


def keep(f, j, at, u):
    return u


def clear_pads(refs, fields, cols, total):
    zero = jnp.zeros((PAD, 128), F32)
    for ref in refs:
        for f in range(fields):
            for j in range(cols):
                ref[f, j, 0:PAD, :] = zero
                ref[f, j, PAD + total : 2 * PAD + total, :] = zero


def restrict(ref, f, base):
    fine = lax.broadcasted_iota(jnp.int32, (128, C), 0) // 2
    coarse = lax.broadcasted_iota(jnp.int32, (128, C), 1)
    out = None
    for j in range(2):
        pair = ref[f, j, pl.ds(base, C, stride=2), :] + ref[f, j, pl.ds(base + 1, C, stride=2), :]
        pick = jnp.where(fine + 64 * j == coarse, 0.25, 0.0).astype(F32)
        part = jnp.dot(pair, pick, precision=lax.Precision.HIGHEST, preferred_element_type=F32)
        out = part if out is None else out + part
    return out


def flag(condition):
    return jnp.where(condition, 1.0, 0.0).astype(F32)


def strips_body(s_top, s_bot, m_top, m_bot, l_all, start, c_top, c_bot, up, down, last):
    is_end = lax.axis_index("tm") == lax.axis_size("tm") - 1
    up[0:8] = s_top[...]
    down[0:8] = s_bot[...]
    up[MID] = m_top[0]
    down[MID] = m_bot[0]
    up[COEF] = c_top[...]
    down[COEF] = c_bot[...]

    @pl.when(is_end)
    def _():
        last[...] = start[...]

    @pl.when(jnp.logical_not(is_end))
    def _():
        last[...] = l_all[0]

    up[LAST] = last[0:HALO, :]
    down[LAST] = last[N - HALO : N, :]


def make_strips(iterate, source, start, conduct):
    hi = N // HALO - 1
    return pl.pallas_call(
        strips_body,
        grid=(1,),
        out_shape=[
            jax.ShapeDtypeStruct((FIELDS, HALO, N), F32),
            jax.ShapeDtypeStruct((FIELDS, HALO, N), F32),
            jax.ShapeDtypeStruct((N, N), F32),
        ],
        in_specs=[
            pl.BlockSpec((8, HALO, N), lambda i: (0, 0, 0)),
            pl.BlockSpec((8, HALO, N), lambda i: (0, hi, 0)),
            pl.BlockSpec((1, HALO, N), lambda i: (3, 0, 0)),
            pl.BlockSpec((1, HALO, N), lambda i: (3, hi, 0)),
            pl.BlockSpec((1, N, N), lambda i: (7, 0, 0)),
            pl.BlockSpec((N, N), lambda i: (0, 0)),
            pl.BlockSpec((HALO, N), lambda i: (0, 0)),
            pl.BlockSpec((HALO, N), lambda i: (hi, 0)),
        ],
        out_specs=[
            pl.BlockSpec((FIELDS, HALO, N), lambda i: (0, 0, 0)),
            pl.BlockSpec((FIELDS, HALO, N), lambda i: (0, 0, 0)),
            pl.BlockSpec((N, N), lambda i: (0, 0)),
        ],
        name="strips",
        compiler_params=pltpu.CompilerParams(vmem_limit_bytes=LIMIT),
    )(source, source, iterate, iterate, iterate, start, conduct, conduct)


def pack_edges(pieces, rows):
    lane = lanes(rows)
    low = [jnp.zeros((rows, 128), F32) for _ in range((len(pieces) + 7) // 8)]
    high = list(low)
    for f, (head, tail) in enumerate(pieces):
        at, k = HALO * (f % 8), f // 8
        inside = (lane >= at) & (lane < at + HALO)
        low[k] = jnp.where(inside, roll(head, at), low[k])
        high[k] = jnp.where(inside, roll(tail, at + HALO), high[k])
    return low, high


def center_body(source, middle, last, conduct, ext, low, high):
    rows = 16

    def chunk(i, carry):
        base = pl.multiple_of(i * rows, 8)
        pieces = []
        for f in range(FIELDS):
            at = (pl.ds(base, rows), slice(None))
            x = source[(f, *at)] if f < 8 else middle[(0, *at)] if f == MID else last[at] if f == LAST else conduct[at]
            head, tail = x[:, :128], x[:, 128:]
            ext[f, 0, pl.ds(TOP + base, rows), :] = head
            ext[f, 1, pl.ds(TOP + base, rows), :] = tail
            pieces.append((head, tail))
        lo, hi = pack_edges(pieces, rows)
        for k in range(2):
            low[pl.ds(base, rows), 128 * k : 128 * k + 128] = lo[k]
            high[pl.ds(base, rows), 128 * k : 128 * k + 128] = hi[k]
        return carry

    lax.fori_loop(0, N // rows, chunk, 0)


def make_center(source, iterate, last, conduct):
    return pl.pallas_call(
        center_body,
        grid=(1,),
        out_shape=[
            jax.ShapeDtypeStruct((FIELDS, 3, ROWS, 128), F32),
            jax.ShapeDtypeStruct((N, 256), F32),
            jax.ShapeDtypeStruct((N, 256), F32),
        ],
        in_specs=[
            VM,
            pl.BlockSpec((1, N, N), lambda i: (3, 0, 0)),
            VM,
            VM,
        ],
        out_specs=[VM, VM, VM],
        name="center",
        compiler_params=pltpu.CompilerParams(vmem_limit_bytes=LIMIT),
        cost_estimate=pl.CostEstimate(flops=20_000_000, bytes_accessed=1000, transcendentals=0),
    )(source, iterate, last, conduct)


def edges_body(above, below, low_c, high_c, low, high):
    place, ends = lax.axis_index("sx"), lax.axis_size("sx") - 1
    low[HALO : HALO + N, :] = low_c[...]
    high[HALO : HALO + N, :] = high_c[...]
    for ref, base, present in ((above, 0, flag(place > 0)), (below, HALO + N, flag(place < ends))):
        pieces = [(ref[f, :, :128] * present, ref[f, :, 128:] * present) for f in range(FIELDS)]
        lo, hi = pack_edges(pieces, HALO)
        for k in range(2):
            low[base : base + HALO, 128 * k : 128 * k + 128] = lo[k]
            high[base : base + HALO, 128 * k : 128 * k + 128] = hi[k]


def side_column(before, after, f, rows, first, final):
    lane = lanes(rows)
    at = HALO * (f % 8)
    right = jnp.where(lane < HALO, roll(after, -at) * final, 0.0)
    return jnp.where(lane >= 128 - HALO, roll(before, -HALO - at) * first, right)


MAIN_ROWS = 272
PART1 = 2 * MAIN_ROWS
PART2 = PART1 + 4 * HALO
MAIN = PART2 + EXT // 2


def window(x, width):
    return roll(x, width)


def fold(dest, base, columns, width, groups, rows_in):
    span = 2 * width
    rows = rows_in // groups
    lane = lanes(rows)
    out = jnp.zeros((rows, 128), F32)
    for g in range(groups):
        for k, read in enumerate(columns):
            at = (g * len(columns) + k) * span
            inside = (lane >= at) & (lane < at + span)
            out = jnp.where(inside, roll(read(g * rows, rows), width + at), out)
    dest[base : base + rows, :] = out


def unfold(src, base, k, count, width, groups, rows_in, write):
    span = 2 * width
    rows = rows_in // groups
    lane = lanes(rows)
    for g in range(groups):
        at = (g * count + k) * span
        x = roll(src[base : base + rows, :], -width - at)
        write(g * rows, rows, jnp.where((lane < width) | (lane >= 128 - width), x, 0.0))


def local_body(
    ext_in, above, below, before, after,
    ext, coefs, forced, own_new, main, up, down, low_c, high_c, coarse,
    rhs, mid, scaled,
):
    del ext_in
    t, x, z = lax.axis_index("tm"), lax.axis_index("sx"), lax.axis_index("sy")
    not_end = flag(t < lax.axis_size("tm") - 1)
    x_first, x_final = flag(x > 0), flag(x < lax.axis_size("sx") - 1)
    z_first, z_final = flag(z > 0), flag(z < lax.axis_size("sy") - 1)
    inv, cof = coefs.at[0], coefs.at[1]
    for f in range(FIELDS):
        for j in range(2):
            ext[f, j, PAD:TOP, :] = above[f, :, 128 * j : 128 * j + 128] * x_first
            ext[f, j, TOP + N : TOP + N + HALO, :] = below[f, :, 128 * j : 128 * j + 128] * x_final

    def columns(base):
        at = pl.ds(base - PAD, 32)
        for k in range(2):
            left, right = before[at, 128 * k : 128 * k + 128], after[at, 128 * k : 128 * k + 128]
            for f in range(8 * k, min(8 * k + 8, FIELDS)):
                ext[f, 2, pl.ds(base, 32), :] = side_column(left, right, f, 32, z_first, z_final)

    loop(EXT, 32, columns)
    clear_pads((rhs, mid), 3, 3, EXT)

    def prepare(base):
        at = pl.ds(base, 32)
        for j in range(3):
            c = ext[COEF, j, at, :]
            r = 1.0 / (1.0 + 4.0 * c)
            inv[j, at, :] = r
            cof[j, at, :] = c * r
            rhs[0, j, at, :] = ext[MID, j, at, :] + ext[4, j, at, :]
            rhs[1, j, at, :] = ext[0, j, at, :]
            rhs[2, j, at, :] = ext[LAST, j, at, :]

    loop(EXT, 32, prepare)
    for k in range(1, FACTOR):

        def add(f, j, at, u, k=k):
            return u + ext[4 + k, j, at, :] if f == 0 else u + ext[k, j, at, :] if f == 1 else u

        step(rhs, mid, scaled, inv, cof, range(3), 3, EXT, 32, add)
    step(rhs, mid, scaled, inv, cof, range(3), 3, EXT, 32, keep)

    def between(base):
        at = pl.ds(base, 32)
        for j in range(3):
            new, old = rhs[0, j, at, :], ext[LAST, j, at, :]
            scaled[0, j, at, :] = old + not_end * (new - old)
            if j < 2:
                own_new[j, at, :] = new
            rhs[0, j, at, :] = not_end * (new - old)
            s = rhs[1, j, at, :]
            forced[j, at, :] = s
            rhs[1, j, at, :] = s - ext[MID, j, at, :]

    loop(EXT, 32, between)
    for j in range(2):
        main[MAIN_ROWS * j : MAIN_ROWS * (j + 1), :] = scaled[0, j, 2 * PAD : 2 * PAD + MAIN_ROWS, :]
        main[PART1 + 2 * HALO * j : PART1 + 2 * HALO * j + HALO, :] = ext[LAST, j, PAD:TOP, :]
        main[PART1 + 2 * HALO * j + HALO : PART1 + 2 * HALO * (j + 1), :] = ext[LAST, j, TOP + N : TOP + N + HALO, :]
    fold(
        main, PART2,
        [lambda r, n: scaled[0, 2, PAD + r : PAD + r + n, :], lambda r, n: ext[LAST, 2, PAD + r : PAD + r + n, :]],
        HALO, 2, EXT,
    )
    for k in range(FACTOR):
        step(rhs, mid, scaled, inv, cof, range(3), 3, EXT, 32, keep)
    coarse[0] = restrict(rhs, 1, TOP)
    coarse[1] = restrict(rhs, 0, TOP)
    coarse[2] = restrict(rhs, 2, TOP)
    coarse[3] = restrict(ext, COEF, TOP)
    for k in range(4):
        up[k] = coarse[k, 0:HALO, :]
        down[k] = coarse[k, C - HALO : C, :]
    lo, hi = pack_edges([(coarse[k], coarse[k]) for k in range(4)], C)
    low_c[...] = lo[0]
    high_c[...] = hi[0]


def coarse_edges_body(above, below, low_c, high_c, low, high):
    place, ends = lax.axis_index("sx"), lax.axis_size("sx") - 1
    low[HALO : HALO + C, :] = low_c[...]
    high[HALO : HALO + C, :] = high_c[...]
    for ref, base, present in ((above, 0, flag(place > 0)), (below, HALO + C, flag(place < ends))):
        lo, hi = pack_edges([(ref[k] * present,) * 2 for k in range(4)], HALO)
        low[base : base + HALO, :] = lo[0]
        high[base : base + HALO, :] = hi[0]


SENT = 144
SENT_AT = 2 * PAD


def coarse_body(coarse, above, below, before, after, one, two, three, four, coefs, ext, rhs, mid, scaled):
    t, x, z = lax.axis_index("tm"), lax.axis_index("sx"), lax.axis_index("sy")
    not_end = flag(t < lax.axis_size("tm") - 1)
    x_first, x_final = flag(x > 0), flag(x < lax.axis_size("sx") - 1)
    z_first, z_final = flag(z > 0), flag(z < lax.axis_size("sy") - 1)
    for k in range(4):
        ext[k, 0, PAD:TOP, :] = above[k] * x_first
        ext[k, 0, TOP : TOP + C, :] = coarse[k]
        ext[k, 0, TOP + C : TOP + C + HALO, :] = below[k] * x_final
        ext[k, 1, PAD : PAD + CEXT, :] = side_column(before[...], after[...], k, CEXT, z_first, z_final)
    inv, cof = coefs.at[0], coefs.at[1]
    clear_pads((rhs, mid), 2, 2, CEXT)
    own = pl.ds(PAD, CEXT)
    for j in range(2):
        c = ext[3, j, own, :]
        r = 1.0 / (1.0 + 4.0 * c)
        inv[j, own, :] = r
        cof[j, own, :] = c * r
        rhs[0, j, own, :] = ext[0, j, own, :] * not_end
        rhs[1, j, own, :] = ext[1, j, own, :]

    def advance(fields, after_step):
        step(rhs, mid, scaled, inv, cof, fields, 2, CEXT, 32, after_step)

    advance(range(2), lambda f, j, at, u: u if f == 0 else u + ext[2, j, at, :])
    for j in range(2):
        ext[2, j, own, :] = rhs[1, j, own, :]
    advance(range(2), lambda f, j, at, u: u + ext[2, j, at, :] if f == 0 else u)
    rows = slice(SENT_AT, SENT_AT + SENT)

    def reader(ref, f):
        return lambda r, n: ref[f, 1, SENT_AT + r : SENT_AT + r + n, :]

    one[0:SENT, :] = ext[0, 0, rows, :]
    one[SENT : 2 * SENT, :] = ext[1, 0, rows, :]
    fold(one, 2 * SENT, [reader(ext, 0), reader(ext, 1)], 8, 3, SENT)
    two[0:SENT, :] = rhs[0, 0, rows, :]
    fold(two, SENT, [reader(rhs, 0)], 8, 6, SENT)
    advance(range(2), keep)
    advance(range(2), keep)
    three[0:SENT, :] = rhs[0, 0, rows, :]
    fold(three, SENT, [reader(rhs, 0)], 8, 6, SENT)
    advance(range(1, 2), keep)
    for j in range(2):
        four[j] = rhs[1, j, rows, :]


def arrive_body(last, main, ext, coefs, forced, resid, new_start, new_mid, coarse_mid, rhs, mid, scaled):
    inv, cof = coefs.at[0], coefs.at[1]
    clear_pads((rhs, mid), 2, 3, EXT)
    for j in range(2):
        rhs[0, j, PAD:TOP, :] = main[PART1 + 2 * HALO * j : PART1 + 2 * HALO * j + HALO, :]
        rhs[0, j, TOP : TOP + N, :] = last[:, 128 * j : 128 * j + 128]
        rhs[0, j, TOP + N : TOP + N + HALO, :] = main[PART1 + 2 * HALO * j + HALO : PART1 + 2 * HALO * (j + 1), :]
        new_start[j, PAD : 2 * PAD, :] = jnp.zeros((PAD, 128), F32)
        new_start[j, 2 * PAD : 2 * PAD + MAIN_ROWS, :] = main[MAIN_ROWS * j : MAIN_ROWS * (j + 1), :]
        new_start[j, 2 * PAD + MAIN_ROWS : 3 * PAD + MAIN_ROWS, :] = jnp.zeros((PAD, 128), F32)

    def put_new(r, n, value):
        new_start[2, PAD + r : PAD + r + n, :] = value

    def put_old(r, n, value):
        rhs[0, 2, PAD + r : PAD + r + n, :] = value

    unfold(main, PART2, 0, 2, HALO, 2, EXT, put_new)
    unfold(main, PART2, 1, 2, HALO, 2, EXT, put_old)

    def difference(base):
        at = pl.ds(base, 32)
        for j in range(3):
            rhs[1, j, at, :] = new_start[j, at, :] - rhs[0, j, at, :]

    loop(EXT, 32, difference)
    for k in range(FACTOR):
        step(rhs, mid, scaled, inv, cof, range(2), 3, EXT, 32, keep)

    def between(base):
        at = pl.ds(base, 32)
        for j in range(3):
            u = rhs[0, j, at, :] + forced[j, at, :]
            new_mid[j, at, :] = u
            rhs[0, j, at, :] = u - ext[MID, j, at, :]

    loop(EXT, 32, between)
    for k in range(FACTOR):
        step(rhs, mid, scaled, inv, cof, range(1), 3, EXT, 32, keep)
    for k in range(2):
        for j in range(2):
            resid[k, :, 128 * j : 128 * j + 128] = rhs[1 - k, j, TOP : TOP + N, :]
    coarse_mid[...] = restrict(rhs, 0, TOP)


def final_body(
    one, two, three, four, ccoefs, coarse_mid, ext, coefs, new_start, new_mid, own_new,
    out, err, cmid, cscaled, fix, rhs, mid, scaled,
):
    t = lax.axis_index("tm")
    m1, m2, m3, m4 = flag(t > 0), flag(t > 0), flag(t > 1), flag(t > 2)
    inv, cof = ccoefs.at[0], ccoefs.at[1]
    clear_pads((err, cmid), 1, 2, CEXT)
    rows = slice(SENT_AT, SENT_AT + SENT)
    zero = jnp.zeros((PAD, 128), F32)
    for j in range(2):
        err[0, j, PAD:SENT_AT, :] = zero
        err[0, j, SENT_AT + SENT : SENT_AT + SENT + PAD, :] = zero
        cmid[0, j, PAD:SENT_AT, :] = zero
        cmid[0, j, SENT_AT + SENT : SENT_AT + SENT + PAD, :] = zero
    holds = (scaled.at[0, 1], scaled.at[0, 2], scaled.at[1, 1], scaled.at[1, 2])

    def put(ref):
        def write(r, n, value):
            ref[r : r + n, :] = value

        return write

    unfold(one, 2 * SENT, 0, 2, 8, 3, SENT, put(holds[0]))
    unfold(one, 2 * SENT, 1, 2, 8, 3, SENT, put(holds[1]))
    unfold(two, SENT, 0, 1, 8, 6, SENT, put(holds[2]))
    unfold(three, SENT, 0, 1, 8, 6, SENT, put(holds[3]))
    err[0, 0, rows, :] = m1 * one[0:SENT, :] + m2 * two[0:SENT, :] + m3 * three[0:SENT, :] + m4 * four[0]
    err[0, 1, rows, :] = (
        m1 * holds[0][0:SENT, :] + m2 * holds[2][0:SENT, :] + m3 * holds[3][0:SENT, :] + m4 * four[1]
    )

    def spread(k, sides):
        count = C + 8 if sides else C
        base = TOP - 4 if sides else TOP
        to = TOP - 8 if sides else TOP
        src = lax.broadcasted_iota(jnp.int32, (128, 128), 0)
        dst = lax.broadcasted_iota(jnp.int32, (128, 128), 1)
        for j in range(3 if sides else 2):
            if j < 2:
                pick = src == dst // 2 + 64 * j
            else:
                pick = ((dst < HALO) & (src == dst // 2)) | ((dst >= 128 - HALO) & (src == 64 + dst // 2))
            wide = jnp.dot(
                err[0, j // 2, base : base + count, :], flag(pick), precision=lax.Precision.HIGHEST,
                preferred_element_type=F32,
            )
            fix[k, j, pl.ds(to, count, stride=2), :] = wide
            fix[k, j, pl.ds(to + 1, count, stride=2), :] = wide

    clear_pads((rhs, mid), 2, 3, EXT)
    for k in range(2):
        for j in range(3):
            fix[k, j, PAD : TOP - 8, :] = zero
            fix[k, j, TOP + N + 8 : TOP + N + HALO, :] = zero
    spread(0, True)
    step(err, cmid, cscaled, inv, cof, range(1), 2, CEXT, 32, keep)
    err[0, 0, rows, :] += one[SENT : 2 * SENT, :]
    err[0, 1, rows, :] += holds[1][0:SENT, :]
    spread(1, True)
    step(err, cmid, cscaled, inv, cof, range(1), 2, CEXT, 32, keep)
    err[0, 0, TOP : TOP + C, :] += coarse_mid[...]
    spread(2, False)
    inv, cof = coefs.at[0], coefs.at[1]

    def begin(base):
        at = pl.ds(base, 32)
        for j in range(3):
            rhs[0, j, at, :] = new_start[j, at, :] + fix[0, j, at, :] + ext[0, j, at, :]
            u = new_mid[j, at, :] + fix[1, j, at, :]
            new_mid[j, at, :] = u
            rhs[1, j, at, :] = u + ext[4, j, at, :]

    loop(EXT, 32, begin)
    for j in range(2):
        cols = slice(128 * j, 128 * j + 128)
        out[3, :, cols] = new_mid[j, TOP : TOP + N, :]
        out[7, :, cols] = own_new[j, TOP : TOP + N, :] + fix[2, j, TOP : TOP + N, :]
    for k in range(FACTOR - 1):
        step(rhs, mid, scaled, inv, cof, range(2), 3, EXT, 32, keep)
        for f in range(2):
            for j in range(2):
                out[4 * f + k, :, 128 * j : 128 * j + 128] = rhs[f, j, TOP : TOP + N, :]
        if k + 1 < FACTOR - 1:

            def force(base, k=k):
                at = pl.ds(base, 32)
                for f in range(2):
                    for j in range(3):
                        rhs[f, j, at, :] += ext[4 * f + k + 1, j, at, :]

            loop(EXT, 32, force)


def ring(x, axis, by):
    count = lax.axis_size(axis)
    return lax.ppermute(x, axis, [(i, (i + by) % count) for i in range(count)])


def fine_scratch(fields):
    return [pltpu.VMEM((fields, 3, ROWS, 128), F32)] * 3


def shards(iterate, source, start_field, conduct):
    up, down, last = make_strips(iterate, source, start_field, conduct)
    above, below = ring(down, "sx", 1), ring(up, "sx", -1)
    last_in = ring(last, "tm", 1)
    ext, low_c, high_c = make_center(source, iterate, last, conduct)
    low, high = call(edges_body, [(EXT, 256)] * 2, 4, name="edges", flops=1_000_000)(above, below, low_c, high_c)
    before, after = ring(high, "sy", 1), ring(low, "sy", -1)
    ext, coefs, forced, own_new, main, c_up, c_down, c_low, c_high, coarse = call(
        local_body,
        [
            (FIELDS, 3, ROWS, 128), (2, 3, ROWS, 128), (3, ROWS, 128), (2, ROWS, 128), (MAIN, 128),
            (4, HALO, 128), (4, HALO, 128), (C, 128), (C, 128), (4, C, 128),
        ],
        5, fine_scratch(3), {0: 0}, "local", 50_000_000,
    )(ext, above, below, before, after)
    c_above, c_below = ring(c_down, "sx", 1), ring(c_up, "sx", -1)
    main_in = ring(main, "tm", 1)
    c_lo, c_hi = call(coarse_edges_body, [(CEXT, 128)] * 2, 4, name="coarse_edges")(c_above, c_below, c_low, c_high)
    c_before, c_after = ring(c_hi, "sy", 1), ring(c_lo, "sy", -1)
    one, two, three, four, ccoefs = call(
        coarse_body,
        [(2 * SENT + 48, 128), (SENT + 24, 128), (SENT + 24, 128), (2, SENT, 128), (2, 2, CROWS, 128)],
        5,
        [pltpu.VMEM((4, 2, CROWS, 128), F32)] + [pltpu.VMEM((2, 2, CROWS, 128), F32)] * 3,
        name="coarse",
    )(coarse, c_above, c_below, c_before, c_after)
    one, two, three = ring(one, "tm", 1), ring(two, "tm", 2), ring(three, "tm", 3)
    resid, new_start, new_mid, coarse_mid = call(
        arrive_body,
        [(2, N, N), (3, ROWS, 128), (3, ROWS, 128), (C, C)],
        5, fine_scratch(2), name="arrive", flops=30_000_000,
    )(last_in, main_in, ext, coefs, forced)
    (updated,) = call(
        final_body,
        [(8, N, N)],
        11,
        [pltpu.VMEM((1, 2, CROWS, 128), F32)] * 3 + [pltpu.VMEM((3, 3, ROWS, 128), F32)] + fine_scratch(2),
        name="final",
    )(one, two, three, four, ccoefs, coarse_mid, ext, coefs, new_start, new_mid, own_new)
    return updated, resid


def solution(mesh):
    in_specs = (P("tm", "sx", "sy"), P("tm", "sx", "sy"), P("sx", "sy"), P("sx", "sy"))
    out_specs = (P("tm", "sx", "sy"), P("tm", "sx", "sy"))
    return jax.shard_map(shards, mesh=mesh, in_specs=in_specs, out_specs=out_specs, check_vma=False)
```

time: 621 us -> 103 us (0.17)
  the two profiles are of different devices: /device:TPU:9 before, /device:TPU:64 now
where the time goes in v1:
time: 103 us
  Pallas kernels  61.3 us (60%)
  starting transfers between devices  19.9 us (19%)
  waiting for transfers between devices  16.2 us (16%)
  local copies, waits for them, and re-layouts  5.08 us (5%)
    pallas_call x1, Pallas kernels, shards(): call(local_body, [(FIELDS, 3, ROWS, 128), (2, 3, ROWS, 128), (3, ROWS, 12...  24.3 us
    ppermute x13, starting transfers between devices, ring(): return lax.ppermute(x, axis, [(i, (i + by) % count) for i in range(count)])  19.9 us
    pallas_call x1, Pallas kernels, shards(): call(arrive_body, [(2, N, N), (3, ROWS, 128), (3, ROWS, 128), (C, C)], 5,...  17.5 us
    ppermute x13, waiting for transfers between devices, ring(): return lax.ppermute(x, axis, [(i, (i + by) % count) for i in range(count)])  16.2 us
    pallas_call x1, Pallas kernels, shards(): call(final_body, [(8, N, N)], 11, [pltpu.VMEM((1, 2, CROWS, 128), F32)] *...  11.9 us
    pallas_call x1, Pallas kernels, shards(): call(coarse_body, [(2 * SENT + 48, 128), (SENT + 24, 128), (SENT + 24, 12...  5.59 us
    unnamed x10, local copies, waits for them, and re-layouts  5.08 us
  transfers between devices with their start and end apart: 13, of which 5 were waited for; matrix products, arithmetic and copies ran while one was open for 0% of the time, Pallas kernels for 24%

profile of v1, /device:TPU:64, one launch (start us, length us, event | category | flops | bytes accessed | tf_op | source)
XLA Modules:
  0.0 103.2 jit_solution(8156527193605409960)
XLA Ops:
  0.6 0.0 copy-start
  0.6 1.6 %copy-done = f32[8,256,256]{2,1,0:T(8,128)S(1)} copy-done((f32[8,256,256]{2,1,0:T(8,128)S(1)}, f32[8,256,256]{2,1,0:T(8,128)}, u32[]{:S(2)}) %copy-start) | copy-done | bytes 2097176
  2.2 0.0 copy-start.1
  2.2 1.6 %copy-done.1 = f32[8,256,256]{2,1,0:T(8,128)S(1)} copy-done((f32[8,256,256]{2,1,0:T(8,128)S(1)}, f32[8,256,256]{2,1,0:T(8,128)}, u32[]{:S(2)}) %copy-start.1) | copy-done | bytes 2097176
  3.8 0.0 copy-start.2
  3.8 0.9 copy-done.2
  4.8 0.0 copy-start.4
  4.8 0.9 copy-done.4
  5.7 0.0 copy-start.3
  5.8 0.0 collective-permute-start
  5.8 2.9 %collective-permute-start.1 = (f32[11,16,256]{2,1,0:T(8,128)S(1)}, f32[11,16,256]{2,1,0:T(8,128)S(1)}, u32[]{:S(2)}, u32[]{:S(2)}) collective-permute-start(f32[11,16,256]{2,1,0:T(8,128)S(1)} %get-tuple-element.34), channel_id=1, source_target_pairs={{0,56},{8,0},{16,8},{24,16},{32,24},{40,32},{48,40},{56,48},{1,57}... | collective-permute-start | bytes 540680 | tf_op jit(solution)/shard_map/ppermute | solution.py:569
  8.7 0.0 copy-done.3
  8.7 1.8 %center.1 = (f32[11,3,304,128]{3,2,1,0:T(8,128)S(1)}, f32[256,256]{1,0:T(8,128)S(1)}, f32[256,256]{1,0:T(8,128)S(1)}) custom-call(f32[8,256,256]{2,1,0:T(8,128)S(1)} %copy-done.1, f32[8,256,256]{2,1,0:T(8,128)S(1)} %copy-done, f32[256,256]{1,0:T(8,128)S(1)} %get-tuple-element.31.last, f32[256,256]{1,0:T(8,128)S(1)} %copy-done.3), custom_call_target="tpu_custom_call" | custom-call | flops 20000000 | bytes 1000 | tf_op jit(solution)/shard_map/center/pallas_call | solution.py:212
  10.5 1.4 %collective-permute-done.above = f32[11,16,256]{2,1,0:T(8,128)S(1)} collective-permute-done((f32[11,16,256]{2,1,0:T(8,128)S(1)}, f32[11,16,256]{2,1,0:T(8,128)S(1)}, u32[]{:S(2)}, u32[]{:S(2)}) %collective-permute-start) | collective-permute-done | bytes 180256 | tf_op jit(solution)/shard_map/ppermute | solution.py:569
  11.9 0.0 collective-permute-done.1.below
  11.9 0.2 edges.1
  12.1 2.0 %collective-permute-start.2 = (f32[288,256]{1,0:T(8,128)S(1)}, f32[288,256]{1,0:T(8,128)S(1)}, u32[]{:S(2)}, u32[]{:S(2)}) collective-permute-start(f32[288,256]{1,0:T(8,128)S(1)} %get-tuple-element.37), channel_id=1, source_target_pairs={{0,1},{1,2},{2,3},{3,4},{4,5},{5,6},{6,7},{7,0},{8,9},{9,10},{10,1... | collective-permute-start | bytes 884744 | tf_op jit(solution)/shard_map/ppermute | solution.py:569
  14.1 0.1 collective-permute-start.3
  14.2 7.3 %collective-permute-done.2.before = f32[288,256]{1,0:T(8,128)S(1)} collective-permute-done((f32[288,256]{1,0:T(8,128)S(1)}, f32[288,256]{1,0:T(8,128)S(1)}, u32[]{:S(2)}, u32[]{:S(2)}) %collective-permute-start.2) | collective-permute-done | bytes 294944 | tf_op jit(solution)/shard_map/ppermute | solution.py:569
  21.5 3.0 %collective-permute-done.3.after = f32[288,256]{1,0:T(8,128)S(1)} collective-permute-done((f32[288,256]{1,0:T(8,128)S(1)}, f32[288,256]{1,0:T(8,128)S(1)}, u32[]{:S(2)}, u32[]{:S(2)}) %collective-permute-start.3) | collective-permute-done | bytes 294944 | tf_op jit(solution)/shard_map/ppermute | solution.py:569
  24.5 24.3 %local.1 = (f32[11,3,304,128]{3,2,1,0:T(8,128)S(1)}, f32[2,3,304,128]{3,2,1,0:T(8,128)S(1)}, f32[3,304,128]{2,1,0:T(8,128)S(1)}, f32[2,304,128]{2,1,0:T(8,128)S(...) custom-call(f32[11,3,304,128]{3,2,1,0:T(8,128)S(1)} %get-tuple-eleme, ...), custom_call_target="tpu_custom_call", output_to_operand_aliasing={{0}: (0, {})} | custom-call | flops 50000000 | bytes 1000 | tf_op jit(solution)/shard_map/local/pallas_call | solution.py:583
  48.8 1.7 %collective-permute-start.12 = (f32[752,128]{1,0:T(8,128)S(1)}, f32[752,128]{1,0:T(8,128)S(1)}, u32[]{:S(2)}, u32[]{:S(2)}) collective-permute-start(f32[752,128]{1,0:T(8,128)S(1)} %get-tuple-element.51), channel_id=1, source_target_pairs={{0,64},{64,128},{128,192},{192,0},{1,65},{65,129},{129,193},{193,1... | collective-permute-start | bytes 1155080 | tf_op jit(solution)/shard_map/ppermute | solution.py:569
  50.5 0.0 collective-permute-start.4
  50.5 3.0 %collective-permute-start.5 = (f32[4,16,128]{2,1,0:T(8,128)S(1)}, f32[4,16,128]{2,1,0:T(8,128)S(1)}, u32[]{:S(2)}, u32[]{:S(2)}) collective-permute-start(f32[4,16,128]{2,1,0:T(8,128)S(1)} %get-tuple-element.41), channel_id=1, source_target_pairs={{0,56},{8,0},{16,8},{24,16},{32,24},{40,32},{48,40},{56,48},{1,57}... | collective-permute-start | bytes 98312 | tf_op jit(solution)/shard_map/ppermute | solution.py:569
  53.4 1.6 %collective-permute-start.11 = (f32[256,256]{1,0:T(8,128)S(1)}, f32[256,256]{1,0:T(8,128)S(1)}, u32[]{:S(2)}, u32[]{:S(2)}) collective-permute-start(f32[256,256]{1,0:T(8,128)S(1)} %get-tuple-element.31.last), channel_id=1, source_target_pairs={{0,64},{64,128},{128,192},{192,0},{1,65},{65,129},{129,193},{193,1... | collective-permute-start | bytes 786440 | tf_op jit(solution)/shard_map/ppermute | solution.py:569
  55.0 0.0 collective-permute-done.4.above
  55.0 0.0 collective-permute-done.5.below
  55.0 0.1 coarse_edges.1
  55.2 3.0 %collective-permute-start.6 = (f32[160,128]{1,0:T(8,128)S(1)}, f32[160,128]{1,0:T(8,128)S(1)}, u32[]{:S(2)}, u32[]{:S(2)}) collective-permute-start(f32[160,128]{1,0:T(8,128)S(1)} %get-tuple-element.44), channel_id=1, source_target_pairs={{0,1},{1,2},{2,3},{3,4},{4,5},{5,6},{6,7},{7,0},{8,9},{9,10},{10,1... | collective-permute-start | bytes 245768 | tf_op jit(solution)/shard_map/ppermute | solution.py:569
  58.2 0.0 collective-permute-start.7
  58.2 2.1 %collective-permute-done.6.before = f32[160,128]{1,0:T(8,128)S(1)} collective-permute-done((f32[160,128]{1,0:T(8,128)S(1)}, f32[160,128]{1,0:T(8,128)S(1)}, u32[]{:S(2)}, u32[]{:S(2)}) %collective-permute-start.6) | collective-permute-done | bytes 81952 | tf_op jit(solution)/shard_map/ppermute | solution.py:569
  60.2 2.4 %collective-permute-done.7.after = f32[160,128]{1,0:T(8,128)S(1)} collective-permute-done((f32[160,128]{1,0:T(8,128)S(1)}, f32[160,128]{1,0:T(8,128)S(1)}, u32[]{:S(2)}, u32[]{:S(2)}) %collective-permute-start.7) | collective-permute-done | bytes 81952 | tf_op jit(solution)/shard_map/ppermute | solution.py:569
  62.6 5.6 %coarse.1 = (f32[336,128]{1,0:T(8,128)S(1)}, f32[168,128]{1,0:T(8,128)S(1)}, f32[168,128]{1,0:T(8,128)S(1)}, f32[2,144,128]{2,1,0:T(8,128)S(1)}, f32[2,2,176,128]{3,2,1,0:T(8,128)S(1)}) custom-call(f32[4,128,128]{2,1,0:T(8,128)S(1)} %get-tuple-element.39.coarse, f32[4,16,128]{2,1,0:T(8,128)S(1)} %collective-permute-done.4.above, ...), custom_call_target="tpu_custom_call" | custom-call | bytes 1000 | tf_op jit(solution)/shard_map/coarse/pallas_call | solution.py:595
  68.2 1.6 %collective-permute-start.8 = (f32[336,128]{1,0:T(8,128)S(1)}, f32[336,128]{1,0:T(8,128)S(1)}, u32[]{:S(2)}, u32[]{:S(2)}) collective-permute-start(f32[336,128]{1,0:T(8,128)S(1)} %get-tuple-element.46), channel_id=1, source_target_pairs={{0,64},{64,128},{128,192},{192,0},{1,65},{65,129},{129,193},{193,1... | collective-permute-start | bytes 516104 | tf_op jit(solution)/shard_map/ppermute | solution.py:569
  69.9 1.5 %collective-permute-start.9 = (f32[168,128]{1,0:T(8,128)S(1)}, f32[168,128]{1,0:T(8,128)S(1)}, u32[]{:S(2)}, u32[]{:S(2)}) collective-permute-start(f32[168,128]{1,0:T(8,128)S(1)} %get-tuple-element.47), channel_id=1, source_target_pairs={{0,128},{64,192},{128,0},{192,64},{1,129},{65,193},{129,1},{193,65... | collective-permute-start | bytes 258056 | tf_op jit(solution)/shard_map/ppermute | solution.py:569
  71.4 2.4 %collective-permute-start.10 = (f32[168,128]{1,0:T(8,128)S(1)}, f32[168,128]{1,0:T(8,128)S(1)}, u32[]{:S(2)}, u32[]{:S(2)}) collective-permute-start(f32[168,128]{1,0:T(8,128)S(1)} %get-tuple-element.48), channel_id=1, source_target_pairs={{0,192},{64,0},{128,64},{192,128},{1,193},{65,1},{129,65},{193,129... | collective-permute-start | bytes 258056 | tf_op jit(solution)/shard_map/ppermute | solution.py:569
  73.8 0.0 collective-permute-done.11.last
  73.8 0.0 collective-permute-done.12.main
  73.8 17.5 %arrive.1 = (f32[2,256,256]{2,1,0:T(8,128)}, f32[3,304,128]{2,1,0:T(8,128)S(1)}, f32[3,304,128]{2,1,0:T(8,128)S(1)}, f32[128,128]{1,0:T(8,128)S(1)}) custom-call(f32[256,256]{1,0:T(8,128)S(1)} %collective-permute-done.11.last, f32[752,128]{1,0:T(8,128)S(1)} %collective-permute-done.12.main, f32[11,3,304,128]{3,2,1,0:T(8,128)S(1)} %get-tuple-element.52.ext, ...), custom_call_target="tpu_custom_call" | custom-call | flops 30000000 | bytes 1000 | tf_op jit(solution)/shard_map/arrive/pallas_call | solution.py:603
  91.3 0.0 collective-permute-done.9.two
  91.3 0.0 collective-permute-done.10.three
  91.3 0.0 collective-permute-done.8.one
  91.3 11.9 %final.1 = f32[8,256,256]{2,1,0:T(8,128)} custom-call(f32[336,128]{1,0:T(8,128)S(1)} %collective-permute-done.8.one, f32[168,128]{1,0:T(8,128)S(1)} %collective-permute-done.9.two, f32[168,128]{1,0:T(8,128)S(1)} %collective-permute-done.10.three, f32[2,144,128]{2,1,0:T(8,128)S(1)} %get-tuple-element.49.four, ...), custom_call_target="tpu_custom_call" | custom-call | bytes 1000 | tf_op jit(solution)/shard_map/final/pallas_call | solution.py:608
  (1 shorter events, 0.0 us)
Async XLA Ops:
  0.6 1.6 %copy-start = (f32[8,256,256]{2,1,0:T(8,128)S(1)}, f32[8,256,256]{2,1,0:T(8,128)}, u32[]{:S(2)}) copy-start(f32[8,256,256]{2,1,0:T(8,128)} %middle.1) | copy-start | bytes 6291460
  2.2 1.6 %copy-start.1 = (f32[8,256,256]{2,1,0:T(8,128)S(1)}, f32[8,256,256]{2,1,0:T(8,128)}, u32[]{:S(2)}) copy-start(f32[8,256,256]{2,1,0:T(8,128)} %source.1) | copy-start | bytes 6291460
  3.8 0.9 copy-start.2
  4.8 0.9 copy-start.4
  5.7 3.0 %copy-start.3 = (f32[256,256]{1,0:T(8,128)S(1)}, f32[256,256]{1,0:T(8,128)}, u32[]{:S(2)}) copy-start(f32[256,256]{1,0:T(8,128)} %conduct.1) | copy-start | bytes 786436
  5.8 6.1 %collective-permute-start = (f32[11,16,256]{2,1,0:T(8,128)S(1)}, f32[11,16,256]{2,1,0:T(8,128)S(1)}, u32[]{:S(2)}, u32[]{:S(2)}) collective-permute-start(f32[11,16,256]{2,1,0:T(8,128)S(1)} %get-tuple-element.33), channel_id=1, source_target_pairs={{0,8},{8,16},{16,24},{24,32},{32,40},{40,48},{48,56},{56,0},{1,9},... | collective-permute-start | bytes 540680 | tf_op jit(solution)/shard_map/ppermute | solution.py:569
  5.8 6.1 %collective-permute-start.1 = (f32[11,16,256]{2,1,0:T(8,128)S(1)}, f32[11,16,256]{2,1,0:T(8,128)S(1)}, u32[]{:S(2)}, u32[]{:S(2)}) collective-permute-start(f32[11,16,256]{2,1,0:T(8,128)S(1)} %get-tuple-element.34), channel_id=1, source_target_pairs={{0,56},{8,0},{16,8},{24,16},{32,24},{40,32},{48,40},{56,48},{1,57}... | collective-permute-start | bytes 540680 | tf_op jit(solution)/shard_map/ppermute | solution.py:569
  12.1 9.4 %collective-permute-start.2 = (f32[288,256]{1,0:T(8,128)S(1)}, f32[288,256]{1,0:T(8,128)S(1)}, u32[]{:S(2)}, u32[]{:S(2)}) collective-permute-start(f32[288,256]{1,0:T(8,128)S(1)} %get-tuple-element.37), channel_id=1, source_target_pairs={{0,1},{1,2},{2,3},{3,4},{4,5},{5,6},{6,7},{7,0},{8,9},{9,10},{10,1... | collective-permute-start | bytes 884744 | tf_op jit(solution)/shard_map/ppermute | solution.py:569
  14.1 10.4 %collective-permute-start.3 = (f32[288,256]{1,0:T(8,128)S(1)}, f32[288,256]{1,0:T(8,128)S(1)}, u32[]{:S(2)}, u32[]{:S(2)}) collective-permute-start(f32[288,256]{1,0:T(8,128)S(1)} %get-tuple-element.38), channel_id=1, source_target_pairs={{0,7},{1,0},{2,1},{3,2},{4,3},{5,4},{6,5},{7,6},{8,15},{9,8},{10,9... | collective-permute-start | bytes 884744 | tf_op jit(solution)/shard_map/ppermute | solution.py:569
  48.8 25.0 %collective-permute-start.12 = (f32[752,128]{1,0:T(8,128)S(1)}, f32[752,128]{1,0:T(8,128)S(1)}, u32[]{:S(2)}, u32[]{:S(2)}) collective-permute-start(f32[752,128]{1,0:T(8,128)S(1)} %get-tuple-element.51), channel_id=1, source_target_pairs={{0,64},{64,128},{128,192},{192,0},{1,65},{65,129},{129,193},{193,1... | collective-permute-start | bytes 1155080 | tf_op jit(solution)/shard_map/ppermute | solution.py:569
  50.5 4.6 %collective-permute-start.4 = (f32[4,16,128]{2,1,0:T(8,128)S(1)}, f32[4,16,128]{2,1,0:T(8,128)S(1)}, u32[]{:S(2)}, u32[]{:S(2)}) collective-permute-start(f32[4,16,128]{2,1,0:T(8,128)S(1)} %get-tuple-element.40), channel_id=1, source_target_pairs={{0,8},{8,16},{16,24},{24,32},{32,40},{40,48},{48,56},{56,0},{1,9},... | collective-permute-start | bytes 98312 | tf_op jit(solution)/shard_map/ppermute | solution.py:569
  50.5 4.6 %collective-permute-start.5 = (f32[4,16,128]{2,1,0:T(8,128)S(1)}, f32[4,16,128]{2,1,0:T(8,128)S(1)}, u32[]{:S(2)}, u32[]{:S(2)}) collective-permute-start(f32[4,16,128]{2,1,0:T(8,128)S(1)} %get-tuple-element.41), channel_id=1, source_target_pairs={{0,56},{8,0},{16,8},{24,16},{32,24},{40,32},{48,40},{56,48},{1,57}... | collective-permute-start | bytes 98312 | tf_op jit(solution)/shard_map/ppermute | solution.py:569
  53.4 20.4 %collective-permute-start.11 = (f32[256,256]{1,0:T(8,128)S(1)}, f32[256,256]{1,0:T(8,128)S(1)}, u32[]{:S(2)}, u32[]{:S(2)}) collective-permute-start(f32[256,256]{1,0:T(8,128)S(1)} %get-tuple-element.31.last), channel_id=1, source_target_pairs={{0,64},{64,128},{128,192},{192,0},{1,65},{65,129},{129,193},{193,1... | collective-permute-start | bytes 786440 | tf_op jit(solution)/shard_map/ppermute | solution.py:569
  55.2 5.1 %collective-permute-start.6 = (f32[160,128]{1,0:T(8,128)S(1)}, f32[160,128]{1,0:T(8,128)S(1)}, u32[]{:S(2)}, u32[]{:S(2)}) collective-permute-start(f32[160,128]{1,0:T(8,128)S(1)} %get-tuple-element.44), channel_id=1, source_target_pairs={{0,1},{1,2},{2,3},{3,4},{4,5},{5,6},{6,7},{7,0},{8,9},{9,10},{10,1... | collective-permute-start | bytes 245768 | tf_op jit(solution)/shard_map/ppermute | solution.py:569
  58.2 4.4 %collective-permute-start.7 = (f32[160,128]{1,0:T(8,128)S(1)}, f32[160,128]{1,0:T(8,128)S(1)}, u32[]{:S(2)}, u32[]{:S(2)}) collective-permute-start(f32[160,128]{1,0:T(8,128)S(1)} %get-tuple-element.45), channel_id=1, source_target_pairs={{0,7},{1,0},{2,1},{3,2},{4,3},{5,4},{6,5},{7,6},{8,15},{9,8},{10,9... | collective-permute-start | bytes 245768 | tf_op jit(solution)/shard_map/ppermute | solution.py:569
  68.2 23.1 %collective-permute-start.8 = (f32[336,128]{1,0:T(8,128)S(1)}, f32[336,128]{1,0:T(8,128)S(1)}, u32[]{:S(2)}, u32[]{:S(2)}) collective-permute-start(f32[336,128]{1,0:T(8,128)S(1)} %get-tuple-element.46), channel_id=1, source_target_pairs={{0,64},{64,128},{128,192},{192,0},{1,65},{65,129},{129,193},{193,1... | collective-permute-start | bytes 516104 | tf_op jit(solution)/shard_map/ppermute | solution.py:569
  69.9 21.4 %collective-permute-start.9 = (f32[168,128]{1,0:T(8,128)S(1)}, f32[168,128]{1,0:T(8,128)S(1)}, u32[]{:S(2)}, u32[]{:S(2)}) collective-permute-start(f32[168,128]{1,0:T(8,128)S(1)} %get-tuple-element.47), channel_id=1, source_target_pairs={{0,128},{64,192},{128,0},{192,64},{1,129},{65,193},{129,1},{193,65... | collective-permute-start | bytes 258056 | tf_op jit(solution)/shard_map/ppermute | solution.py:569
  71.4 19.9 %collective-permute-start.10 = (f32[168,128]{1,0:T(8,128)S(1)}, f32[168,128]{1,0:T(8,128)S(1)}, u32[]{:S(2)}, u32[]{:S(2)}) collective-permute-start(f32[168,128]{1,0:T(8,128)S(1)} %get-tuple-element.48), channel_id=1, source_target_pairs={{0,192},{64,0},{128,64},{192,128},{1,193},{65,1},{129,65},{193,129... | collective-permute-start | bytes 258056 | tf_op jit(solution)/shard_map/ppermute | solution.py:569

commit v2 on v0

v2 whole, which is shorter than its diff:
```python
import jax
import jax.numpy as jnp
from jax import lax
from jax.experimental import pallas as pl
from jax.experimental.pallas import tpu as pltpu
from jax.sharding import PartitionSpec as P

FACTOR = 4
N = 256
HALO = 16
EXT = N + 2 * HALO
V = EXT // 8
C = N // 2
CEXT = C + 2 * HALO
CV = CEXT // 8
HALF = EXT // 2
HV = HALF // 8
FIELDS = 11
MID, LAST, COEF = 8, 9, 10
F32 = jnp.float32
LIMIT = 24 * 1024 * 1024

VM = pl.BlockSpec(memory_space=pltpu.VMEM)
HB = pl.BlockSpec(memory_space=pltpu.HBM)


def call(body, outs, ins, scratch=(), aliases=None, name=None, flops=0):
    return pl.pallas_call(
        body,
        out_shape=[jax.ShapeDtypeStruct(s, F32) for s in outs],
        in_specs=[VM] * ins if isinstance(ins, int) else ins,
        out_specs=[VM] * len(outs),
        scratch_shapes=list(scratch),
        input_output_aliases=aliases or {},
        name=name,
        compiler_params=pltpu.CompilerParams(vmem_limit_bytes=LIMIT),
        cost_estimate=pl.CostEstimate(flops=flops, bytes_accessed=1000, transcendentals=0),
    )


def lanes(rows):
    return lax.broadcasted_iota(jnp.int32, (rows, 128), 1)


def roll(x, by):
    by %= 128
    return pltpu.roll(x, by, 1) if by else x


def flag(condition):
    return jnp.where(condition, 1.0, 0.0).astype(F32)


def vec(v):
    return slice(8 * v, 8 * v + 8)


def mix(dest, read, count):
    for v in range(count):
        dest[vec(v), :] = read(v)


def natural(ref, count, offset=0):
    return lambda v: ref[pl.ds(offset + v, 8, stride=count), :]


def unmix(dest, read, count):
    for v in range(count):
        dest[pl.ds(v, 8, stride=count), :] = read(v)


def sweep(src, fields, cols, count, emit):
    lane = lanes(8)
    first, last = lane == 0, lane == 127
    held = {}

    def at(f, j, v):
        if (f, j, v) not in held:
            held[f, j, v] = src[f, j, vec(v), :]
        return held[f, j, v]

    for v in range(count):
        for f in fields:
            mid = [at(f, j, v) for j in range(cols)]
            left = [pltpu.roll(m, 1, 1) for m in mid]
            right = [pltpu.roll(m, 127, 1) for m in mid]
            for j in range(cols):
                below = at(f, j, v + 1) if v + 1 < count else pltpu.roll(src[f, j, vec(0), :], 7, 0)
                above = at(f, j, v - 1) if v else pltpu.roll(src[f, j, vec(count - 1), :], 1, 0)
                side = jnp.where(first, left[j - 1], left[j]) + jnp.where(last, right[(j + 1) % cols], right[j])
                emit(f, j, v, mid[j], (below + above) + side)
        for key in [k for k in held if k[2] < v]:
            del held[key]


def step(rhs, mid, scaled, inv, cof, fields, cols, count, after):
    def one(f, j, v, own, total):
        b = own * inv[j, vec(v), :]
        scaled[f, j, vec(v), :] = b
        mid[f, j, vec(v), :] = b + cof[j, vec(v), :] * total

    def two(f, j, v, own, total):
        u = scaled[f, j, vec(v), :] + cof[j, vec(v), :] * total
        rhs[f, j, vec(v), :] = after(f, j, v, u)

    sweep(rhs, fields, cols, count, one)
    sweep(mid, fields, cols, count, two)


def keep(f, j, v, u):
    return u


def repeat(count, body):
    def one(k, carry):
        body(k)
        return carry

    lax.fori_loop(0, count, one, 0)


def restrict(ref, f, pair):
    fine = lax.broadcasted_iota(jnp.int32, (128, C), 0) // 2
    coarse = lax.broadcasted_iota(jnp.int32, (128, C), 1)
    out = None
    for j in range(2):
        for i in range(HV):
            pair[vec(i), :] = ref[f, j, vec(2 * i), :] + ref[f, j, vec(2 * i + 1), :]
        pick = jnp.where(fine + 64 * j == coarse, 0.25, 0.0).astype(F32)
        part = jnp.dot(pair[...], pick, precision=lax.Precision.HIGHEST, preferred_element_type=F32)
        out = part if out is None else out + part
    return out


def strips_body(source, iterate, start, conduct, up, down, last, sems):
    is_end = lax.axis_index("tm") == lax.axis_size("tm") - 1
    low, high = pl.ds(0, HALO), pl.ds(N - HALO, HALO)
    copies = []
    for ref, rows in ((up, low), (down, high)):
        copies.append((source.at[:, rows, :], ref.at[pl.ds(0, 8)]))
        copies.append((iterate.at[3, rows, :], ref.at[MID]))
        copies.append((conduct.at[rows, :], ref.at[COEF]))
    copies = [pltpu.make_async_copy(a, b, sems.at[i]) for i, (a, b) in enumerate(copies)]
    for c in copies:
        c.start()

    @pl.when(is_end)
    def _():
        c = pltpu.make_async_copy(start, last, sems.at[6])
        c.start()
        c.wait()

    @pl.when(jnp.logical_not(is_end))
    def _():
        c = pltpu.make_async_copy(iterate.at[7], last, sems.at[6])
        c.start()
        c.wait()

    up[LAST] = last[0:HALO, :]
    down[LAST] = last[N - HALO : N, :]
    for c in copies:
        c.wait()


def pack_edges(pieces, rows):
    lane = lanes(rows)
    low = [jnp.zeros((rows, 128), F32) for _ in range((len(pieces) + 7) // 8)]
    high = list(low)
    for f, (head, tail) in enumerate(pieces):
        at, k = HALO * (f % 8), f // 8
        inside = (lane >= at) & (lane < at + HALO)
        low[k] = jnp.where(inside, roll(head, at), low[k])
        high[k] = jnp.where(inside, roll(tail, at + HALO), high[k])
    return low, high


REST = HALO * (FIELDS - 8)


def center_body(source, iterate, last, conduct, ext, low, high, src, middle, coef, wide, sems):
    pairs = ((source, src), (iterate.at[3], middle), (conduct, coef))
    copies = [pltpu.make_async_copy(a, b, sems.at[i]) for i, (a, b) in enumerate(pairs)]
    for c in copies:
        c.start()
    for c in copies:
        c.wait()
    refs = [src.at[f] for f in range(8)] + [middle, last, coef]
    rows = 16

    def chunk(i, carry):
        base = pl.multiple_of(i * rows, 8)
        pieces = [(ref[pl.ds(base, rows), :128], ref[pl.ds(base, rows), 128:]) for ref in refs]
        lo, hi = pack_edges(pieces, rows)
        for ref, got in ((low, lo), (high, hi)):
            ref[pl.ds(base, rows), :] = got[0]
            @pl.when(i < 8)
            def _(ref=ref, got=got):
                ref[pl.ds(N + base, rows), :] = got[1]

            @pl.when(i >= 8)
            def _(ref=ref, got=got):
                at = pl.ds(N + base - 128, rows)
                ref[at, :] = jnp.where(lanes(rows) < REST, ref[at, :], roll(got[1], REST))
        return carry

    lax.fori_loop(0, N // rows, chunk, 0)
    zero = jnp.zeros((HALO, 128), F32)
    wide[0:HALO, :] = zero
    wide[HALO + N : EXT, :] = zero
    for f, ref in enumerate(refs):
        for j in range(2):
            wide[HALO : HALO + N, :] = ref[:, 128 * j : 128 * j + 128]
            mix(ext.at[f, j], natural(wide, V), V)


def corners_body(above, below, low, high):
    place, ends = lax.axis_index("sx"), lax.axis_size("sx") - 1
    lane = lanes(HALO)
    got = []
    for ref, present in ((above, flag(place > 0)), (below, flag(place < ends))):
        pieces = [(ref[f, :, :128] * present, ref[f, :, 128:] * present) for f in range(FIELDS)]
        got.append(pack_edges(pieces, HALO))
    for k, ref in ((0, low), (1, high)):
        ref[0:HALO, :] = got[0][k][0]
        ref[HALO : 2 * HALO, :] = got[1][k][0]
        ref[2 * HALO : 3 * HALO, :] = jnp.where(lane < REST, got[0][k][1], roll(got[1][k][1], REST))


def side_column(before, after, f, rows, first, final):
    lane = lanes(rows)
    at = HALO * (f % 8)
    right = jnp.where(lane < HALO, roll(after, -at) * final, 0.0)
    return jnp.where(lane >= 128 - HALO, roll(before, -HALO - at) * first, right)


PART1 = 2 * EXT
PART2 = PART1 + 4 * HALO
MAIN = PART2 + EXT // 2


def fold(dest, base, columns, width, groups, rows_in):
    span = 2 * width
    rows = rows_in // groups
    lane = lanes(rows)
    out = jnp.zeros((rows, 128), F32)
    for g in range(groups):
        for k, read in enumerate(columns):
            at = (g * len(columns) + k) * span
            inside = (lane >= at) & (lane < at + span)
            out = jnp.where(inside, roll(read(g * rows, rows), width + at), out)
    dest[base : base + rows, :] = out


def unfold(src, base, k, count, width, groups, rows_in, write):
    span = 2 * width
    rows = rows_in // groups
    lane = lanes(rows)
    for g in range(groups):
        at = (g * count + k) * span
        x = roll(src[base : base + rows, :], -width - at)
        write(g * rows, rows, jnp.where((lane < width) | (lane >= 128 - width), x, 0.0))


def local_body(
    ext_in, above, below, before, after, before_c, after_c,
    ext, coefs, forced, own_new, main, up, down, low_c, high_c, coarse,
    rhs, mid, scaled, wide, pair, rows_c,
):
    del ext_in
    t, x, z = lax.axis_index("tm"), lax.axis_index("sx"), lax.axis_index("sy")
    not_end = flag(t < lax.axis_size("tm") - 1)
    x_first, x_final = flag(x > 0), flag(x < lax.axis_size("sx") - 1)
    z_first, z_final = flag(z > 0), flag(z < lax.axis_size("sy") - 1)
    inv, cof = coefs.at[0], coefs.at[1]
    for f in range(FIELDS):
        for j in range(2):
            cols = slice(128 * j, 128 * j + 128)
            for h in range(2):
                part = slice(8 * h, 8 * h + 8)
                ext[f, j, pl.ds(64 * h, 8, stride=8), :] = above[f, part, cols] * x_first
                ext[f, j, pl.ds(8 * (V - HALO) + 64 * h + 7, 8, stride=8), :] = below[f, part, cols] * x_final
    for k, (own, corner) in enumerate(((before, before_c), (after, after_c))):
        wide[k, 0, 0:HALO, :] = corner[0:HALO, :]
        wide[k, 0, HALO : HALO + N, :] = own[0:N, :]
        wide[k, 0, HALO + N : EXT, :] = corner[HALO : 2 * HALO, :]
        rest = corner[2 * HALO : 3 * HALO, :]
        wide[k, 1, 0:HALO, :] = rest
        wide[k, 1, HALO : HALO + 128, :] = own[N : N + 128, :]
        wide[k, 1, HALO + 128 : HALO + N, :] = roll(own[N : N + 128, :], -REST)
        wide[k, 1, HALO + N : EXT, :] = roll(rest, -REST)
    for v in range(V):
        for g in range(2):
            left, right = natural(wide.at[0, g], V)(v), natural(wide.at[1, g], V)(v)
            for f in range(8 * g, min(8 * g + 8, FIELDS)):
                ext[f, 2, vec(v), :] = side_column(left, right, f, 8, z_first, z_final)
    for v in range(V):
        for j in range(3):
            c = ext[COEF, j, vec(v), :]
            r = 1.0 / (1.0 + 4.0 * c)
            inv[j, vec(v), :] = r
            cof[j, vec(v), :] = c * r
            rhs[0, j, vec(v), :] = ext[MID, j, vec(v), :] + ext[4, j, vec(v), :]
            rhs[1, j, vec(v), :] = ext[0, j, vec(v), :]
            rhs[2, j, vec(v), :] = ext[LAST, j, vec(v), :]

    def forced_step(k):
        def add(f, j, v, u):
            return u if f == 2 else u + ext[(5 if f == 0 else 1) + k, j, vec(v), :]

        step(rhs, mid, scaled, inv, cof, range(3), 3, V, add)

    repeat(FACTOR - 1, forced_step)

    def between():
        for v in range(V):
            for j in range(3):
                new, old = rhs[0, j, vec(v), :], ext[LAST, j, vec(v), :]
                moved = not_end * (new - old)
                if j < 2:
                    own_new[j, vec(v), :] = new
                    main[EXT * j + 8 * v : EXT * j + 8 * v + 8, :] = old + moved
                else:
                    scaled[0, j, vec(v), :] = old + moved
                rhs[0, j, vec(v), :] = moved
                s = rhs[1, j, vec(v), :]
                forced[j, vec(v), :] = s
                rhs[1, j, vec(v), :] = s - ext[MID, j, vec(v), :]
        for j in range(2):
            cols = slice(128 * j, 128 * j + 128)
            at = PART1 + 2 * HALO * j
            main[at : at + HALO, :] = above[LAST, :, cols] * x_first
            main[at + HALO : at + 2 * HALO, :] = below[LAST, :, cols] * x_final
        fold(
            main, PART2,
            [lambda r, n: scaled[0, 2, r : r + n, :], lambda r, n: ext[LAST, 2, r : r + n, :]],
            HALO, 2, EXT,
        )

    def free_step(k):
        step(rhs, mid, scaled, inv, cof, range(3), 3, V, keep)
        pl.when(k == 0)(between)

    repeat(FACTOR + 1, free_step)
    for k, (ref, f) in enumerate(((rhs, 1), (rhs, 0), (rhs, 2), (ext, COEF))):
        got = restrict(ref, f, pair)
        pair[...] = got
        unmix(rows_c, lambda v: pair[vec(v), :], HV)
        coarse[k] = rows_c[8 : 8 + C, :]
    for k in range(4):
        up[k] = coarse[k, 0:HALO, :]
        down[k] = coarse[k, C - HALO : C, :]
    lo, hi = pack_edges([(coarse[k], coarse[k]) for k in range(4)], C)
    low_c[...] = lo[0]
    high_c[...] = hi[0]


def coarse_edges_body(above, below, low_c, high_c, low, high):
    place, ends = lax.axis_index("sx"), lax.axis_size("sx") - 1
    low[HALO : HALO + C, :] = low_c[...]
    high[HALO : HALO + C, :] = high_c[...]
    for ref, base, present in ((above, 0, flag(place > 0)), (below, HALO + C, flag(place < ends))):
        lo, hi = pack_edges([(ref[k] * present,) * 2 for k in range(4)], HALO)
        low[base : base + HALO, :] = lo[0]
        high[base : base + HALO, :] = hi[0]


ONE = 2 * CEXT + CEXT // 4
TWO = CEXT + CEXT // 5


def coarse_body(coarse, above, below, before, after, one, two, three, four, coefs, ext, rhs, mid, scaled, wide):
    t, x, z = lax.axis_index("tm"), lax.axis_index("sx"), lax.axis_index("sy")
    not_end = flag(t < lax.axis_size("tm") - 1)
    x_first, x_final = flag(x > 0), flag(x < lax.axis_size("sx") - 1)
    z_first, z_final = flag(z > 0), flag(z < lax.axis_size("sy") - 1)
    for k in range(4):
        wide[0:HALO, :] = above[k] * x_first
        wide[HALO : HALO + C, :] = coarse[k]
        wide[HALO + C : CEXT, :] = below[k] * x_final
        mix(ext.at[k, 0], natural(wide, CV), CV)
    for v in range(CV):
        left, right = natural(before, CV)(v), natural(after, CV)(v)
        for k in range(4):
            ext[k, 1, vec(v), :] = side_column(left, right, k, 8, z_first, z_final)
    inv, cof = coefs.at[0], coefs.at[1]
    for j in range(2):
        c = ext[3, j]
        r = 1.0 / (1.0 + 4.0 * c)
        inv[j] = r
        cof[j] = c * r
        rhs[0, j] = ext[0, j] * not_end
        rhs[1, j] = ext[1, j]

    def advance(fields, after_step):
        step(rhs, mid, scaled, inv, cof, fields, 2, CV, after_step)

    def reader(ref, f):
        return lambda r, n: ref[f, 1, r : r + n, :]

    one[0:CEXT, :] = ext[0, 0]
    one[CEXT : 2 * CEXT, :] = ext[1, 0]
    fold(one, 2 * CEXT, [reader(ext, 0), reader(ext, 1)], 8, 4, CEXT)
    advance(range(2), lambda f, j, v, u: u if f == 0 else u + ext[2, j, vec(v), :])
    for j in range(2):
        ext[2, j] = rhs[1, j]
    advance(range(2), lambda f, j, v, u: u + ext[2, j, vec(v), :] if f == 0 else u)
    two[0:CEXT, :] = rhs[0, 0]
    fold(two, CEXT, [reader(rhs, 0)], 8, 5, CEXT)
    repeat(2, lambda k: advance(range(2), keep))
    three[0:CEXT, :] = rhs[0, 0]
    fold(three, CEXT, [reader(rhs, 0)], 8, 5, CEXT)
    advance(range(1, 2), keep)
    for j in range(2):
        four[j] = rhs[1, j]


def arrive_body(last, main, ext, coefs, forced, resid, new_start, new_mid, coarse_mid, rhs, mid, scaled, wide, pair):
    inv, cof = coefs.at[0], coefs.at[1]
    for j in range(2):
        at = PART1 + 2 * HALO * j
        wide[0:HALO, :] = main[at : at + HALO, :]
        wide[HALO : HALO + N, :] = last[:, 128 * j : 128 * j + 128]
        wide[HALO + N : EXT, :] = main[at + HALO : at + 2 * HALO, :]
        mix(rhs.at[0, j], natural(wide, V), V)
        new_start[j] = main[EXT * j : EXT * (j + 1), :]

    def put_new(r, n, value):
        new_start[2, r : r + n, :] = value

    def put_old(r, n, value):
        rhs[0, 2, r : r + n, :] = value

    unfold(main, PART2, 0, 2, HALO, 2, EXT, put_new)
    unfold(main, PART2, 1, 2, HALO, 2, EXT, put_old)
    for j in range(3):
        rhs[1, j] = new_start[j] - rhs[0, j]
    repeat(FACTOR, lambda k: step(rhs, mid, scaled, inv, cof, range(2), 3, V, keep))
    for j in range(3):
        for v in range(V):
            u = rhs[0, j, vec(v), :] + forced[j, vec(v), :]
            new_mid[j, vec(v), :] = u
            rhs[0, j, vec(v), :] = u - ext[MID, j, vec(v), :]
    repeat(FACTOR, lambda k: step(rhs, mid, scaled, inv, cof, range(1), 3, V, keep))
    for k in range(2):
        for j in range(2):
            unmix(wide, lambda v: rhs[1 - k, j, vec(v), :], V)
            resid[k, :, 128 * j : 128 * j + 128] = wide[HALO : HALO + N, :]
    coarse_mid[...] = restrict(rhs, 0, pair)


def final_body(
    one, two, three, four, ccoefs, coarse_mid, ext, coefs, new_start, new_mid, own_new,
    out, err, cmid, cscaled, sent, fix, rhs, mid, scaled, wide, pair, rows_c,
):
    t = lax.axis_index("tm")
    m1, m2, m3 = flag(t > 0), flag(t > 1), flag(t > 2)
    inv, cof = ccoefs.at[0], ccoefs.at[1]

    def put(k):
        def write(r, n, value):
            sent[k, r : r + n, :] = value

        return write

    unfold(one, 2 * CEXT, 0, 2, 8, 4, CEXT, put(0))
    unfold(one, 2 * CEXT, 1, 2, 8, 4, CEXT, put(1))
    unfold(two, CEXT, 0, 1, 8, 5, CEXT, put(2))
    unfold(three, CEXT, 0, 1, 8, 5, CEXT, put(3))
    err[0, 0] = m1 * (one[0:CEXT, :] + two[0:CEXT, :]) + m2 * three[0:CEXT, :] + m3 * four[0]
    err[0, 1] = m1 * (sent[0] + sent[2]) + m2 * sent[3] + m3 * four[1]

    def spread(k, extra=None):
        src = lax.broadcasted_iota(jnp.int32, (128, 128), 0)
        dst = lax.broadcasted_iota(jnp.int32, (128, 128), 1)
        for c in range(2 if extra is None else 1):
            unmix(rows_c, lambda v: err[0, c, vec(v), :], CV)
            mix(pair, natural(rows_c, HV, 8), HV)
            value = pair[...] if extra is None else pair[...] + extra[...]
            for j in (0, 1) if c == 0 else (2,):
                if c == 0:
                    pick = src == dst // 2 + 64 * j
                else:
                    pick = ((dst < HALO) & (src == dst // 2)) | ((dst >= 128 - HALO) & (src == 64 + dst // 2))
                fix[k, j] = jnp.dot(value, flag(pick), precision=lax.Precision.HIGHEST, preferred_element_type=F32)

    spread(0)
    step(err, cmid, cscaled, inv, cof, range(1), 2, CV, keep)
    err[0, 0] += one[CEXT : 2 * CEXT, :]
    err[0, 1] += sent[1]
    spread(1)
    step(err, cmid, cscaled, inv, cof, range(1), 2, CV, keep)
    spread(2, coarse_mid)
    inv, cof = coefs.at[0], coefs.at[1]
    for v in range(V):
        for j in range(3):
            rhs[0, j, vec(v), :] = new_start[j, vec(v), :] + fix[0, j, vec(v // 2), :] + ext[0, j, vec(v), :]
            u = new_mid[j, vec(v), :] + fix[1, j, vec(v // 2), :]
            scaled[0, j, vec(v), :] = u
            rhs[1, j, vec(v), :] = u + ext[4, j, vec(v), :]
            if j < 2:
                scaled[1, j, vec(v), :] = own_new[j, vec(v), :] + fix[2, j, vec(v // 2), :]

    def give(at):
        for f in range(2):
            for j in range(2):
                unmix(wide, lambda v: scaled[f, j, vec(v), :], V)
                out[4 * f + at, :, 128 * j : 128 * j + 128] = wide[HALO : HALO + N, :]

    give(FACTOR - 1)

    def fine(k):
        def add(f, j, v, u):
            scaled[f, j, vec(v), :] = u
            return u + ext[4 * f + 1 + k, j, vec(v), :]

        step(rhs, mid, scaled, inv, cof, range(2), 3, V, add)
        give(k)

    repeat(FACTOR - 1, fine)


def ring(x, axis, by):
    count = lax.axis_size(axis)
    return lax.ppermute(x, axis, [(i, (i + by) % count) for i in range(count)])


def vmem(*shape):
    return pltpu.VMEM(shape, F32)


def shards(iterate, source, start_field, conduct):
    up, down, last = call(
        strips_body, [(FIELDS, HALO, N)] * 2 + [(N, N)], [HB] * 4, [pltpu.SemaphoreType.DMA((7,))], name="strips"
    )(source, iterate, start_field, conduct)
    above, below = ring(down, "sx", 1), ring(up, "sx", -1)
    last_in = ring(last, "tm", 1)
    ext, low, high = call(
        center_body,
        [(FIELDS, 3, EXT, 128), (N + 128, 128), (N + 128, 128)],
        [HB, HB, VM, HB],
        [vmem(8, N, N), vmem(N, N), vmem(N, N), vmem(EXT, 128), pltpu.SemaphoreType.DMA((3,))],
        name="center", flops=20_000_000,
    )(source, iterate, last, conduct)
    before, after = ring(high, "sy", 1), ring(low, "sy", -1)
    c_lo, c_hi = call(corners_body, [(3 * HALO, 128)] * 2, 2, name="corners")(above, below)
    before_c, after_c = ring(c_hi, "sy", 1), ring(c_lo, "sy", -1)
    before, after, before_c, after_c, last_in = lax.optimization_barrier((before, after, before_c, after_c, last_in))
    ext, coefs, forced, own_new, main, c_up, c_down, c_low, c_high, coarse = call(
        local_body,
        [
            (FIELDS, 3, EXT, 128), (2, 3, EXT, 128), (3, EXT, 128), (2, EXT, 128), (MAIN, 128),
            (4, HALO, 128), (4, HALO, 128), (C, 128), (C, 128), (4, C, 128),
        ],
        7, [vmem(3, 3, EXT, 128)] * 3 + [vmem(2, 2, EXT, 128), vmem(HALF, 128), vmem(HALF, 128)],
        {0: 0}, "local", 50_000_000,
    )(ext, above, below, before, after, before_c, after_c)
    c_above, c_below = ring(c_down, "sx", 1), ring(c_up, "sx", -1)
    main_in = ring(main, "tm", 1)
    c_lo, c_hi = call(coarse_edges_body, [(CEXT, 128)] * 2, 4, name="coarse_edges")(c_above, c_below, c_low, c_high)
    c_before, c_after = ring(c_hi, "sy", 1), ring(c_lo, "sy", -1)
    one, two, three, four, ccoefs = call(
        coarse_body,
        [(ONE, 128), (TWO, 128), (TWO, 128), (2, CEXT, 128), (2, 2, CEXT, 128)],
        5,
        [vmem(4, 2, CEXT, 128)] + [vmem(2, 2, CEXT, 128)] * 3 + [vmem(CEXT, 128)],
        name="coarse",
    )(coarse, c_above, c_below, c_before, c_after)
    one, two, three = ring(one, "tm", 1), ring(two, "tm", 2), ring(three, "tm", 3)
    resid, new_start, new_mid, coarse_mid = call(
        arrive_body,
        [(2, N, N), (3, EXT, 128), (3, EXT, 128), (HALF, 128)],
        5, [vmem(2, 3, EXT, 128)] * 3 + [vmem(EXT, 128), vmem(HALF, 128)], name="arrive", flops=30_000_000,
    )(last_in, main_in, ext, coefs, forced)
    (updated,) = call(
        final_body,
        [(8, N, N)],
        11,
        [vmem(1, 2, CEXT, 128)] * 3 + [vmem(4, CEXT, 128), vmem(3, 3, HALF, 128)] + [vmem(2, 3, EXT, 128)] * 3
        + [vmem(EXT, 128), vmem(HALF, 128), vmem(CEXT, 128)],
        name="final",
    )(one, two, three, four, ccoefs, coarse_mid, ext, coefs, new_start, new_mid, own_new)
    return updated, resid


def solution(mesh):
    in_specs = (P("tm", "sx", "sy"), P("tm", "sx", "sy"), P("sx", "sy"), P("sx", "sy"))
    out_specs = (P("tm", "sx", "sy"), P("tm", "sx", "sy"))
    return jax.shard_map(shards, mesh=mesh, in_specs=in_specs, out_specs=out_specs, check_vma=False)
```

time: 621 us -> 72.4 us (0.12)
  the two profiles are of different devices: /device:TPU:9 before, /device:TPU:64 now
where the time goes in v2:
time: 72.4 us; the launch traced here: 72.2 us
  Pallas kernels  33.3 us (46%)
  starting transfers between devices  22 us (30%)
  waiting for transfers between devices  11.1 us (15%)
  local copies, waits for them, and re-layouts  5.08 us (7%)
    ppermute x15, starting transfers between devices, ring(): return lax.ppermute(x, axis, [(i, (i + by) % count) for i in range(count)])  22 us
    pallas_call x1, Pallas kernels, shards(): call(local_body, [(FIELDS, 3, EXT, 128), (2, 3, EXT, 128), (3, EXT, 128),...  13.4 us
    ppermute x15, waiting for transfers between devices, ring(): return lax.ppermute(x, axis, [(i, (i + by) % count) for i in range(count)])  11.1 us
    pallas_call x1, Pallas kernels, shards(): call(arrive_body, [(2, N, N), (3, EXT, 128), (3, EXT, 128), (HALF, 128)],...  7.5 us
    pallas_call x1, Pallas kernels, shards(): call(final_body, [(8, N, N)], 11, [vmem(1, 2, CEXT, 128)] * 3 + [vmem(4,...  6.09 us
    unnamed x10, local copies, waits for them, and re-layouts  5.08 us
    pallas_call x1, Pallas kernels, shards(): call(center_body, [(FIELDS, 3, EXT, 128), (N + 128, 128), (N + 128, 128)]...  3.64 us
    pallas_call x1, Pallas kernels, shards(): call(coarse_body, [(ONE, 128), (TWO, 128), (TWO, 128), (2, CEXT, 128), (2...  2.16 us
  transfers between devices with their start and end apart: 15, of which 6 were waited for; matrix products, arithmetic and copies ran while one was open for 0% of the time, Pallas kernels for 19%

profile of v2, /device:TPU:64, one launch (start us, length us, event | category | flops | bytes accessed | tf_op | source)
XLA Modules:
  0.0 72.2 jit_solution(14175541726671594974)
XLA Ops:
  0.6 0.0 copy-start
  0.6 1.6 %copy-done = f32[8,256,256]{2,1,0:T(8,128)S(1)} copy-done((f32[8,256,256]{2,1,0:T(8,128)S(1)}, f32[8,256,256]{2,1,0:T(8,128)}, u32[]{:S(2)}) %copy-start) | copy-done | bytes 2097176
  2.2 0.0 copy-start.1
  2.2 1.6 %copy-done.1 = f32[8,256,256]{2,1,0:T(8,128)S(1)} copy-done((f32[8,256,256]{2,1,0:T(8,128)S(1)}, f32[8,256,256]{2,1,0:T(8,128)}, u32[]{:S(2)}) %copy-start.1) | copy-done | bytes 2097176
  3.8 0.0 copy-start.2
  3.8 0.9 %copy-done.2 = f32[256,256]{1,0:T(8,128)S(1)} copy-done((f32[256,256]{1,0:T(8,128)S(1)}, f32[256,256]{1,0:T(8,128)}, u32[]{:S(2)}) %copy-start.2) | copy-done | bytes 262168
  4.8 0.0 copy-start.4
  4.8 0.9 %copy-done.4 = f32[256,256]{1,0:T(8,128)S(1)} copy-done((f32[256,256]{1,0:T(8,128)S(1)}, f32[256,256]{1,0:T(8,128)}, u32[]{:S(2)}) %copy-start.4) | copy-done | bytes 262168
  5.7 0.0 copy-start.3
  5.7 0.2 strips.1
  6.0 1.7 %collective-permute-start.6 = (f32[256,256]{1,0:T(8,128)S(1)}, f32[256,256]{1,0:T(8,128)S(1)}, u32[]{:S(2)}, u32[]{:S(2)}) collective-permute-start(f32[256,256]{1,0:T(8,128)S(1)} %get-tuple-element.36.last), channel_id=1, source_target_pairs={{0,64},{64,128},{128,192},{192,0},{1,65},{65,129},{129,193},{193,1... | collective-permute-start | bytes 786440 | tf_op jit(solution)/shard_map/ppermute | solution.py:524
  7.6 0.0 collective-permute-start
  7.6 3.0 %collective-permute-start.1 = (f32[11,16,256]{2,1,0:T(8,128)S(1)}, f32[11,16,256]{2,1,0:T(8,128)S(1)}, u32[]{:S(2)}, u32[]{:S(2)}) collective-permute-start(f32[11,16,256]{2,1,0:T(8,128)S(1)} %get-tuple-element.39), channel_id=1, source_target_pairs={{0,56},{8,0},{16,8},{24,16},{32,24},{40,32},{48,40},{56,48},{1,57}... | collective-permute-start | bytes 540680 | tf_op jit(solution)/shard_map/ppermute | solution.py:524
  10.6 0.0 copy-done.3
  10.6 3.6 %center.1 = (f32[11,3,288,128]{3,2,1,0:T(8,128)S(1)}, f32[384,128]{1,0:T(8,128)S(1)}, f32[384,128]{1,0:T(8,128)S(1)}) custom-call(f32[8,256,256]{2,1,0:T(8,128)S(1)} %copy-done, f32[8,256,256]{2,1,0:T(8,128)S(1)} %copy-done.1, f32[256,256]{1,0:T(8,128)S(1)} %get-tuple-element.36.last, f32[256,256]{1,0:T(8,128)S(1)} %copy-done.3), custom_call_target="tpu_custom_call" | custom-call | flops 20000000 | bytes 1000 | tf_op jit(solution)/shard_map/center/pallas_call | solution.py:537
  14.2 2.0 %collective-permute-start.2 = (f32[384,128]{1,0:T(8,128)S(1)}, f32[384,128]{1,0:T(8,128)S(1)}, u32[]{:S(2)}, u32[]{:S(2)}) collective-permute-start(f32[384,128]{1,0:T(8,128)S(1)} %get-tuple-element.40), channel_id=1, source_target_pairs={{0,1},{1,2},{2,3},{3,4},{4,5},{5,6},{6,7},{7,0},{8,9},{9,10},{10,1... | collective-permute-start | bytes 589832 | tf_op jit(solution)/shard_map/ppermute | solution.py:524
  16.2 0.1 collective-permute-start.3
  16.3 0.0 collective-permute-done.above
  16.3 0.0 collective-permute-done.1.below
  16.3 0.2 corners.1
  16.5 3.1 %collective-permute-start.4 = (f32[48,128]{1,0:T(8,128)S(1)}, f32[48,128]{1,0:T(8,128)S(1)}, u32[]{:S(2)}, u32[]{:S(2)}) collective-permute-start(f32[48,128]{1,0:T(8,128)S(1)} %get-tuple-element.42), channel_id=1, source_target_pairs={{0,1},{1,2},{2,3},{3,4},{4,5},{5,6},{6,7},{7,0},{8,9},{9,10},{10,1... | collective-permute-start | bytes 73736 | tf_op jit(solution)/shard_map/ppermute | solution.py:524
  19.6 0.0 collective-permute-start.5
  19.6 0.4 collective-permute-done.2.before
  20.0 3.2 %collective-permute-done.3.after = f32[384,128]{1,0:T(8,128)S(1)} collective-permute-done((f32[384,128]{1,0:T(8,128)S(1)}, f32[384,128]{1,0:T(8,128)S(1)}, u32[]{:S(2)}, u32[]{:S(2)}) %collective-permute-start.3) | collective-permute-done | bytes 196640 | tf_op jit(solution)/shard_map/ppermute | solution.py:524
  23.2 0.0 collective-permute-done.4.before_c
  23.2 1.4 %collective-permute-done.5.after_c = f32[48,128]{1,0:T(8,128)S(1)} collective-permute-done((f32[48,128]{1,0:T(8,128)S(1)}, f32[48,128]{1,0:T(8,128)S(1)}, u32[]{:S(2)}, u32[]{:S(2)}) %collective-permute-start.5) | collective-permute-done | bytes 24608 | tf_op jit(solution)/shard_map/ppermute | solution.py:524
  24.6 0.0 collective-permute-done.6.last
  24.6 13.4 %local.1 = (f32[11,3,288,128]{3,2,1,0:T(8,128)S(1)}, f32[2,3,288,128]{3,2,1,0:T(8,128)S(1)}, f32[3,288,128]{2,1,0:T(8,128)S(1)}, f32[2,288,128]{2,1,0:T(8,128)S(...) custom-call(f32[11,3,288,128]{3,2,1,0:T(8,128)S(1)} %get-tuple-eleme, ...), custom_call_target="tpu_custom_call", output_to_operand_aliasing={{0}: (0, {})} | custom-call | flops 50000000 | bytes 1000 | tf_op jit(solution)/shard_map/local/pallas_call | solution.py:548
  38.1 1.7 %collective-permute-start.14 = (f32[784,128]{1,0:T(8,128)S(1)}, f32[784,128]{1,0:T(8,128)S(1)}, u32[]{:S(2)}, u32[]{:S(2)}) collective-permute-start(f32[784,128]{1,0:T(8,128)S(1)} %get-tuple-element.61), channel_id=1, source_target_pairs={{0,64},{64,128},{128,192},{192,0},{1,65},{65,129},{129,193},{193,1... | collective-permute-start | bytes 1204232 | tf_op jit(solution)/shard_map/ppermute | solution.py:524
  39.7 0.0 collective-permute-start.7
  39.7 3.0 %collective-permute-start.8 = (f32[4,16,128]{2,1,0:T(8,128)S(1)}, f32[4,16,128]{2,1,0:T(8,128)S(1)}, u32[]{:S(2)}, u32[]{:S(2)}) collective-permute-start(f32[4,16,128]{2,1,0:T(8,128)S(1)} %get-tuple-element.50), channel_id=1, source_target_pairs={{0,56},{8,0},{16,8},{24,16},{32,24},{40,32},{48,40},{56,48},{1,57}... | collective-permute-start | bytes 98312 | tf_op jit(solution)/shard_map/ppermute | solution.py:524
  42.7 1.6 %collective-permute-done.7.above = f32[4,16,128]{2,1,0:T(8,128)S(1)} collective-permute-done((f32[4,16,128]{2,1,0:T(8,128)S(1)}, f32[4,16,128]{2,1,0:T(8,128)S(1)}, u32[]{:S(2)}, u32[]{:S(2)}) %collective-permute-start.7) | collective-permute-done | bytes 32800 | tf_op jit(solution)/shard_map/ppermute | solution.py:524
  44.3 0.0 collective-permute-done.8.below
  44.3 0.1 coarse_edges.1
  44.4 3.3 %collective-permute-start.9 = (f32[160,128]{1,0:T(8,128)S(1)}, f32[160,128]{1,0:T(8,128)S(1)}, u32[]{:S(2)}, u32[]{:S(2)}) collective-permute-start(f32[160,128]{1,0:T(8,128)S(1)} %get-tuple-element.53), channel_id=1, source_target_pairs={{0,1},{1,2},{2,3},{3,4},{4,5},{5,6},{6,7},{7,0},{8,9},{9,10},{10,1... | collective-permute-start | bytes 245768 | tf_op jit(solution)/shard_map/ppermute | solution.py:524
  47.7 0.0 collective-permute-start.10
  47.7 2.1 %collective-permute-done.9.before = f32[160,128]{1,0:T(8,128)S(1)} collective-permute-done((f32[160,128]{1,0:T(8,128)S(1)}, f32[160,128]{1,0:T(8,128)S(1)}, u32[]{:S(2)}, u32[]{:S(2)}) %collective-permute-start.9) | collective-permute-done | bytes 81952 | tf_op jit(solution)/shard_map/ppermute | solution.py:524
  49.8 2.4 %collective-permute-done.10.after = f32[160,128]{1,0:T(8,128)S(1)} collective-permute-done((f32[160,128]{1,0:T(8,128)S(1)}, f32[160,128]{1,0:T(8,128)S(1)}, u32[]{:S(2)}, u32[]{:S(2)}) %collective-permute-start.10) | collective-permute-done | bytes 81952 | tf_op jit(solution)/shard_map/ppermute | solution.py:524
  52.1 2.2 %coarse.1 = (f32[360,128]{1,0:T(8,128)S(1)}, f32[192,128]{1,0:T(8,128)S(1)}, f32[192,128]{1,0:T(8,128)S(1)}, f32[2,160,128]{2,1,0:T(8,128)S(1)}, f32[2,2,160,128]{3,2,1,0:T(8,128)S(1)}) custom-call(f32[4,128,128]{2,1,0:T(8,128)S(1)} %get-tuple-element.48.coarse, f32[4,16,128]{2,1,0:T(8,128)S(1)} %collective-permute-done.7.above, ...), custom_call_target="tpu_custom_call" | custom-call | bytes 1000 | tf_op jit(solution)/shard_map/coarse/pallas_call | solution.py:561
  54.3 1.4 %collective-permute-start.11 = (f32[360,128]{1,0:T(8,128)S(1)}, f32[360,128]{1,0:T(8,128)S(1)}, u32[]{:S(2)}, u32[]{:S(2)}) collective-permute-start(f32[360,128]{1,0:T(8,128)S(1)} %get-tuple-element.55), channel_id=1, source_target_pairs={{0,64},{64,128},{128,192},{192,0},{1,65},{65,129},{129,193},{193,1... | collective-permute-start | bytes 552968 | tf_op jit(solution)/shard_map/ppermute | solution.py:524
  55.7 1.8 %collective-permute-start.12 = (f32[192,128]{1,0:T(8,128)S(1)}, f32[192,128]{1,0:T(8,128)S(1)}, u32[]{:S(2)}, u32[]{:S(2)}) collective-permute-start(f32[192,128]{1,0:T(8,128)S(1)} %get-tuple-element.56), channel_id=1, source_target_pairs={{0,128},{64,192},{128,0},{192,64},{1,129},{65,193},{129,1},{193,65... | collective-permute-start | bytes 294920 | tf_op jit(solution)/shard_map/ppermute | solution.py:524
  57.5 1.1 %collective-permute-start.13 = (f32[192,128]{1,0:T(8,128)S(1)}, f32[192,128]{1,0:T(8,128)S(1)}, u32[]{:S(2)}, u32[]{:S(2)}) collective-permute-start(f32[192,128]{1,0:T(8,128)S(1)} %get-tuple-element.57), channel_id=1, source_target_pairs={{0,192},{64,0},{128,64},{192,128},{1,193},{65,1},{129,65},{193,129... | collective-permute-start | bytes 294920 | tf_op jit(solution)/shard_map/ppermute | solution.py:524
  58.6 0.0 collective-permute-done.14.main
  58.6 7.5 %arrive.1 = (f32[2,256,256]{2,1,0:T(8,128)}, f32[3,288,128]{2,1,0:T(8,128)S(1)}, f32[3,288,128]{2,1,0:T(8,128)S(1)}, f32[144,128]{1,0:T(8,128)S(1)}) custom-call(f32[256,256]{1,0:T(8,128)S(1)} %collective-permute-done.6.last, f32[784,128]{1,0:T(8,128)S(1)} %collective-permute-done.14.main, f32[11,3,288,128]{3,2,1,0:T(8,128)S(1)} %get-tuple-element.62.ext, ...), custom_call_target="tpu_custom_call" | custom-call | flops 30000000 | bytes 1000 | tf_op jit(solution)/shard_map/arrive/pallas_call | solution.py:569
  66.1 0.0 collective-permute-done.12.two
  66.1 0.0 collective-permute-done.13.three
  66.1 0.0 collective-permute-done.11.one
  66.1 6.1 %final.1 = f32[8,256,256]{2,1,0:T(8,128)} custom-call(f32[360,128]{1,0:T(8,128)S(1)} %collective-permute-done.11.one, f32[192,128]{1,0:T(8,128)S(1)} %collective-permute-done.12.two, f32[192,128]{1,0:T(8,128)S(1)} %collective-permute-done.13.three, f32[2,160,128]{2,1,0:T(8,128)S(1)} %get-tuple-element.58.four, ...), custom_call_target="tpu_custom_call" | custom-call | bytes 1000 | tf_op jit(solution)/shard_map/final/pallas_call | solution.py:574
Async XLA Ops:
  0.6 1.6 %copy-start = (f32[8,256,256]{2,1,0:T(8,128)S(1)}, f32[8,256,256]{2,1,0:T(8,128)}, u32[]{:S(2)}) copy-start(f32[8,256,256]{2,1,0:T(8,128)} %source.3) | copy-start | bytes 6291460
  2.2 1.6 %copy-start.1 = (f32[8,256,256]{2,1,0:T(8,128)S(1)}, f32[8,256,256]{2,1,0:T(8,128)}, u32[]{:S(2)}) copy-start(f32[8,256,256]{2,1,0:T(8,128)} %iterate.3) | copy-start | bytes 6291460
  3.8 0.9 %copy-start.2 = (f32[256,256]{1,0:T(8,128)S(1)}, f32[256,256]{1,0:T(8,128)}, u32[]{:S(2)}) copy-start(f32[256,256]{1,0:T(8,128)} %conduct.3) | copy-start | bytes 786436
  4.8 0.9 %copy-start.4 = (f32[256,256]{1,0:T(8,128)S(1)}, f32[256,256]{1,0:T(8,128)}, u32[]{:S(2)}) copy-start(f32[256,256]{1,0:T(8,128)} %start.1) | copy-start | bytes 786436
  5.7 4.9 %copy-start.3 = (f32[256,256]{1,0:T(8,128)S(1)}, f32[256,256]{1,0:T(8,128)}, u32[]{:S(2)}) copy-start(f32[256,256]{1,0:T(8,128)} %conduct.3) | copy-start | bytes 786436
  6.0 18.7 %collective-permute-start.6 = (f32[256,256]{1,0:T(8,128)S(1)}, f32[256,256]{1,0:T(8,128)S(1)}, u32[]{:S(2)}, u32[]{:S(2)}) collective-permute-start(f32[256,256]{1,0:T(8,128)S(1)} %get-tuple-element.36.last), channel_id=1, source_target_pairs={{0,64},{64,128},{128,192},{192,0},{1,65},{65,129},{129,193},{193,1... | collective-permute-start | bytes 786440 | tf_op jit(solution)/shard_map/ppermute | solution.py:524
  7.6 8.7 %collective-permute-start = (f32[11,16,256]{2,1,0:T(8,128)S(1)}, f32[11,16,256]{2,1,0:T(8,128)S(1)}, u32[]{:S(2)}, u32[]{:S(2)}) collective-permute-start(f32[11,16,256]{2,1,0:T(8,128)S(1)} %get-tuple-element.38), channel_id=1, source_target_pairs={{0,8},{8,16},{16,24},{24,32},{32,40},{40,48},{48,56},{56,0},{1,9},... | collective-permute-start | bytes 540680 | tf_op jit(solution)/shard_map/ppermute | solution.py:524
  7.6 8.7 %collective-permute-start.1 = (f32[11,16,256]{2,1,0:T(8,128)S(1)}, f32[11,16,256]{2,1,0:T(8,128)S(1)}, u32[]{:S(2)}, u32[]{:S(2)}) collective-permute-start(f32[11,16,256]{2,1,0:T(8,128)S(1)} %get-tuple-element.39), channel_id=1, source_target_pairs={{0,56},{8,0},{16,8},{24,16},{32,24},{40,32},{48,40},{56,48},{1,57}... | collective-permute-start | bytes 540680 | tf_op jit(solution)/shard_map/ppermute | solution.py:524
  14.2 5.8 %collective-permute-start.2 = (f32[384,128]{1,0:T(8,128)S(1)}, f32[384,128]{1,0:T(8,128)S(1)}, u32[]{:S(2)}, u32[]{:S(2)}) collective-permute-start(f32[384,128]{1,0:T(8,128)S(1)} %get-tuple-element.40), channel_id=1, source_target_pairs={{0,1},{1,2},{2,3},{3,4},{4,5},{5,6},{6,7},{7,0},{8,9},{9,10},{10,1... | collective-permute-start | bytes 589832 | tf_op jit(solution)/shard_map/ppermute | solution.py:524
  16.2 7.0 %collective-permute-start.3 = (f32[384,128]{1,0:T(8,128)S(1)}, f32[384,128]{1,0:T(8,128)S(1)}, u32[]{:S(2)}, u32[]{:S(2)}) collective-permute-start(f32[384,128]{1,0:T(8,128)S(1)} %get-tuple-element.41), channel_id=1, source_target_pairs={{0,7},{1,0},{2,1},{3,2},{4,3},{5,4},{6,5},{7,6},{8,15},{9,8},{10,9... | collective-permute-start | bytes 589832 | tf_op jit(solution)/shard_map/ppermute | solution.py:524
  16.5 6.8 %collective-permute-start.4 = (f32[48,128]{1,0:T(8,128)S(1)}, f32[48,128]{1,0:T(8,128)S(1)}, u32[]{:S(2)}, u32[]{:S(2)}) collective-permute-start(f32[48,128]{1,0:T(8,128)S(1)} %get-tuple-element.42), channel_id=1, source_target_pairs={{0,1},{1,2},{2,3},{3,4},{4,5},{5,6},{6,7},{7,0},{8,9},{9,10},{10,1... | collective-permute-start | bytes 73736 | tf_op jit(solution)/shard_map/ppermute | solution.py:524
  19.6 5.0 %collective-permute-start.5 = (f32[48,128]{1,0:T(8,128)S(1)}, f32[48,128]{1,0:T(8,128)S(1)}, u32[]{:S(2)}, u32[]{:S(2)}) collective-permute-start(f32[48,128]{1,0:T(8,128)S(1)} %get-tuple-element.43), channel_id=1, source_target_pairs={{0,7},{1,0},{2,1},{3,2},{4,3},{5,4},{6,5},{7,6},{8,15},{9,8},{10,9... | collective-permute-start | bytes 73736 | tf_op jit(solution)/shard_map/ppermute | solution.py:524
  38.1 20.5 %collective-permute-start.14 = (f32[784,128]{1,0:T(8,128)S(1)}, f32[784,128]{1,0:T(8,128)S(1)}, u32[]{:S(2)}, u32[]{:S(2)}) collective-permute-start(f32[784,128]{1,0:T(8,128)S(1)} %get-tuple-element.61), channel_id=1, source_target_pairs={{0,64},{64,128},{128,192},{192,0},{1,65},{65,129},{129,193},{193,1... | collective-permute-start | bytes 1204232 | tf_op jit(solution)/shard_map/ppermute | solution.py:524
  39.7 4.6 %collective-permute-start.7 = (f32[4,16,128]{2,1,0:T(8,128)S(1)}, f32[4,16,128]{2,1,0:T(8,128)S(1)}, u32[]{:S(2)}, u32[]{:S(2)}) collective-permute-start(f32[4,16,128]{2,1,0:T(8,128)S(1)} %get-tuple-element.49), channel_id=1, source_target_pairs={{0,8},{8,16},{16,24},{24,32},{32,40},{40,48},{48,56},{56,0},{1,9},... | collective-permute-start | bytes 98312 | tf_op jit(solution)/shard_map/ppermute | solution.py:524
  39.7 4.6 %collective-permute-start.8 = (f32[4,16,128]{2,1,0:T(8,128)S(1)}, f32[4,16,128]{2,1,0:T(8,128)S(1)}, u32[]{:S(2)}, u32[]{:S(2)}) collective-permute-start(f32[4,16,128]{2,1,0:T(8,128)S(1)} %get-tuple-element.50), channel_id=1, source_target_pairs={{0,56},{8,0},{16,8},{24,16},{32,24},{40,32},{48,40},{56,48},{1,57}... | collective-permute-start | bytes 98312 | tf_op jit(solution)/shard_map/ppermute | solution.py:524
  44.4 5.4 %collective-permute-start.9 = (f32[160,128]{1,0:T(8,128)S(1)}, f32[160,128]{1,0:T(8,128)S(1)}, u32[]{:S(2)}, u32[]{:S(2)}) collective-permute-start(f32[160,128]{1,0:T(8,128)S(1)} %get-tuple-element.53), channel_id=1, source_target_pairs={{0,1},{1,2},{2,3},{3,4},{4,5},{5,6},{6,7},{7,0},{8,9},{9,10},{10,1... | collective-permute-start | bytes 245768 | tf_op jit(solution)/shard_map/ppermute | solution.py:524
  47.7 4.4 %collective-permute-start.10 = (f32[160,128]{1,0:T(8,128)S(1)}, f32[160,128]{1,0:T(8,128)S(1)}, u32[]{:S(2)}, u32[]{:S(2)}) collective-permute-start(f32[160,128]{1,0:T(8,128)S(1)} %get-tuple-element.54), channel_id=1, source_target_pairs={{0,7},{1,0},{2,1},{3,2},{4,3},{5,4},{6,5},{7,6},{8,15},{9,8},{10,9... | collective-permute-start | bytes 245768 | tf_op jit(solution)/shard_map/ppermute | solution.py:524
  54.3 11.8 %collective-permute-start.11 = (f32[360,128]{1,0:T(8,128)S(1)}, f32[360,128]{1,0:T(8,128)S(1)}, u32[]{:S(2)}, u32[]{:S(2)}) collective-permute-start(f32[360,128]{1,0:T(8,128)S(1)} %get-tuple-element.55), channel_id=1, source_target_pairs={{0,64},{64,128},{128,192},{192,0},{1,65},{65,129},{129,193},{193,1... | collective-permute-start | bytes 552968 | tf_op jit(solution)/shard_map/ppermute | solution.py:524
  55.7 10.4 %collective-permute-start.12 = (f32[192,128]{1,0:T(8,128)S(1)}, f32[192,128]{1,0:T(8,128)S(1)}, u32[]{:S(2)}, u32[]{:S(2)}) collective-permute-start(f32[192,128]{1,0:T(8,128)S(1)} %get-tuple-element.56), channel_id=1, source_target_pairs={{0,128},{64,192},{128,0},{192,64},{1,129},{65,193},{129,1},{193,65... | collective-permute-start | bytes 294920 | tf_op jit(solution)/shard_map/ppermute | solution.py:524
  57.5 8.6 %collective-permute-start.13 = (f32[192,128]{1,0:T(8,128)S(1)}, f32[192,128]{1,0:T(8,128)S(1)}, u32[]{:S(2)}, u32[]{:S(2)}) collective-permute-start(f32[192,128]{1,0:T(8,128)S(1)} %get-tuple-element.57), channel_id=1, source_target_pairs={{0,192},{64,0},{128,64},{192,128},{1,193},{65,1},{129,65},{193,129... | collective-permute-start | bytes 294920 | tf_op jit(solution)/shard_map/ppermute | solution.py:524

commit v3 on v2

--- a/solution.py
+++ b/solution.py
@@ -17,6 +17,7 @@
 HV = HALF // 8
 FIELDS = 11
 MID, LAST, COEF = 8, 9, 10
+LIVE = EXT // 3
 F32 = jnp.float32
 LIMIT = 24 * 1024 * 1024
 
@@ -24,7 +25,7 @@
 HB = pl.BlockSpec(memory_space=pltpu.HBM)
 
 
-def call(body, outs, ins, scratch=(), aliases=None, name=None, flops=0):
+def call(body, outs, ins, scratch=(), aliases=None, name=None, flops=0, limit=LIMIT):
     return pl.pallas_call(
         body,
         out_shape=[jax.ShapeDtypeStruct(s, F32) for s in outs],
@@ -33,7 +34,7 @@
         scratch_shapes=list(scratch),
         input_output_aliases=aliases or {},
         name=name,
-        compiler_params=pltpu.CompilerParams(vmem_limit_bytes=LIMIT),
+        compiler_params=pltpu.CompilerParams(vmem_limit_bytes=limit),
         cost_estimate=pl.CostEstimate(flops=flops, bytes_accessed=1000, transcendentals=0),
     )
 
@@ -82,13 +83,18 @@
     for v in range(count):
         for f in fields:
             mid = [at(f, j, v) for j in range(cols)]
-            left = [pltpu.roll(m, 1, 1) for m in mid]
-            right = [pltpu.roll(m, 127, 1) for m in mid]
+            if cols == 3:
+                left = [pltpu.roll(mid[2], 1, 1), mid[0], mid[1]]
+                right = [mid[1], mid[2], pltpu.roll(mid[0], 127, 1)]
+            else:
+                back = [pltpu.roll(m, 1, 1) for m in mid]
+                ahead = [pltpu.roll(m, 127, 1) for m in mid]
+                left = [jnp.where(first, back[1 - j], back[j]) for j in range(2)]
+                right = [jnp.where(last, ahead[1 - j], ahead[j]) for j in range(2)]
             for j in range(cols):
                 below = at(f, j, v + 1) if v + 1 < count else pltpu.roll(src[f, j, vec(0), :], 7, 0)
                 above = at(f, j, v - 1) if v else pltpu.roll(src[f, j, vec(count - 1), :], 1, 0)
-                side = jnp.where(first, left[j - 1], left[j]) + jnp.where(last, right[(j + 1) % cols], right[j])
-                emit(f, j, v, mid[j], (below + above) + side)
+                emit(f, j, v, mid[j], (below + above) + (left[j] + right[j]))
         for key in [k for k in held if k[2] < v]:
             del held[key]
 
@@ -119,14 +125,53 @@
     lax.fori_loop(0, count, one, 0)
 
 
+def turn(dst, ref):
+    for h in range(2):
+        for b in range(2):
+            block = ref[128 * b : 128 * b + 128, 128 * h : 128 * h + 128]
+            dst[b, HALO + 128 * h : HALO + 128 * h + 128, :] = block.T
+
+
+def turn_edge(dst, above, below, edge):
+    for h in range(2):
+        cols = slice(128 * h, 128 * h + 128)
+        edge[0:HALO, :] = below[:, cols]
+        edge[128 - HALO : 128, :] = above[:, cols]
+        dst[2, HALO + 128 * h : HALO + 128 * h + 128, :] = edge[...].T
+
+
+def lay(dst, turned, line):
+    pad = jnp.zeros((128 - LIVE, 128), F32)
+    for j in range(3):
+        for b in range(3):
+            got = jnp.concatenate([turned[b, pl.ds(j, LIVE, stride=3), :], pad], axis=0).T
+            if b < 2:
+                line[HALO + 128 * b : HALO + 128 * b + 128, :] = got
+            else:
+                line[HALO + N : EXT, :] = got[0:HALO, :]
+                line[0:HALO, :] = got[128 - HALO : 128, :]
+        mix(dst.at[j], natural(line, V), V)
+
+
+def unlay(write, read, line, turned):
+    for j in range(3):
+        unmix(line, lambda v: read(j, v), V)
+        for b in range(2):
+            got = line[HALO + 128 * b : HALO + 128 * b + 128, :].T
+            turned[b, pl.ds(j, LIVE, stride=3), :] = got[0:LIVE, :]
+    for b in range(2):
+        for h in range(2):
+            write(b, h, turned[b, HALO + 128 * h : HALO + 128 * h + 128, :].T)
+
+
 def restrict(ref, f, pair):
-    fine = lax.broadcasted_iota(jnp.int32, (128, C), 0) // 2
+    lane = lax.broadcasted_iota(jnp.int32, (128, C), 0)
     coarse = lax.broadcasted_iota(jnp.int32, (128, C), 1)
     out = None
-    for j in range(2):
+    for j in range(3):
         for i in range(HV):
             pair[vec(i), :] = ref[f, j, vec(2 * i), :] + ref[f, j, vec(2 * i + 1), :]
-        pick = jnp.where(fine + 64 * j == coarse, 0.25, 0.0).astype(F32)
+        pick = jnp.where((3 * lane + j) // 2 - 8 == coarse, 0.25, 0.0).astype(F32)
         part = jnp.dot(pair[...], pick, precision=lax.Precision.HIGHEST, preferred_element_type=F32)
         out = part if out is None else out + part
     return out
@@ -174,56 +219,40 @@
     return low, high
 
 
-REST = HALO * (FIELDS - 8)
-
-
-def center_body(source, iterate, last, conduct, ext, low, high, src, middle, coef, wide, sems):
+def center_body(source, iterate, last, conduct, turned, low, high, src, middle, coef, sems):
     pairs = ((source, src), (iterate.at[3], middle), (conduct, coef))
     copies = [pltpu.make_async_copy(a, b, sems.at[i]) for i, (a, b) in enumerate(pairs)]
     for c in copies:
         c.start()
     for c in copies:
         c.wait()
-    refs = [src.at[f] for f in range(8)] + [middle, last, coef]
-    rows = 16
-
-    def chunk(i, carry):
-        base = pl.multiple_of(i * rows, 8)
-        pieces = [(ref[pl.ds(base, rows), :128], ref[pl.ds(base, rows), 128:]) for ref in refs]
-        lo, hi = pack_edges(pieces, rows)
-        for ref, got in ((low, lo), (high, hi)):
-            ref[pl.ds(base, rows), :] = got[0]
-            @pl.when(i < 8)
-            def _(ref=ref, got=got):
-                ref[pl.ds(N + base, rows), :] = got[1]
-
-            @pl.when(i >= 8)
-            def _(ref=ref, got=got):
-                at = pl.ds(N + base - 128, rows)
-                ref[at, :] = jnp.where(lanes(rows) < REST, ref[at, :], roll(got[1], REST))
-        return carry
-
-    lax.fori_loop(0, N // rows, chunk, 0)
-    zero = jnp.zeros((HALO, 128), F32)
-    wide[0:HALO, :] = zero
-    wide[HALO + N : EXT, :] = zero
-    for f, ref in enumerate(refs):
-        for j in range(2):
-            wide[HALO : HALO + N, :] = ref[:, 128 * j : 128 * j + 128]
-            mix(ext.at[f, j], natural(wide, V), V)
-
-
-def corners_body(above, below, low, high):
+    for f, ref in enumerate([src.at[f] for f in range(8)] + [middle, last, coef]):
+        turn(turned.at[f], ref)
+        for b in range(2):
+            at = slice(HALO * f, HALO * f + HALO)
+            low[b, at, :] = turned[f, b, HALO : 2 * HALO, :]
+            high[b, at, :] = turned[f, b, N : N + HALO, :]
+
+
+def rows_body(turned_in, above, below, turned, low, high, top, bottom, edge):
+    del turned_in
     place, ends = lax.axis_index("sx"), lax.axis_size("sx") - 1
+    up, down = flag(place > 0), flag(place < ends)
+    edge[...] = jnp.zeros((128, 128), F32)
     lane = lanes(HALO)
-    got = []
-    for ref, present in ((above, flag(place > 0)), (below, flag(place < ends))):
-        pieces = [(ref[f, :, :128] * present, ref[f, :, 128:] * present) for f in range(FIELDS)]
-        got.append(pack_edges(pieces, HALO))
-    for k, ref in ((0, low), (1, high)):
-        ref[0:HALO, :] = got[0][k][0]
-        ref[HALO : 2 * HALO, :] = got[1][k][0]
-        ref[2 * HALO : 3 * HALO, :] = jnp.where(lane < REST, got[0][k][1], roll(got[1][k][1], REST))
+    out = {}
+    for f in range(FIELDS):
+        top[...] = above[f] * up
+        bottom[...] = below[f] * down
+        turn_edge(turned.at[f], top, bottom, edge)
+        at = 2 * HALO * (f // 3)
+        for k, base in ((0, HALO), (1, N)):
+            x = roll(turned[f, 2, base : base + HALO, :], HALO + at)
+            old = out.get((k, f % 3), jnp.zeros((HALO, 128), F32))
+            out[k, f % 3] = jnp.where((lane >= at) & (lane < at + 2 * HALO), x, old)
+    for i in range(3):
+        low[HALO * i : HALO * i + HALO, :] = out[0, i]
+        high[HALO * i : HALO * i + HALO, :] = out[1, i]
 
 
 def side_column(before, after, f, rows, first, final):
@@ -233,9 +262,36 @@
     return jnp.where(lane >= 128 - HALO, roll(before, -HALO - at) * first, right)
 
 
-PART1 = 2 * EXT
+QUARTER = EXT // 4
+PART1 = 2 * EXT + QUARTER
 PART2 = PART1 + 4 * HALO
-MAIN = PART2 + EXT // 2
+MAIN = PART2 + 6 * HALO
+
+
+def squeeze(dest, ref):
+    lane = lanes(8)
+    for v in range(V):
+        third = ref[2, vec(v), :]
+        dest[8 * v : 8 * v + 8, :] = jnp.where(lane < LIVE, ref[0, vec(v), :], roll(third, 96))
+        dest[EXT + 8 * v : EXT + 8 * v + 8, :] = jnp.where(lane < LIVE, ref[1, vec(v), :], roll(third, 64))
+    for i in range(QUARTER // 8):
+        out = None
+        for g in range(4):
+            x = roll(ref[2, vec(i + g * QUARTER // 8), :], 32 * g - 64)
+            out = x if out is None else jnp.where(lane >= 32 * g, x, out)
+        dest[2 * EXT + 8 * i : 2 * EXT + 8 * i + 8, :] = out
+
+
+def unsqueeze(dest, src):
+    lane = lanes(8)
+    for v in range(V):
+        a, b = src[8 * v : 8 * v + 8, :], src[EXT + 8 * v : EXT + 8 * v + 8, :]
+        dest[0, vec(v), :] = jnp.where(lane < LIVE, a, 0.0)
+        dest[1, vec(v), :] = jnp.where(lane < LIVE, b, 0.0)
+        g, i = divmod(v, QUARTER // 8)
+        rest = roll(src[2 * EXT + 8 * i : 2 * EXT + 8 * i + 8, :], 64 - 32 * g)
+        third = jnp.where(lane < 32, roll(a, 32), jnp.where(lane < 64, roll(b, 64), rest))
+        dest[2, vec(v), :] = jnp.where(lane < LIVE, third, 0.0)
 
 
 def fold(dest, base, columns, width, groups, rows_in):
@@ -262,37 +318,29 @@
 
 
 def local_body(
-    ext_in, above, below, before, after, before_c, after_c,
-    ext, coefs, forced, own_new, main, up, down, low_c, high_c, coarse,
-    rhs, mid, scaled, wide, pair, rows_c,
+    turned_in, above, below, before, after, before_c, after_c,
+    turned, ext, coefs, forced, own_new, main, up, down, low_c, high_c, coarse,
+    rhs, mid, scaled, line, pair, rows_c,
 ):
-    del ext_in
+    del turned_in
     t, x, z = lax.axis_index("tm"), lax.axis_index("sx"), lax.axis_index("sy")
     not_end = flag(t < lax.axis_size("tm") - 1)
     x_first, x_final = flag(x > 0), flag(x < lax.axis_size("sx") - 1)
     z_first, z_final = flag(z > 0), flag(z < lax.axis_size("sy") - 1)
     inv, cof = coefs.at[0], coefs.at[1]
+    lane = lanes(HALO)
+    ends = (lane < HALO) | (lane >= 128 - HALO)
     for f in range(FIELDS):
-        for j in range(2):
-            cols = slice(128 * j, 128 * j + 128)
-            for h in range(2):
-                part = slice(8 * h, 8 * h + 8)
-                ext[f, j, pl.ds(64 * h, 8, stride=8), :] = above[f, part, cols] * x_first
-                ext[f, j, pl.ds(8 * (V - HALO) + 64 * h + 7, 8, stride=8), :] = below[f, part, cols] * x_final
-    for k, (own, corner) in enumerate(((before, before_c), (after, after_c))):
-        wide[k, 0, 0:HALO, :] = corner[0:HALO, :]
-        wide[k, 0, HALO : HALO + N, :] = own[0:N, :]
-        wide[k, 0, HALO + N : EXT, :] = corner[HALO : 2 * HALO, :]
-        rest = corner[2 * HALO : 3 * HALO, :]
-        wide[k, 1, 0:HALO, :] = rest
-        wide[k, 1, HALO : HALO + 128, :] = own[N : N + 128, :]
-        wide[k, 1, HALO + 128 : HALO + N, :] = roll(own[N : N + 128, :], -REST)
-        wide[k, 1, HALO + N : EXT, :] = roll(rest, -REST)
-    for v in range(V):
-        for g in range(2):
-            left, right = natural(wide.at[0, g], V)(v), natural(wide.at[1, g], V)(v)
-            for f in range(8 * g, min(8 * g + 8, FIELDS)):
-                ext[f, 2, vec(v), :] = side_column(left, right, f, 8, z_first, z_final)
+        for own, corner, base, present in ((before, before_c, 0, z_first), (after, after_c, HALO + N, z_final)):
+            for b in range(2):
+                turned[f, b, base : base + HALO, :] = own[b, HALO * f : HALO * f + HALO, :] * present
+            x = roll(corner[HALO * (f % 3) : HALO * (f % 3) + HALO, :], -HALO - 2 * HALO * (f // 3))
+            turned[f, 2, base : base + HALO, :] = jnp.where(ends, x * present, 0.0)
+
+    def lay_field(f):
+        lay(ext.at[f], turned.at[f], line)
+
+    repeat(FIELDS, lay_field)
     for v in range(V):
         for j in range(3):
             c = ext[COEF, j, vec(v), :]
@@ -316,25 +364,22 @@
             for j in range(3):
                 new, old = rhs[0, j, vec(v), :], ext[LAST, j, vec(v), :]
                 moved = not_end * (new - old)
-                if j < 2:
-                    own_new[j, vec(v), :] = new
-                    main[EXT * j + 8 * v : EXT * j + 8 * v + 8, :] = old + moved
-                else:
-                    scaled[0, j, vec(v), :] = old + moved
+                own_new[j, vec(v), :] = new
+                scaled[0, j, vec(v), :] = old + moved
                 rhs[0, j, vec(v), :] = moved
                 s = rhs[1, j, vec(v), :]
                 forced[j, vec(v), :] = s
                 rhs[1, j, vec(v), :] = s - ext[MID, j, vec(v), :]
+        squeeze(main, scaled.at[0])
         for j in range(2):
             cols = slice(128 * j, 128 * j + 128)
             at = PART1 + 2 * HALO * j
             main[at : at + HALO, :] = above[LAST, :, cols] * x_first
             main[at + HALO : at + 2 * HALO, :] = below[LAST, :, cols] * x_final
-        fold(
-            main, PART2,
-            [lambda r, n: scaled[0, 2, r : r + n, :], lambda r, n: ext[LAST, 2, r : r + n, :]],
-            HALO, 2, EXT,
-        )
+        for b in range(3):
+            at = PART2 + 2 * HALO * b
+            main[at : at + HALO, :] = turned[LAST, b, 0:HALO, :]
+            main[at + HALO : at + 2 * HALO, :] = turned[LAST, b, HALO + N : EXT, :]
 
     def free_step(k):
         step(rhs, mid, scaled, inv, cof, range(3), 3, V, keep)
@@ -414,24 +459,24 @@
         four[j] = rhs[1, j]
 
 
-def arrive_body(last, main, ext, coefs, forced, resid, new_start, new_mid, coarse_mid, rhs, mid, scaled, wide, pair):
+def arrive_body(
+    last, main, ext, coefs, forced, resid, new_start, new_mid, coarse_mid,
+    rhs, mid, scaled, turned, top, bottom, edge, line, pair,
+):
     inv, cof = coefs.at[0], coefs.at[1]
+    edge[...] = jnp.zeros((128, 128), F32)
     for j in range(2):
-        at = PART1 + 2 * HALO * j
-        wide[0:HALO, :] = main[at : at + HALO, :]
-        wide[HALO : HALO + N, :] = last[:, 128 * j : 128 * j + 128]
-        wide[HALO + N : EXT, :] = main[at + HALO : at + 2 * HALO, :]
-        mix(rhs.at[0, j], natural(wide, V), V)
-        new_start[j] = main[EXT * j : EXT * (j + 1), :]
-
-    def put_new(r, n, value):
-        new_start[2, r : r + n, :] = value
-
-    def put_old(r, n, value):
-        rhs[0, 2, r : r + n, :] = value
-
-    unfold(main, PART2, 0, 2, HALO, 2, EXT, put_new)
-    unfold(main, PART2, 1, 2, HALO, 2, EXT, put_old)
+        at, cols = PART1 + 2 * HALO * j, slice(128 * j, 128 * j + 128)
+        top[:, cols] = main[at : at + HALO, :]
+        bottom[:, cols] = main[at + HALO : at + 2 * HALO, :]
+    for b in range(3):
+        at = PART2 + 2 * HALO * b
+        turned[b, 0:HALO, :] = main[at : at + HALO, :]
+        turned[b, HALO + N : EXT, :] = main[at + HALO : at + 2 * HALO, :]
+    turn(turned, last)
+    turn_edge(turned, top, bottom, edge)
+    lay(rhs.at[0], turned, line)
+    unsqueeze(new_start, main)
     for j in range(3):
         rhs[1, j] = new_start[j] - rhs[0, j]
     repeat(FACTOR, lambda k: step(rhs, mid, scaled, inv, cof, range(2), 3, V, keep))
@@ -442,15 +487,17 @@
             rhs[0, j, vec(v), :] = u - ext[MID, j, vec(v), :]
     repeat(FACTOR, lambda k: step(rhs, mid, scaled, inv, cof, range(1), 3, V, keep))
     for k in range(2):
-        for j in range(2):
-            unmix(wide, lambda v: rhs[1 - k, j, vec(v), :], V)
-            resid[k, :, 128 * j : 128 * j + 128] = wide[HALO : HALO + N, :]
+
+        def put(b, h, block, k=k):
+            resid[k, 128 * b : 128 * b + 128, 128 * h : 128 * h + 128] = block
+
+        unlay(put, lambda j, v, k=k: rhs[1 - k, j, vec(v), :], line, turned)
     coarse_mid[...] = restrict(rhs, 0, pair)
 
 
 def final_body(
     one, two, three, four, ccoefs, coarse_mid, ext, coefs, new_start, new_mid, own_new,
-    out, err, cmid, cscaled, sent, fix, rhs, mid, scaled, wide, pair, rows_c,
+    out, err, cmid, cscaled, sent, fix, rhs, mid, scaled, turned, line, pair, rows_c,
 ):
     t = lax.axis_index("tm")
     m1, m2, m3 = flag(t > 0), flag(t > 1), flag(t > 2)
@@ -476,12 +523,12 @@
             unmix(rows_c, lambda v: err[0, c, vec(v), :], CV)
             mix(pair, natural(rows_c, HV, 8), HV)
             value = pair[...] if extra is None else pair[...] + extra[...]
-            for j in (0, 1) if c == 0 else (2,):
-                if c == 0:
-                    pick = src == dst // 2 + 64 * j
-                else:
-                    pick = ((dst < HALO) & (src == dst // 2)) | ((dst >= 128 - HALO) & (src == 64 + dst // 2))
-                fix[k, j] = jnp.dot(value, flag(pick), precision=lax.Precision.HIGHEST, preferred_element_type=F32)
+            for j in range(3):
+                cell = (3 * dst + j) // 2 - 8
+                if c == 1:
+                    cell = jnp.where(cell < 0, cell + C, jnp.where((cell >= C) & (dst < LIVE), cell - C, -1))
+                got = jnp.dot(value, flag(src == cell), precision=lax.Precision.HIGHEST, preferred_element_type=F32)
+                fix[k, j] = got if c == 0 else fix[k, j] + got
 
     spread(0)
     step(err, cmid, cscaled, inv, cof, range(1), 2, CV, keep)
@@ -497,14 +544,15 @@
             u = new_mid[j, vec(v), :] + fix[1, j, vec(v // 2), :]
             scaled[0, j, vec(v), :] = u
             rhs[1, j, vec(v), :] = u + ext[4, j, vec(v), :]
-            if j < 2:
-                scaled[1, j, vec(v), :] = own_new[j, vec(v), :] + fix[2, j, vec(v // 2), :]
+            scaled[1, j, vec(v), :] = own_new[j, vec(v), :] + fix[2, j, vec(v // 2), :]
 
     def give(at):
         for f in range(2):
-            for j in range(2):
-                unmix(wide, lambda v: scaled[f, j, vec(v), :], V)
-                out[4 * f + at, :, 128 * j : 128 * j + 128] = wide[HALO : HALO + N, :]
+
+            def put(b, h, block, f=f):
+                out[4 * f + at, 128 * b : 128 * b + 128, 128 * h : 128 * h + 128] = block
+
+            unlay(put, lambda j, v, f=f: scaled[f, j, vec(v), :], line, turned)
 
     give(FACTOR - 1)
 
@@ -530,30 +578,34 @@
 
 def shards(iterate, source, start_field, conduct):
     up, down, last = call(
-        strips_body, [(FIELDS, HALO, N)] * 2 + [(N, N)], [HB] * 4, [pltpu.SemaphoreType.DMA((7,))], name="strips"
+        strips_body, [(FIELDS, HALO, N)] * 2 + [(N, N)], [HB] * 4, [pltpu.SemaphoreType.DMA((7,))], name="strips",
+        limit=63_000_000,
     )(source, iterate, start_field, conduct)
     above, below = ring(down, "sx", 1), ring(up, "sx", -1)
     last_in = ring(last, "tm", 1)
-    ext, low, high = call(
+    turned, low, high = call(
         center_body,
-        [(FIELDS, 3, EXT, 128), (N + 128, 128), (N + 128, 128)],
+        [(FIELDS, 3, EXT, 128), (2, HALO * FIELDS, 128), (2, HALO * FIELDS, 128)],
         [HB, HB, VM, HB],
-        [vmem(8, N, N), vmem(N, N), vmem(N, N), vmem(EXT, 128), pltpu.SemaphoreType.DMA((3,))],
+        [vmem(8, N, N), vmem(N, N), vmem(N, N), pltpu.SemaphoreType.DMA((3,))],
         name="center", flops=20_000_000,
     )(source, iterate, last, conduct)
     before, after = ring(high, "sy", 1), ring(low, "sy", -1)
-    c_lo, c_hi = call(corners_body, [(3 * HALO, 128)] * 2, 2, name="corners")(above, below)
+    turned, c_lo, c_hi = call(
+        rows_body, [(FIELDS, 3, EXT, 128), (3 * HALO, 128), (3 * HALO, 128)], 3,
+        [vmem(HALO, N), vmem(HALO, N), vmem(128, 128)], {0: 0}, "rows",
+    )(turned, above, below)
     before_c, after_c = ring(c_hi, "sy", 1), ring(c_lo, "sy", -1)
     before, after, before_c, after_c, last_in = lax.optimization_barrier((before, after, before_c, after_c, last_in))
-    ext, coefs, forced, own_new, main, c_up, c_down, c_low, c_high, coarse = call(
+    _, ext, coefs, forced, own_new, main, c_up, c_down, c_low, c_high, coarse = call(
         local_body,
         [
-            (FIELDS, 3, EXT, 128), (2, 3, EXT, 128), (3, EXT, 128), (2, EXT, 128), (MAIN, 128),
+            (FIELDS, 3, EXT, 128), (FIELDS, 3, EXT, 128), (2, 3, EXT, 128), (3, EXT, 128), (3, EXT, 128), (MAIN, 128),
             (4, HALO, 128), (4, HALO, 128), (C, 128), (C, 128), (4, C, 128),
         ],
-        7, [vmem(3, 3, EXT, 128)] * 3 + [vmem(2, 2, EXT, 128), vmem(HALF, 128), vmem(HALF, 128)],
+        7, [vmem(3, 3, EXT, 128)] * 3 + [vmem(EXT, 128), vmem(HALF, 128), vmem(HALF, 128)],
         {0: 0}, "local", 50_000_000,
-    )(ext, above, below, before, after, before_c, after_c)
+    )(turned, above, below, before, after, before_c, after_c)
     c_above, c_below = ring(c_down, "sx", 1), ring(c_up, "sx", -1)
     main_in = ring(main, "tm", 1)
     c_lo, c_hi = call(coarse_edges_body, [(CEXT, 128)] * 2, 4, name="coarse_edges")(c_above, c_below, c_low, c_high)
@@ -569,14 +621,17 @@
     resid, new_start, new_mid, coarse_mid = call(
         arrive_body,
         [(2, N, N), (3, EXT, 128), (3, EXT, 128), (HALF, 128)],
-        5, [vmem(2, 3, EXT, 128)] * 3 + [vmem(EXT, 128), vmem(HALF, 128)], name="arrive", flops=30_000_000,
+        5,
+        [vmem(2, 3, EXT, 128)] * 3
+        + [vmem(3, EXT, 128), vmem(HALO, N), vmem(HALO, N), vmem(128, 128), vmem(EXT, 128), vmem(HALF, 128)],
+        name="arrive", flops=30_000_000,
     )(last_in, main_in, ext, coefs, forced)
     (updated,) = call(
         final_body,
         [(8, N, N)],
         11,
         [vmem(1, 2, CEXT, 128)] * 3 + [vmem(4, CEXT, 128), vmem(3, 3, HALF, 128)] + [vmem(2, 3, EXT, 128)] * 3
-        + [vmem(EXT, 128), vmem(HALF, 128), vmem(CEXT, 128)],
+        + [vmem(2, EXT, 128), vmem(EXT, 128), vmem(HALF, 128), vmem(CEXT, 128)],
         name="final",
     )(one, two, three, four, ccoefs, coarse_mid, ext, coefs, new_start, new_mid, own_new)
     return updated, resid

time: 72.4 us -> 65.1 us (0.90)
  Pallas kernels: 33.3 us -> 28.4 us
  local copies, waits for them, and re-layouts: 5.08 us -> 2.55 us
    pallas_call x3, Pallas kernels: 17.2 us -> 12.4 us  [the longest x1 10.9 us: shards(): call(local_body, [(FIELDS, 3, EXT, 128), (FIELDS, 3, EXT, 128), (2, 3, EX...]
    unnamed x10 -> x8, local copies, waits for them, and re-layouts: 5.08 us -> 2.55 us
    pallas_call x1, Pallas kernels: 7.5 us -> 5.18 us  [shards(): call(arrive_body, [(2, N, N), (3, EXT, 128), (3, EXT, 128), (HALF, 128)],...]
    pallas_call x1, Pallas kernels: 0.23 us -> 2.19 us  [shards(): call(strips_body, [(FIELDS, HALO, N)] * 2 + [(N, N)], [HB] * 4, [pltpu.Se...]
  transfers between devices with their start and end apart: 15 -> 15, of which waited for: 6 -> 6; matrix products, arithmetic and copies ran while one was open for 0% -> 0% of each run, Pallas kernels for 19% -> 14%
where the time goes in v3:
time: 65.1 us; the launch traced here: 65 us
  Pallas kernels  28.4 us (44%)
  starting transfers between devices  22.2 us (34%)
  waiting for transfers between devices  11.1 us (17%)
  local copies, waits for them, and re-layouts  2.55 us (4%)
  between operations  0.71 us (1%)
    ppermute x15, starting transfers between devices, ring(): return lax.ppermute(x, axis, [(i, (i + by) % count) for i in range(count)])  22.2 us
    ppermute x15, waiting for transfers between devices, ring(): return lax.ppermute(x, axis, [(i, (i + by) % count) for i in range(count)])  11.1 us
    pallas_call x1, Pallas kernels, shards(): call(local_body, [(FIELDS, 3, EXT, 128), (FIELDS, 3, EXT, 128), (2, 3, EX...  10.9 us
    pallas_call x1, Pallas kernels, shards(): call(final_body, [(8, N, N)], 11, [vmem(1, 2, CEXT, 128)] * 3 + [vmem(4,...  6.37 us
    pallas_call x1, Pallas kernels, shards(): call(arrive_body, [(2, N, N), (3, EXT, 128), (3, EXT, 128), (HALF, 128)],...  5.18 us
    unnamed x8, local copies, waits for them, and re-layouts  2.55 us
    pallas_call x1, Pallas kernels, shards(): call(strips_body, [(FIELDS, HALO, N)] * 2 + [(N, N)], [HB] * 4, [pltpu.Se...  2.19 us
    pallas_call x1, Pallas kernels, shards(): call(coarse_body, [(ONE, 128), (TWO, 128), (TWO, 128), (2, CEXT, 128), (2...  2.16 us
  transfers between devices with their start and end apart: 15, of which 6 were waited for; matrix products, arithmetic and copies ran while one was open for 0% of the time, Pallas kernels for 14%

profile of v3, /device:TPU:64, one launch (start us, length us, event | category | flops | bytes accessed | tf_op | source)
XLA Modules:
  0.0 65.0 jit_solution(7574297687611831213)
XLA Ops:
  0.6 0.0 copy-start.2
  0.6 0.0 copy-start
  0.7 2.2 %strips.1 = (f32[11,16,256]{2,1,0:T(8,128)}, f32[11,16,256]{2,1,0:T(8,128)}, f32[256,256]{1,0:T(8,128)}) custom-call(f32[8,256,256]{2,1,0:T(8,128)} %source.3, f32[8,256,256]{2,1,0:T(8,128)} %iterate.3, f32[256,256]{1,0:T(8,128)} %start.1, f32[256,256]{1,0:T(8,128)} %conduct.3), custom_call_target="tpu_custom_call" | custom-call | bytes 1000 | tf_op jit(solution)/shard_map/strips/pallas_call | solution.py:580
  2.8 1.7 %collective-permute-start.6 = (f32[256,256]{1,0:T(8,128)}, f32[256,256]{1,0:T(8,128)S(1)}, u32[]{:S(2)}, u32[]{:S(2)}) collective-permute-start(f32[256,256]{1,0:T(8,128)} %get-tuple-element.37.last), channel_id=1, source_target_pairs={{0,64},{64,128},{128,192},{192,0},{1,65},{65,129},{129,193},{193,1... | collective-permute-start | bytes 786440 | tf_op jit(solution)/shard_map/ppermute | solution.py:572
  4.5 0.0 collective-permute-start
  4.5 3.0 %collective-permute-start.1 = (f32[11,16,256]{2,1,0:T(8,128)}, f32[11,16,256]{2,1,0:T(8,128)S(1)}, u32[]{:S(2)}, u32[]{:S(2)}) collective-permute-start(f32[11,16,256]{2,1,0:T(8,128)} %get-tuple-element.40), channel_id=1, source_target_pairs={{0,56},{8,0},{16,8},{24,16},{32,24},{40,32},{48,40},{56,48},{1,57}... | collective-permute-start | bytes 540680 | tf_op jit(solution)/shard_map/ppermute | solution.py:572
  7.5 0.0 copy-done.2
  7.5 0.0 copy-done
  7.5 0.0 copy-start.1
  7.5 1.6 %copy-done.1 = f32[8,256,256]{2,1,0:T(8,128)S(1)} copy-done((f32[8,256,256]{2,1,0:T(8,128)S(1)}, f32[8,256,256]{2,1,0:T(8,128)}, u32[]{:S(2)}) %copy-start.1) | copy-done | bytes 2097176
  9.1 0.0 copy-start.3
  9.1 0.9 %copy-done.3 = f32[256,256]{1,0:T(8,128)S(1)} copy-done((f32[256,256]{1,0:T(8,128)S(1)}, f32[256,256]{1,0:T(8,128)}, u32[]{:S(2)}) %copy-start.3) | copy-done | bytes 262168
  10.0 1.0 %center.1 = (f32[11,3,288,128]{3,2,1,0:T(8,128)S(1)}, f32[2,176,128]{2,1,0:T(8,128)S(1)}, f32[2,176,128]{2,1,0:T(8,128)S(1)}) custom-call(f32[8,256,256]{2,1,0:T(8,128)S(1)} %copy-done, f32[8,256,256]{2,1,0:T(8,128)S(1)} %copy-done.1, f32[256,256]{1,0:T(8,128)S(1)} %copy-done.3, f32[256,256]{1,0:T(8,128)S(1)} %copy-done.2), custom_call_target="tpu_custom_call" | custom-call | flops 20000000 | bytes 1000 | tf_op jit(solution)/shard_map/center/pallas_call | solution.py:586
  11.0 2.0 %collective-permute-start.2 = (f32[2,176,128]{2,1,0:T(8,128)S(1)}, f32[2,176,128]{2,1,0:T(8,128)S(1)}, u32[]{:S(2)}, u32[]{:S(2)}) collective-permute-start(f32[2,176,128]{2,1,0:T(8,128)S(1)} %get-tuple-element.42), channel_id=1, source_target_pairs={{0,1},{1,2},{2,3},{3,4},{4,5},{5,6},{6,7},{7,0},{8,9},{9,10},{10,1... | collective-permute-start | bytes 540680 | tf_op jit(solution)/shard_map/ppermute | solution.py:572
  13.0 0.1 collective-permute-start.3
  13.1 0.0 collective-permute-done.above
  13.1 0.0 collective-permute-done.1.below
  13.1 0.5 rows.1
  13.7 3.1 %collective-permute-start.4 = (f32[48,128]{1,0:T(8,128)S(1)}, f32[48,128]{1,0:T(8,128)S(1)}, u32[]{:S(2)}, u32[]{:S(2)}) collective-permute-start(f32[48,128]{1,0:T(8,128)S(1)} %get-tuple-element.44), channel_id=1, source_target_pairs={{0,1},{1,2},{2,3},{3,4},{4,5},{5,6},{6,7},{7,0},{8,9},{9,10},{10,1... | collective-permute-start | bytes 73736 | tf_op jit(solution)/shard_map/ppermute | solution.py:572
  16.8 0.0 collective-permute-start.5
  16.8 0.1 collective-permute-done.2.before
  16.9 3.0 %collective-permute-done.3.after = f32[2,176,128]{2,1,0:T(8,128)S(1)} collective-permute-done((f32[2,176,128]{2,1,0:T(8,128)S(1)}, f32[2,176,128]{2,1,0:T(8,128)S(1)}, u32[]{:S(2)}, u32[]{:S(2)}) %collective-permute-start.3) | collective-permute-done | bytes 180256 | tf_op jit(solution)/shard_map/ppermute | solution.py:572
  19.9 0.0 collective-permute-done.4.before_c
  19.9 1.9 %collective-permute-done.5.after_c = f32[48,128]{1,0:T(8,128)S(1)} collective-permute-done((f32[48,128]{1,0:T(8,128)S(1)}, f32[48,128]{1,0:T(8,128)S(1)}, u32[]{:S(2)}, u32[]{:S(2)}) %collective-permute-start.5) | collective-permute-done | bytes 24608 | tf_op jit(solution)/shard_map/ppermute | solution.py:572
  21.8 0.0 collective-permute-done.6.last
  21.8 10.9 %local.1 = (f32[11,3,288,128]{3,2,1,0:T(8,128)S(1)}, f32[11,3,288,128]{3,2,1,0:T(8,128)S(1)}, f32[2,3,288,128]{3,2,1,0:T(8,128)S(1)}, f32[3,288,128]{2,1,0:T(8,1...) custom-call(f32[11,3,288,128]{3,2,1,0:T(8,128)S(1)} %get-tuple-eleme, ...), custom_call_target="tpu_custom_call", output_to_operand_aliasing={{0}: (0, {})} | custom-call | flops 50000000 | bytes 1000 | tf_op jit(solution)/shard_map/local/pallas_call | solution.py:600
  32.7 1.7 %collective-permute-start.14 = (f32[808,128]{1,0:T(8,128)S(1)}, f32[808,128]{1,0:T(8,128)S(1)}, u32[]{:S(2)}, u32[]{:S(2)}) collective-permute-start(f32[808,128]{1,0:T(8,128)S(1)} %get-tuple-element.63), channel_id=1, source_target_pairs={{0,64},{64,128},{128,192},{192,0},{1,65},{65,129},{129,193},{193,1... | collective-permute-start | bytes 1241096 | tf_op jit(solution)/shard_map/ppermute | solution.py:572
  34.4 0.0 collective-permute-start.7
  34.4 3.0 %collective-permute-start.8 = (f32[4,16,128]{2,1,0:T(8,128)S(1)}, f32[4,16,128]{2,1,0:T(8,128)S(1)}, u32[]{:S(2)}, u32[]{:S(2)}) collective-permute-start(f32[4,16,128]{2,1,0:T(8,128)S(1)} %get-tuple-element.52), channel_id=1, source_target_pairs={{0,56},{8,0},{16,8},{24,16},{32,24},{40,32},{48,40},{56,48},{1,57}... | collective-permute-start | bytes 98312 | tf_op jit(solution)/shard_map/ppermute | solution.py:572
  37.3 1.6 %collective-permute-done.7.above = f32[4,16,128]{2,1,0:T(8,128)S(1)} collective-permute-done((f32[4,16,128]{2,1,0:T(8,128)S(1)}, f32[4,16,128]{2,1,0:T(8,128)S(1)}, u32[]{:S(2)}, u32[]{:S(2)}) %collective-permute-start.7) | collective-permute-done | bytes 32800 | tf_op jit(solution)/shard_map/ppermute | solution.py:572
  38.9 0.0 collective-permute-done.8.below
  38.9 0.1 coarse_edges.1
  39.0 3.3 %collective-permute-start.9 = (f32[160,128]{1,0:T(8,128)S(1)}, f32[160,128]{1,0:T(8,128)S(1)}, u32[]{:S(2)}, u32[]{:S(2)}) collective-permute-start(f32[160,128]{1,0:T(8,128)S(1)} %get-tuple-element.55), channel_id=1, source_target_pairs={{0,1},{1,2},{2,3},{3,4},{4,5},{5,6},{6,7},{7,0},{8,9},{9,10},{10,1... | collective-permute-start | bytes 245768 | tf_op jit(solution)/shard_map/ppermute | solution.py:572
  42.4 0.0 collective-permute-start.10
  42.4 2.1 %collective-permute-done.9.before = f32[160,128]{1,0:T(8,128)S(1)} collective-permute-done((f32[160,128]{1,0:T(8,128)S(1)}, f32[160,128]{1,0:T(8,128)S(1)}, u32[]{:S(2)}, u32[]{:S(2)}) %collective-permute-start.9) | collective-permute-done | bytes 81952 | tf_op jit(solution)/shard_map/ppermute | solution.py:572
  44.4 2.4 %collective-permute-done.10.after = f32[160,128]{1,0:T(8,128)S(1)} collective-permute-done((f32[160,128]{1,0:T(8,128)S(1)}, f32[160,128]{1,0:T(8,128)S(1)}, u32[]{:S(2)}, u32[]{:S(2)}) %collective-permute-start.10) | collective-permute-done | bytes 81952 | tf_op jit(solution)/shard_map/ppermute | solution.py:572
  46.8 2.2 %coarse.1 = (f32[360,128]{1,0:T(8,128)S(1)}, f32[192,128]{1,0:T(8,128)S(1)}, f32[192,128]{1,0:T(8,128)S(1)}, f32[2,160,128]{2,1,0:T(8,128)S(1)}, f32[2,2,160,128]{3,2,1,0:T(8,128)S(1)}) custom-call(f32[4,128,128]{2,1,0:T(8,128)S(1)} %get-tuple-element.50.coarse, f32[4,16,128]{2,1,0:T(8,128)S(1)} %collective-permute-done.7.above, ...), custom_call_target="tpu_custom_call" | custom-call | bytes 1000 | tf_op jit(solution)/shard_map/coarse/pallas_call | solution.py:613
  49.0 1.5 %collective-permute-start.11 = (f32[360,128]{1,0:T(8,128)S(1)}, f32[360,128]{1,0:T(8,128)S(1)}, u32[]{:S(2)}, u32[]{:S(2)}) collective-permute-start(f32[360,128]{1,0:T(8,128)S(1)} %get-tuple-element.57), channel_id=1, source_target_pairs={{0,64},{64,128},{128,192},{192,0},{1,65},{65,129},{129,193},{193,1... | collective-permute-start | bytes 552968 | tf_op jit(solution)/shard_map/ppermute | solution.py:572
  50.5 1.8 %collective-permute-start.12 = (f32[192,128]{1,0:T(8,128)S(1)}, f32[192,128]{1,0:T(8,128)S(1)}, u32[]{:S(2)}, u32[]{:S(2)}) collective-permute-start(f32[192,128]{1,0:T(8,128)S(1)} %get-tuple-element.58), channel_id=1, source_target_pairs={{0,128},{64,192},{128,0},{192,64},{1,129},{65,193},{129,1},{193,65... | collective-permute-start | bytes 294920 | tf_op jit(solution)/shard_map/ppermute | solution.py:572
  52.3 1.1 %collective-permute-start.13 = (f32[192,128]{1,0:T(8,128)S(1)}, f32[192,128]{1,0:T(8,128)S(1)}, u32[]{:S(2)}, u32[]{:S(2)}) collective-permute-start(f32[192,128]{1,0:T(8,128)S(1)} %get-tuple-element.59), channel_id=1, source_target_pairs={{0,192},{64,0},{128,64},{192,128},{1,193},{65,1},{129,65},{193,129... | collective-permute-start | bytes 294920 | tf_op jit(solution)/shard_map/ppermute | solution.py:572
  53.4 0.0 collective-permute-done.14.main
  53.4 5.2 %arrive.1 = (f32[2,256,256]{2,1,0:T(8,128)}, f32[3,288,128]{2,1,0:T(8,128)S(1)}, f32[3,288,128]{2,1,0:T(8,128)S(1)}, f32[144,128]{1,0:T(8,128)S(1)}) custom-call(f32[256,256]{1,0:T(8,128)S(1)} %collective-permute-done.6.last, f32[808,128]{1,0:T(8,128)S(1)} %collective-permute-done.14.main, f32[11,3,288,128]{3,2,1,0:T(8,128)S(1)} %get-tuple-element.64.ext, ...), custom_call_target="tpu_custom_call" | custom-call | flops 30000000 | bytes 1000 | tf_op jit(solution)/shard_map/arrive/pallas_call | solution.py:621
  58.6 0.0 collective-permute-done.12.two
  58.6 0.0 collective-permute-done.13.three
  58.6 0.0 collective-permute-done.11.one
  58.6 6.4 %final.1 = f32[8,256,256]{2,1,0:T(8,128)} custom-call(f32[360,128]{1,0:T(8,128)S(1)} %collective-permute-done.11.one, f32[192,128]{1,0:T(8,128)S(1)} %collective-permute-done.12.two, f32[192,128]{1,0:T(8,128)S(1)} %collective-permute-done.13.three, f32[2,160,128]{2,1,0:T(8,128)S(1)} %get-tuple-element.60.four, ...), custom_call_target="tpu_custom_call" | custom-call | bytes 1000 | tf_op jit(solution)/shard_map/final/pallas_call | solution.py:629
Async XLA Ops:
  0.6 6.8 %copy-start.2 = (f32[256,256]{1,0:T(8,128)S(1)}, f32[256,256]{1,0:T(8,128)}, u32[]{:S(2)}) copy-start(f32[256,256]{1,0:T(8,128)} %conduct.3) | copy-start | bytes 786436
  0.6 6.8 %copy-start = (f32[8,256,256]{2,1,0:T(8,128)S(1)}, f32[8,256,256]{2,1,0:T(8,128)}, u32[]{:S(2)}) copy-start(f32[8,256,256]{2,1,0:T(8,128)} %source.3) | copy-start | bytes 6291460
  2.8 19.0 %collective-permute-start.6 = (f32[256,256]{1,0:T(8,128)}, f32[256,256]{1,0:T(8,128)S(1)}, u32[]{:S(2)}, u32[]{:S(2)}) collective-permute-start(f32[256,256]{1,0:T(8,128)} %get-tuple-element.37.last), channel_id=1, source_target_pairs={{0,64},{64,128},{128,192},{192,0},{1,65},{65,129},{129,193},{193,1... | collective-permute-start | bytes 786440 | tf_op jit(solution)/shard_map/ppermute | solution.py:572
  4.5 8.6 %collective-permute-start = (f32[11,16,256]{2,1,0:T(8,128)}, f32[11,16,256]{2,1,0:T(8,128)S(1)}, u32[]{:S(2)}, u32[]{:S(2)}) collective-permute-start(f32[11,16,256]{2,1,0:T(8,128)} %get-tuple-element.39), channel_id=1, source_target_pairs={{0,8},{8,16},{16,24},{24,32},{32,40},{40,48},{48,56},{56,0},{1,9},... | collective-permute-start | bytes 540680 | tf_op jit(solution)/shard_map/ppermute | solution.py:572
  4.5 8.6 %collective-permute-start.1 = (f32[11,16,256]{2,1,0:T(8,128)}, f32[11,16,256]{2,1,0:T(8,128)S(1)}, u32[]{:S(2)}, u32[]{:S(2)}) collective-permute-start(f32[11,16,256]{2,1,0:T(8,128)} %get-tuple-element.40), channel_id=1, source_target_pairs={{0,56},{8,0},{16,8},{24,16},{32,24},{40,32},{48,40},{56,48},{1,57}... | collective-permute-start | bytes 540680 | tf_op jit(solution)/shard_map/ppermute | solution.py:572
  7.5 1.6 %copy-start.1 = (f32[8,256,256]{2,1,0:T(8,128)S(1)}, f32[8,256,256]{2,1,0:T(8,128)}, u32[]{:S(2)}) copy-start(f32[8,256,256]{2,1,0:T(8,128)} %iterate.3) | copy-start | bytes 6291460
  9.1 0.9 %copy-start.3 = (f32[256,256]{1,0:T(8,128)S(1)}, f32[256,256]{1,0:T(8,128)}, u32[]{:S(2)}) copy-start(f32[256,256]{1,0:T(8,128)} %get-tuple-element.37.last) | copy-start | bytes 786436
  11.0 5.8 %collective-permute-start.2 = (f32[2,176,128]{2,1,0:T(8,128)S(1)}, f32[2,176,128]{2,1,0:T(8,128)S(1)}, u32[]{:S(2)}, u32[]{:S(2)}) collective-permute-start(f32[2,176,128]{2,1,0:T(8,128)S(1)} %get-tuple-element.42), channel_id=1, source_target_pairs={{0,1},{1,2},{2,3},{3,4},{4,5},{5,6},{6,7},{7,0},{8,9},{9,10},{10,1... | collective-permute-start | bytes 540680 | tf_op jit(solution)/shard_map/ppermute | solution.py:572
  13.0 6.9 %collective-permute-start.3 = (f32[2,176,128]{2,1,0:T(8,128)S(1)}, f32[2,176,128]{2,1,0:T(8,128)S(1)}, u32[]{:S(2)}, u32[]{:S(2)}) collective-permute-start(f32[2,176,128]{2,1,0:T(8,128)S(1)} %get-tuple-element.43), channel_id=1, source_target_pairs={{0,7},{1,0},{2,1},{3,2},{4,3},{5,4},{6,5},{7,6},{8,15},{9,8},{10,9... | collective-permute-start | bytes 540680 | tf_op jit(solution)/shard_map/ppermute | solution.py:572
  13.7 6.2 %collective-permute-start.4 = (f32[48,128]{1,0:T(8,128)S(1)}, f32[48,128]{1,0:T(8,128)S(1)}, u32[]{:S(2)}, u32[]{:S(2)}) collective-permute-start(f32[48,128]{1,0:T(8,128)S(1)} %get-tuple-element.44), channel_id=1, source_target_pairs={{0,1},{1,2},{2,3},{3,4},{4,5},{5,6},{6,7},{7,0},{8,9},{9,10},{10,1... | collective-permute-start | bytes 73736 | tf_op jit(solution)/shard_map/ppermute | solution.py:572
  16.8 5.0 %collective-permute-start.5 = (f32[48,128]{1,0:T(8,128)S(1)}, f32[48,128]{1,0:T(8,128)S(1)}, u32[]{:S(2)}, u32[]{:S(2)}) collective-permute-start(f32[48,128]{1,0:T(8,128)S(1)} %get-tuple-element.45), channel_id=1, source_target_pairs={{0,7},{1,0},{2,1},{3,2},{4,3},{5,4},{6,5},{7,6},{8,15},{9,8},{10,9... | collective-permute-start | bytes 73736 | tf_op jit(solution)/shard_map/ppermute | solution.py:572
  32.7 20.7 %collective-permute-start.14 = (f32[808,128]{1,0:T(8,128)S(1)}, f32[808,128]{1,0:T(8,128)S(1)}, u32[]{:S(2)}, u32[]{:S(2)}) collective-permute-start(f32[808,128]{1,0:T(8,128)S(1)} %get-tuple-element.63), channel_id=1, source_target_pairs={{0,64},{64,128},{128,192},{192,0},{1,65},{65,129},{129,193},{193,1... | collective-permute-start | bytes 1241096 | tf_op jit(solution)/shard_map/ppermute | solution.py:572
  34.4 4.6 %collective-permute-start.7 = (f32[4,16,128]{2,1,0:T(8,128)S(1)}, f32[4,16,128]{2,1,0:T(8,128)S(1)}, u32[]{:S(2)}, u32[]{:S(2)}) collective-permute-start(f32[4,16,128]{2,1,0:T(8,128)S(1)} %get-tuple-element.51), channel_id=1, source_target_pairs={{0,8},{8,16},{16,24},{24,32},{32,40},{40,48},{48,56},{56,0},{1,9},... | collective-permute-start | bytes 98312 | tf_op jit(solution)/shard_map/ppermute | solution.py:572
  34.4 4.6 %collective-permute-start.8 = (f32[4,16,128]{2,1,0:T(8,128)S(1)}, f32[4,16,128]{2,1,0:T(8,128)S(1)}, u32[]{:S(2)}, u32[]{:S(2)}) collective-permute-start(f32[4,16,128]{2,1,0:T(8,128)S(1)} %get-tuple-element.52), channel_id=1, source_target_pairs={{0,56},{8,0},{16,8},{24,16},{32,24},{40,32},{48,40},{56,48},{1,57}... | collective-permute-start | bytes 98312 | tf_op jit(solution)/shard_map/ppermute | solution.py:572
  39.0 5.4 %collective-permute-start.9 = (f32[160,128]{1,0:T(8,128)S(1)}, f32[160,128]{1,0:T(8,128)S(1)}, u32[]{:S(2)}, u32[]{:S(2)}) collective-permute-start(f32[160,128]{1,0:T(8,128)S(1)} %get-tuple-element.55), channel_id=1, source_target_pairs={{0,1},{1,2},{2,3},{3,4},{4,5},{5,6},{6,7},{7,0},{8,9},{9,10},{10,1... | collective-permute-start | bytes 245768 | tf_op jit(solution)/shard_map/ppermute | solution.py:572
  42.4 4.4 %collective-permute-start.10 = (f32[160,128]{1,0:T(8,128)S(1)}, f32[160,128]{1,0:T(8,128)S(1)}, u32[]{:S(2)}, u32[]{:S(2)}) collective-permute-start(f32[160,128]{1,0:T(8,128)S(1)} %get-tuple-element.56), channel_id=1, source_target_pairs={{0,7},{1,0},{2,1},{3,2},{4,3},{5,4},{6,5},{7,6},{8,15},{9,8},{10,9... | collective-permute-start | bytes 245768 | tf_op jit(solution)/shard_map/ppermute | solution.py:572
  49.0 9.6 %collective-permute-start.11 = (f32[360,128]{1,0:T(8,128)S(1)}, f32[360,128]{1,0:T(8,128)S(1)}, u32[]{:S(2)}, u32[]{:S(2)}) collective-permute-start(f32[360,128]{1,0:T(8,128)S(1)} %get-tuple-element.57), channel_id=1, source_target_pairs={{0,64},{64,128},{128,192},{192,0},{1,65},{65,129},{129,193},{193,1... | collective-permute-start | bytes 552968 | tf_op jit(solution)/shard_map/ppermute | solution.py:572
  50.5 8.1 %collective-permute-start.12 = (f32[192,128]{1,0:T(8,128)S(1)}, f32[192,128]{1,0:T(8,128)S(1)}, u32[]{:S(2)}, u32[]{:S(2)}) collective-permute-start(f32[192,128]{1,0:T(8,128)S(1)} %get-tuple-element.58), channel_id=1, source_target_pairs={{0,128},{64,192},{128,0},{192,64},{1,129},{65,193},{129,1},{193,65... | collective-permute-start | bytes 294920 | tf_op jit(solution)/shard_map/ppermute | solution.py:572
  52.3 6.2 %collective-permute-start.13 = (f32[192,128]{1,0:T(8,128)S(1)}, f32[192,128]{1,0:T(8,128)S(1)}, u32[]{:S(2)}, u32[]{:S(2)}) collective-permute-start(f32[192,128]{1,0:T(8,128)S(1)} %get-tuple-element.59), channel_id=1, source_target_pairs={{0,192},{64,0},{128,64},{192,128},{1,193},{65,1},{129,65},{193,129... | collective-permute-start | bytes 294920 | tf_op jit(solution)/shard_map/ppermute | solution.py:572

commit v4 on v3

--- a/solution.py
+++ b/solution.py
@@ -4,6 +4,7 @@
 from jax.experimental import pallas as pl
 from jax.experimental.pallas import tpu as pltpu
 from jax.sharding import PartitionSpec as P
+
 
 FACTOR = 4
 N = 256
@@ -25,15 +26,14 @@
 HB = pl.BlockSpec(memory_space=pltpu.HBM)
 
 
-def call(body, outs, ins, scratch=(), aliases=None, name=None, flops=0, limit=LIMIT):
+def call(body, outs, ins, scratch=(), aliases=None, flops=0, limit=LIMIT, out_specs=None):
     return pl.pallas_call(
         body,
         out_shape=[jax.ShapeDtypeStruct(s, F32) for s in outs],
         in_specs=[VM] * ins if isinstance(ins, int) else ins,
-        out_specs=[VM] * len(outs),
+        out_specs=out_specs or [VM] * len(outs),
         scratch_shapes=list(scratch),
         input_output_aliases=aliases or {},
-        name=name,
         compiler_params=pltpu.CompilerParams(vmem_limit_bytes=limit),
         cost_estimate=pl.CostEstimate(flops=flops, bytes_accessed=1000, transcendentals=0),
     )
@@ -70,7 +70,7 @@
         dest[pl.ds(v, 8, stride=count), :] = read(v)
 
 
-def sweep(src, fields, cols, count, emit):
+def sweep(src, edge, fields, cols, count, emit):
     lane = lanes(8)
     first, last = lane == 0, lane == 127
     held = {}
@@ -84,8 +84,9 @@
         for f in fields:
             mid = [at(f, j, v) for j in range(cols)]
             if cols == 3:
-                left = [pltpu.roll(mid[2], 1, 1), mid[0], mid[1]]
-                right = [mid[1], mid[2], pltpu.roll(mid[0], 127, 1)]
+                ends = None if edge is None else (edge[f, 0, vec(v), :], edge[f, 1, vec(v), :])
+                ends = ends or (pltpu.roll(mid[2], 1, 1), pltpu.roll(mid[0], 127, 1))
+                left, right = [ends[0], mid[0], mid[1]], [mid[1], mid[2], ends[1]]
             else:
                 back = [pltpu.roll(m, 1, 1) for m in mid]
                 ahead = [pltpu.roll(m, 127, 1) for m in mid]
@@ -99,18 +100,36 @@
             del held[key]
 
 
-def step(rhs, mid, scaled, inv, cof, fields, cols, count, after):
+def put_edge(edge, f, j, v, x):
+    if edge is not None and j == 2:
+        edge[f, 0, vec(v), :] = pltpu.roll(x, 1, 1)
+    if edge is not None and j == 0:
+        edge[f, 1, vec(v), :] = pltpu.roll(x, 127, 1)
+
+
+def step(rhs, mid, scaled, inv, cof, fields, cols, count, after, edges=(None, None)):
     def one(f, j, v, own, total):
         b = own * inv[j, vec(v), :]
         scaled[f, j, vec(v), :] = b
-        mid[f, j, vec(v), :] = b + cof[j, vec(v), :] * total
+        w = b + cof[j, vec(v), :] * total
+        mid[f, j, vec(v), :] = w
+        put_edge(edges[1], f, j, v, w)
 
     def two(f, j, v, own, total):
         u = scaled[f, j, vec(v), :] + cof[j, vec(v), :] * total
-        rhs[f, j, vec(v), :] = after(f, j, v, u)
-
-    sweep(rhs, fields, cols, count, one)
-    sweep(mid, fields, cols, count, two)
+        b = after(f, j, v, u)
+        rhs[f, j, vec(v), :] = b
+        put_edge(edges[0], f, j, v, b)
+
+    sweep(rhs, edges[0], fields, cols, count, one)
+    sweep(mid, edges[1], fields, cols, count, two)
+
+
+def put_edges(edge, rhs, fields):
+    for f in fields:
+        for v in range(V):
+            for j in (0, 2):
+                put_edge(edge, f, j, v, rhs[f, j, vec(v), :])
 
 
 def keep(f, j, v, u):
@@ -164,47 +183,50 @@
             write(b, h, turned[b, HALO + 128 * h : HALO + 128 * h + 128, :].T)
 
 
+def select(x, pick):
+    high = x.astype(jnp.bfloat16)
+    rest = x - high.astype(F32)
+    mid = rest.astype(jnp.bfloat16)
+    low = (rest - mid.astype(F32)).astype(jnp.bfloat16)
+    parts = [jnp.dot(p, pick, preferred_element_type=F32) for p in (low, mid, high)]
+    return (parts[0] + parts[1]) + parts[2]
+
+
 def restrict(ref, f, pair):
-    lane = lax.broadcasted_iota(jnp.int32, (128, C), 0)
-    coarse = lax.broadcasted_iota(jnp.int32, (128, C), 1)
-    out = None
+    lane = lax.broadcasted_iota(jnp.int32, (3 * 128, C), 0)
+    coarse = lax.broadcasted_iota(jnp.int32, (3 * 128, C), 1)
+    column = 3 * (lane % 128) + lane // 128
+    pick = jnp.where(column // 2 - 8 == coarse, 0.25, 0.0).astype(jnp.bfloat16)
     for j in range(3):
         for i in range(HV):
-            pair[vec(i), :] = ref[f, j, vec(2 * i), :] + ref[f, j, vec(2 * i + 1), :]
-        pick = jnp.where((3 * lane + j) // 2 - 8 == coarse, 0.25, 0.0).astype(F32)
-        part = jnp.dot(pair[...], pick, precision=lax.Precision.HIGHEST, preferred_element_type=F32)
-        out = part if out is None else out + part
-    return out
-
-
-def strips_body(source, iterate, start, conduct, up, down, last, sems):
+            pair[vec(i), 128 * j : 128 * j + 128] = ref[f, j, vec(2 * i), :] + ref[f, j, vec(2 * i + 1), :]
+    return select(pair[...], pick)
+
+
+def load_body(source, iterate, start, conduct, up, down, src, middle, last, coef, sems):
     is_end = lax.axis_index("tm") == lax.axis_size("tm") - 1
-    low, high = pl.ds(0, HALO), pl.ds(N - HALO, HALO)
-    copies = []
-    for ref, rows in ((up, low), (down, high)):
-        copies.append((source.at[:, rows, :], ref.at[pl.ds(0, 8)]))
-        copies.append((iterate.at[3, rows, :], ref.at[MID]))
-        copies.append((conduct.at[rows, :], ref.at[COEF]))
-    copies = [pltpu.make_async_copy(a, b, sems.at[i]) for i, (a, b) in enumerate(copies)]
+    pairs = ((source, src), (iterate.at[3], middle), (conduct, coef))
+    copies = [pltpu.make_async_copy(a, b, sems.at[i]) for i, (a, b) in enumerate(pairs)]
     for c in copies:
         c.start()
 
     @pl.when(is_end)
     def _():
-        c = pltpu.make_async_copy(start, last, sems.at[6])
+        c = pltpu.make_async_copy(start, last, sems.at[3])
         c.start()
         c.wait()
 
     @pl.when(jnp.logical_not(is_end))
     def _():
-        c = pltpu.make_async_copy(iterate.at[7], last, sems.at[6])
+        c = pltpu.make_async_copy(iterate.at[7], last, sems.at[3])
         c.start()
         c.wait()
 
-    up[LAST] = last[0:HALO, :]
-    down[LAST] = last[N - HALO : N, :]
     for c in copies:
         c.wait()
+    for f, ref in enumerate([src.at[f] for f in range(8)] + [middle, last, coef]):
+        up[f] = ref[0:HALO, :]
+        down[f] = ref[N - HALO : N, :]
 
 
 def pack_edges(pieces, rows):
@@ -219,13 +241,7 @@
     return low, high
 
 
-def center_body(source, iterate, last, conduct, turned, low, high, src, middle, coef, sems):
-    pairs = ((source, src), (iterate.at[3], middle), (conduct, coef))
-    copies = [pltpu.make_async_copy(a, b, sems.at[i]) for i, (a, b) in enumerate(pairs)]
-    for c in copies:
-        c.start()
-    for c in copies:
-        c.wait()
+def center_body(src, middle, last, coef, turned, low, high):
     for f, ref in enumerate([src.at[f] for f in range(8)] + [middle, last, coef]):
         turn(turned.at[f], ref)
         for b in range(2):
@@ -320,7 +336,7 @@
 def local_body(
     turned_in, above, below, before, after, before_c, after_c,
     turned, ext, coefs, forced, own_new, main, up, down, low_c, high_c, coarse,
-    rhs, mid, scaled, line, pair, rows_c,
+    rhs, mid, scaled, line, pair, rows_c, *edges,
 ):
     del turned_in
     t, x, z = lax.axis_index("tm"), lax.axis_index("sx"), lax.axis_index("sy")
@@ -350,12 +366,13 @@
             rhs[0, j, vec(v), :] = ext[MID, j, vec(v), :] + ext[4, j, vec(v), :]
             rhs[1, j, vec(v), :] = ext[0, j, vec(v), :]
             rhs[2, j, vec(v), :] = ext[LAST, j, vec(v), :]
+    put_edges(edges[0], rhs, range(3))
 
     def forced_step(k):
         def add(f, j, v, u):
             return u if f == 2 else u + ext[(5 if f == 0 else 1) + k, j, vec(v), :]
 
-        step(rhs, mid, scaled, inv, cof, range(3), 3, V, add)
+        step(rhs, mid, scaled, inv, cof, range(3), 3, V, add, edges)
 
     repeat(FACTOR - 1, forced_step)
 
@@ -370,6 +387,7 @@
                 s = rhs[1, j, vec(v), :]
                 forced[j, vec(v), :] = s
                 rhs[1, j, vec(v), :] = s - ext[MID, j, vec(v), :]
+        put_edges(edges[0], rhs, range(2))
         squeeze(main, scaled.at[0])
         for j in range(2):
             cols = slice(128 * j, 128 * j + 128)
@@ -382,14 +400,13 @@
             main[at + HALO : at + 2 * HALO, :] = turned[LAST, b, HALO + N : EXT, :]
 
     def free_step(k):
-        step(rhs, mid, scaled, inv, cof, range(3), 3, V, keep)
+        step(rhs, mid, scaled, inv, cof, range(3), 3, V, keep, edges)
         pl.when(k == 0)(between)
 
     repeat(FACTOR + 1, free_step)
     for k, (ref, f) in enumerate(((rhs, 1), (rhs, 0), (rhs, 2), (ext, COEF))):
-        got = restrict(ref, f, pair)
-        pair[...] = got
-        unmix(rows_c, lambda v: pair[vec(v), :], HV)
+        pair[:, 0:128] = restrict(ref, f, pair)
+        unmix(rows_c, lambda v: pair[vec(v), 0:128], HV)
         coarse[k] = rows_c[8 : 8 + C, :]
     for k in range(4):
         up[k] = coarse[k, 0:HALO, :]
@@ -497,7 +514,7 @@
 
 def final_body(
     one, two, three, four, ccoefs, coarse_mid, ext, coefs, new_start, new_mid, own_new,
-    out, err, cmid, cscaled, sent, fix, rhs, mid, scaled, turned, line, pair, rows_c,
+    out, err, cmid, cscaled, sent, fix, rhs, mid, scaled, turned, line, pair, rows_c, stage, sems,
 ):
     t = lax.axis_index("tm")
     m1, m2, m3 = flag(t > 0), flag(t > 1), flag(t > 2)
@@ -517,18 +534,20 @@
     err[0, 1] = m1 * (sent[0] + sent[2]) + m2 * sent[3] + m3 * four[1]
 
     def spread(k, extra=None):
-        src = lax.broadcasted_iota(jnp.int32, (128, 128), 0)
-        dst = lax.broadcasted_iota(jnp.int32, (128, 128), 1)
-        for c in range(2 if extra is None else 1):
+        src = lax.broadcasted_iota(jnp.int32, (256, 384), 0)
+        dst = lax.broadcasted_iota(jnp.int32, (256, 384), 1)
+        cell = (3 * (dst % 128) + dst // 128) // 2 - 8
+        cell = jnp.where(cell < 0, cell + 2 * C, jnp.where(dst % 128 < LIVE, cell, -1))
+        pick = flag(src == cell).astype(jnp.bfloat16)
+        for c in range(2):
             unmix(rows_c, lambda v: err[0, c, vec(v), :], CV)
-            mix(pair, natural(rows_c, HV, 8), HV)
-            value = pair[...] if extra is None else pair[...] + extra[...]
-            for j in range(3):
-                cell = (3 * dst + j) // 2 - 8
-                if c == 1:
-                    cell = jnp.where(cell < 0, cell + C, jnp.where((cell >= C) & (dst < LIVE), cell - C, -1))
-                got = jnp.dot(value, flag(src == cell), precision=lax.Precision.HIGHEST, preferred_element_type=F32)
-                fix[k, j] = got if c == 0 else fix[k, j] + got
+            for v in range(HV):
+                pair[vec(v), 128 * c : 128 * c + 128] = natural(rows_c, HV, 8)(v)
+        if extra is not None:
+            pair[:, 0:128] += extra[...]
+        got = select(pair[...], pick)
+        for j in range(3):
+            fix[k, j] = got[:, 128 * j : 128 * j + 128]
 
     spread(0)
     step(err, cmid, cscaled, inv, cof, range(1), 2, CV, keep)
@@ -546,13 +565,17 @@
             rhs[1, j, vec(v), :] = u + ext[4, j, vec(v), :]
             scaled[1, j, vec(v), :] = own_new[j, vec(v), :] + fix[2, j, vec(v // 2), :]
 
+    def send(f, at):
+        return pltpu.make_async_copy(stage.at[4 * f + at], out.at[4 * f + at], sems.at[4 * f + at])
+
     def give(at):
         for f in range(2):
 
             def put(b, h, block, f=f):
-                out[4 * f + at, 128 * b : 128 * b + 128, 128 * h : 128 * h + 128] = block
+                stage[4 * f + at, 128 * b : 128 * b + 128, 128 * h : 128 * h + 128] = block
 
             unlay(put, lambda j, v, f=f: scaled[f, j, vec(v), :], line, turned)
+            send(f, at).start()
 
     give(FACTOR - 1)
 
@@ -565,6 +588,9 @@
         give(k)
 
     repeat(FACTOR - 1, fine)
+    for f in range(2):
+        for at in range(FACTOR):
+            send(f, at).wait()
 
 
 def ring(x, axis, by):
@@ -577,45 +603,40 @@
 
 
 def shards(iterate, source, start_field, conduct):
-    up, down, last = call(
-        strips_body, [(FIELDS, HALO, N)] * 2 + [(N, N)], [HB] * 4, [pltpu.SemaphoreType.DMA((7,))], name="strips",
-        limit=63_000_000,
+    up, down, src, middle, last, coef = call(
+        load_body, [(FIELDS, HALO, N)] * 2 + [(8, N, N)] + [(N, N)] * 3, [HB] * 4, [pltpu.SemaphoreType.DMA((4,))],
+        limit=52_000_000,
     )(source, iterate, start_field, conduct)
     above, below = ring(down, "sx", 1), ring(up, "sx", -1)
     last_in = ring(last, "tm", 1)
     turned, low, high = call(
-        center_body,
-        [(FIELDS, 3, EXT, 128), (2, HALO * FIELDS, 128), (2, HALO * FIELDS, 128)],
-        [HB, HB, VM, HB],
-        [vmem(8, N, N), vmem(N, N), vmem(N, N), pltpu.SemaphoreType.DMA((3,))],
-        name="center", flops=20_000_000,
-    )(source, iterate, last, conduct)
+        center_body, [(FIELDS, 3, EXT, 128), (2, HALO * FIELDS, 128), (2, HALO * FIELDS, 128)], 4, flops=20_000_000
+    )(src, middle, last, coef)
     before, after = ring(high, "sy", 1), ring(low, "sy", -1)
     turned, c_lo, c_hi = call(
         rows_body, [(FIELDS, 3, EXT, 128), (3 * HALO, 128), (3 * HALO, 128)], 3,
-        [vmem(HALO, N), vmem(HALO, N), vmem(128, 128)], {0: 0}, "rows",
+        [vmem(HALO, N), vmem(HALO, N), vmem(128, 128)], {0: 0},
     )(turned, above, below)
     before_c, after_c = ring(c_hi, "sy", 1), ring(c_lo, "sy", -1)
-    before, after, before_c, after_c, last_in = lax.optimization_barrier((before, after, before_c, after_c, last_in))
     _, ext, coefs, forced, own_new, main, c_up, c_down, c_low, c_high, coarse = call(
         local_body,
         [
             (FIELDS, 3, EXT, 128), (FIELDS, 3, EXT, 128), (2, 3, EXT, 128), (3, EXT, 128), (3, EXT, 128), (MAIN, 128),
             (4, HALO, 128), (4, HALO, 128), (C, 128), (C, 128), (4, C, 128),
         ],
-        7, [vmem(3, 3, EXT, 128)] * 3 + [vmem(EXT, 128), vmem(HALF, 128), vmem(HALF, 128)],
-        {0: 0}, "local", 50_000_000,
+        7,
+        [vmem(3, 3, EXT, 128)] * 3 + [vmem(EXT, 128), vmem(HALF, 384), vmem(HALF, 128)] + [vmem(3, 2, EXT, 128)] * 2,
+        {0: 0}, 50_000_000,
     )(turned, above, below, before, after, before_c, after_c)
     c_above, c_below = ring(c_down, "sx", 1), ring(c_up, "sx", -1)
     main_in = ring(main, "tm", 1)
-    c_lo, c_hi = call(coarse_edges_body, [(CEXT, 128)] * 2, 4, name="coarse_edges")(c_above, c_below, c_low, c_high)
+    c_lo, c_hi = call(coarse_edges_body, [(CEXT, 128)] * 2, 4)(c_above, c_below, c_low, c_high)
     c_before, c_after = ring(c_hi, "sy", 1), ring(c_lo, "sy", -1)
     one, two, three, four, ccoefs = call(
         coarse_body,
         [(ONE, 128), (TWO, 128), (TWO, 128), (2, CEXT, 128), (2, 2, CEXT, 128)],
         5,
         [vmem(4, 2, CEXT, 128)] + [vmem(2, 2, CEXT, 128)] * 3 + [vmem(CEXT, 128)],
-        name="coarse",
     )(coarse, c_above, c_below, c_before, c_after)
     one, two, three = ring(one, "tm", 1), ring(two, "tm", 2), ring(three, "tm", 3)
     resid, new_start, new_mid, coarse_mid = call(
@@ -623,16 +644,17 @@
         [(2, N, N), (3, EXT, 128), (3, EXT, 128), (HALF, 128)],
         5,
         [vmem(2, 3, EXT, 128)] * 3
-        + [vmem(3, EXT, 128), vmem(HALO, N), vmem(HALO, N), vmem(128, 128), vmem(EXT, 128), vmem(HALF, 128)],
-        name="arrive", flops=30_000_000,
+        + [vmem(3, EXT, 128), vmem(HALO, N), vmem(HALO, N), vmem(128, 128), vmem(EXT, 128), vmem(HALF, 384)],
+        flops=30_000_000,
     )(last_in, main_in, ext, coefs, forced)
     (updated,) = call(
         final_body,
         [(8, N, N)],
         11,
         [vmem(1, 2, CEXT, 128)] * 3 + [vmem(4, CEXT, 128), vmem(3, 3, HALF, 128)] + [vmem(2, 3, EXT, 128)] * 3
-        + [vmem(2, EXT, 128), vmem(EXT, 128), vmem(HALF, 128), vmem(CEXT, 128)],
-        name="final",
+        + [vmem(2, EXT, 128), vmem(EXT, 128), vmem(HALF, 256), vmem(CEXT, 128), vmem(8, N, N)]
+        + [pltpu.SemaphoreType.DMA((8,))],
+        out_specs=[HB],
     )(one, two, three, four, ccoefs, coarse_mid, ext, coefs, new_start, new_mid, own_new)
     return updated, resid
 

time: 65.1 us -> 62.4 us (0.959)
  Pallas kernels: 28.4 us -> 26.6 us
  waiting for transfers between devices: 11.1 us -> 9.76 us
  starting transfers between devices: 22.2 us -> 23.1 us
  local copies, waits for them, and re-layouts: 2.55 us -> 1.89 us
    ppermute x15, waiting for transfers between devices: 11.1 us -> 9.76 us  [ring(): return lax.ppermute(x, axis, [(i, (i + by) % count) for i in range(count)])]
    ppermute x15, starting transfers between devices: 22.2 us -> 23.1 us  [ring(): return lax.ppermute(x, axis, [(i, (i + by) % count) for i in range(count)])]
    pallas_call x1, Pallas kernels: 6.37 us -> 5.61 us  [shards(): call(final_body, [(8, N, N)], 11, [vmem(1, 2, CEXT, 128)] * 3 + [vmem(4,...]
    unnamed x8 -> x4, local copies, waits for them, and re-layouts: 2.55 us -> 1.89 us
where the time goes in v4:
time: 62.4 us; the launch traced here: 62.2 us
  Pallas kernels  26.6 us (43%)
  starting transfers between devices  23.1 us (37%)
  waiting for transfers between devices  9.76 us (16%)
  local copies, waits for them, and re-layouts  1.89 us (3%)
  between operations  0.87 us (1%)
    ppermute x15, starting transfers between devices, ring(): return lax.ppermute(x, axis, [(i, (i + by) % count) for i in range(count)])  23.1 us
    pallas_call x1, Pallas kernels, shards(): call(local_body, [(FIELDS, 3, EXT, 128), (FIELDS, 3, EXT, 128), (2, 3, EX...  10.5 us
    ppermute x15, waiting for transfers between devices, ring(): return lax.ppermute(x, axis, [(i, (i + by) % count) for i in range(count)])  9.76 us
    pallas_call x1, Pallas kernels, shards(): call(final_body, [(8, N, N)], 11, [vmem(1, 2, CEXT, 128)] * 3 + [vmem(4,...  5.61 us
    pallas_call x1, Pallas kernels, shards(): call(arrive_body, [(2, N, N), (3, EXT, 128), (3, EXT, 128), (HALF, 128)],...  5.11 us
    pallas_call x1, Pallas kernels, shards(): call(coarse_body, [(ONE, 128), (TWO, 128), (TWO, 128), (2, CEXT, 128), (2...  2.2 us
    unnamed x4, local copies, waits for them, and re-layouts  1.89 us
    pallas_call x1, Pallas kernels, shards(): call(load_body, [(FIELDS, HALO, N)] * 2 + [(8, N, N)] + [(N, N)] * 3, [HB...  1.72 us
  transfers between devices with their start and end apart: 15, of which 6 were waited for; matrix products, arithmetic and copies ran while one was open for 0% of the time, Pallas kernels for 14%

profile of v4, /device:TPU:64, one launch (start us, length us, event | category | flops | bytes accessed | tf_op | source)
XLA Modules:
  0.0 62.2 jit_solution(16920151527173555001)
XLA Ops:
  0.6 0.0 copy-start
  0.6 0.9 %copy-done = f32[256,256]{1,0:T(8,128)S(1)} copy-done((f32[256,256]{1,0:T(8,128)S(1)}, f32[256,256]{1,0:T(8,128)}, u32[]{:S(2)}) %copy-start) | copy-done | bytes 262168
  1.6 0.0 copy-start.1
  1.6 0.9 %copy-done.1 = f32[256,256]{1,0:T(8,128)S(1)} copy-done((f32[256,256]{1,0:T(8,128)S(1)}, f32[256,256]{1,0:T(8,128)}, u32[]{:S(2)}) %copy-start.1) | copy-done | bytes 262168
  2.5 1.7 %shard_map.59 = (f32[11,16,256]{2,1,0:T(8,128)S(1)}, f32[11,16,256]{2,1,0:T(8,128)S(1)}, f32[8,256,256]{2,1,0:T(8,128)S(1)}, f32[256,256]{1,0:T(8,128)S(1)}, f32...) custom-call(f32[8,256,256]{2,1,0:T(8,128)} %source.1, f32[8,256,256]{2,1,0:T(8,128)} %iterate.1, f32[256,256]{1,0:T(8,128)S(1)} %copy-done, ...), custom_call_target="tpu_custom_call" | custom-call | bytes 1000 | tf_op jit(solution)/shard_map/pallas_call | solution.py:606
  4.3 0.0 collective-permute-start
  4.3 2.9 %collective-permute-start.1 = (f32[11,16,256]{2,1,0:T(8,128)S(1)}, f32[11,16,256]{2,1,0:T(8,128)S(1)}, u32[]{:S(2)}, u32[]{:S(2)}) collective-permute-start(f32[11,16,256]{2,1,0:T(8,128)S(1)} %get-tuple-element.41), channel_id=1, source_target_pairs={{0,56},{8,0},{16,8},{24,16},{32,24},{40,32},{48,40},{56,48},{1,57}... | collective-permute-start | bytes 540680 | tf_op jit(solution)/shard_map/ppermute | solution.py:598
  7.2 0.8 %shard_map.60 = (f32[11,3,288,128]{3,2,1,0:T(8,128)S(1)}, f32[2,176,128]{2,1,0:T(8,128)S(1)}, f32[2,176,128]{2,1,0:T(8,128)S(1)}) custom-call(f32[8,256,256]{2,1,0:T(8,128)S(1)} %get-tuple-element.35.src, f32[256,256]{1,0:T(8,128)S(1)} %get-tuple-element.36.middle, f32[256,256]{1,0:T(8,128)S(1)} %get-tuple-element.37.last, f32[256,256]{1,0:T(8,128)S(1)} %get-tuple-element.38.coef), custom_call_target="tpu_custom_call" | custom-call | flops 20000000 | bytes 1000 | tf_op jit(solution)/shard_map/pallas_call | solution.py:612
  8.0 2.0 %collective-permute-start.2 = (f32[2,176,128]{2,1,0:T(8,128)S(1)}, f32[2,176,128]{2,1,0:T(8,128)S(1)}, u32[]{:S(2)}, u32[]{:S(2)}) collective-permute-start(f32[2,176,128]{2,1,0:T(8,128)S(1)} %get-tuple-element.43), channel_id=1, source_target_pairs={{0,1},{1,2},{2,3},{3,4},{4,5},{5,6},{6,7},{7,0},{8,9},{9,10},{10,1... | collective-permute-start | bytes 540680 | tf_op jit(solution)/shard_map/ppermute | solution.py:598
  10.0 0.1 collective-permute-start.3
  10.1 0.3 collective-permute-done.above
  10.4 0.0 collective-permute-done.1.below
  10.4 0.5 shard_map.61
  10.9 2.9 %collective-permute-start.4 = (f32[48,128]{1,0:T(8,128)S(1)}, f32[48,128]{1,0:T(8,128)S(1)}, u32[]{:S(2)}, u32[]{:S(2)}) collective-permute-start(f32[48,128]{1,0:T(8,128)S(1)} %get-tuple-element.45), channel_id=1, source_target_pairs={{0,1},{1,2},{2,3},{3,4},{4,5},{5,6},{6,7},{7,0},{8,9},{9,10},{10,1... | collective-permute-start | bytes 73736 | tf_op jit(solution)/shard_map/ppermute | solution.py:598
  13.8 0.0 collective-permute-start.5
  13.8 0.0 collective-permute-done.2.before
  13.8 2.9 %collective-permute-done.3.after = f32[2,176,128]{2,1,0:T(8,128)S(1)} collective-permute-done((f32[2,176,128]{2,1,0:T(8,128)S(1)}, f32[2,176,128]{2,1,0:T(8,128)S(1)}, u32[]{:S(2)}, u32[]{:S(2)}) %collective-permute-start.3) | collective-permute-done | bytes 180256 | tf_op jit(solution)/shard_map/ppermute | solution.py:598
  16.6 0.0 collective-permute-done.4.before_c
  16.6 2.2 %collective-permute-done.5.after_c = f32[48,128]{1,0:T(8,128)S(1)} collective-permute-done((f32[48,128]{1,0:T(8,128)S(1)}, f32[48,128]{1,0:T(8,128)S(1)}, u32[]{:S(2)}, u32[]{:S(2)}) %collective-permute-start.5) | collective-permute-done | bytes 24608 | tf_op jit(solution)/shard_map/ppermute | solution.py:598
  18.8 10.5 %shard_map.62 = (f32[11,3,288,128]{3,2,1,0:T(8,128)S(1)}, f32[11,3,288,128]{3,2,1,0:T(8,128)S(1)}, f32[2,3,288,128]{3,2,1,0:T(8,128)S(1)}, f32[3,288,128]{2,1,0:...) custom-call(f32[11,3,288,128]{3,2,1,0:T(8,128)S(1)} %get-tuple-eleme, ...), custom_call_target="tpu_custom_call", output_to_operand_aliasing={{0}: (0, {})} | custom-call | flops 50000000 | bytes 1000 | tf_op jit(solution)/shard_map/pallas_call | solution.py:621
  29.4 1.7 %collective-permute-start.14 = (f32[808,128]{1,0:T(8,128)S(1)}, f32[808,128]{1,0:T(8,128)S(1)}, u32[]{:S(2)}, u32[]{:S(2)}) collective-permute-start(f32[808,128]{1,0:T(8,128)S(1)} %get-tuple-element.59), channel_id=1, source_target_pairs={{0,64},{64,128},{128,192},{192,0},{1,65},{65,129},{129,193},{193,1... | collective-permute-start | bytes 1241096 | tf_op jit(solution)/shard_map/ppermute | solution.py:598
  31.0 0.0 collective-permute-start.6
  31.0 3.0 %collective-permute-start.7 = (f32[4,16,128]{2,1,0:T(8,128)S(1)}, f32[4,16,128]{2,1,0:T(8,128)S(1)}, u32[]{:S(2)}, u32[]{:S(2)}) collective-permute-start(f32[4,16,128]{2,1,0:T(8,128)S(1)} %get-tuple-element.49), channel_id=1, source_target_pairs={{0,56},{8,0},{16,8},{24,16},{32,24},{40,32},{48,40},{56,48},{1,57}... | collective-permute-start | bytes 98312 | tf_op jit(solution)/shard_map/ppermute | solution.py:598
  34.0 1.6 %collective-permute-done.6.above = f32[4,16,128]{2,1,0:T(8,128)S(1)} collective-permute-done((f32[4,16,128]{2,1,0:T(8,128)S(1)}, f32[4,16,128]{2,1,0:T(8,128)S(1)}, u32[]{:S(2)}, u32[]{:S(2)}) %collective-permute-start.6) | collective-permute-done | bytes 32800 | tf_op jit(solution)/shard_map/ppermute | solution.py:598
  35.6 0.0 collective-permute-done.7.below
  35.6 0.1 shard_map.63
  35.7 3.3 %collective-permute-start.8 = (f32[160,128]{1,0:T(8,128)S(1)}, f32[160,128]{1,0:T(8,128)S(1)}, u32[]{:S(2)}, u32[]{:S(2)}) collective-permute-start(f32[160,128]{1,0:T(8,128)S(1)} %get-tuple-element.52), channel_id=1, source_target_pairs={{0,1},{1,2},{2,3},{3,4},{4,5},{5,6},{6,7},{7,0},{8,9},{9,10},{10,1... | collective-permute-start | bytes 245768 | tf_op jit(solution)/shard_map/ppermute | solution.py:598
  39.0 0.0 collective-permute-start.9
  39.0 1.6 %collective-permute-start.13 = (f32[256,256]{1,0:T(8,128)S(1)}, f32[256,256]{1,0:T(8,128)S(1)}, u32[]{:S(2)}, u32[]{:S(2)}) collective-permute-start(f32[256,256]{1,0:T(8,128)S(1)} %get-tuple-element.37.last), channel_id=1, source_target_pairs={{0,64},{64,128},{128,192},{192,0},{1,65},{65,129},{129,193},{193,1... | collective-permute-start | bytes 786440 | tf_op jit(solution)/shard_map/ppermute | solution.py:598
  40.6 0.5 collective-permute-done.8.before
  41.0 2.4 %collective-permute-done.9.after = f32[160,128]{1,0:T(8,128)S(1)} collective-permute-done((f32[160,128]{1,0:T(8,128)S(1)}, f32[160,128]{1,0:T(8,128)S(1)}, u32[]{:S(2)}, u32[]{:S(2)}) %collective-permute-start.9) | collective-permute-done | bytes 81952 | tf_op jit(solution)/shard_map/ppermute | solution.py:598
  43.4 2.2 %shard_map.64 = (f32[360,128]{1,0:T(8,128)S(1)}, f32[192,128]{1,0:T(8,128)S(1)}, f32[192,128]{1,0:T(8,128)S(1)}, f32[2,160,128]{2,1,0:T(8,128)S(1)}, f32[2,2,160,128]{3,2,1,0:T(8,128)S(1)}) custom-call(f32[4,128,128]{2,1,0:T(8,128)S(1)} %get-tuple-element.47.coarse, f32[4,16,128]{2,1,0:T(8,128)S(1)} %collective-permute-done.6.above, ...), custom_call_target="tpu_custom_call" | custom-call | bytes 1000 | tf_op jit(solution)/shard_map/pallas_call | solution.py:635
  45.6 1.8 %collective-permute-start.10 = (f32[360,128]{1,0:T(8,128)S(1)}, f32[360,128]{1,0:T(8,128)S(1)}, u32[]{:S(2)}, u32[]{:S(2)}) collective-permute-start(f32[360,128]{1,0:T(8,128)S(1)} %get-tuple-element.54), channel_id=1, source_target_pairs={{0,64},{64,128},{128,192},{192,0},{1,65},{65,129},{129,193},{193,1... | collective-permute-start | bytes 552968 | tf_op jit(solution)/shard_map/ppermute | solution.py:598
  47.5 1.5 %collective-permute-start.11 = (f32[192,128]{1,0:T(8,128)S(1)}, f32[192,128]{1,0:T(8,128)S(1)}, u32[]{:S(2)}, u32[]{:S(2)}) collective-permute-start(f32[192,128]{1,0:T(8,128)S(1)} %get-tuple-element.55), channel_id=1, source_target_pairs={{0,128},{64,192},{128,0},{192,64},{1,129},{65,193},{129,1},{193,65... | collective-permute-start | bytes 294920 | tf_op jit(solution)/shard_map/ppermute | solution.py:598
  49.0 2.3 %collective-permute-start.12 = (f32[192,128]{1,0:T(8,128)S(1)}, f32[192,128]{1,0:T(8,128)S(1)}, u32[]{:S(2)}, u32[]{:S(2)}) collective-permute-start(f32[192,128]{1,0:T(8,128)S(1)} %get-tuple-element.56), channel_id=1, source_target_pairs={{0,192},{64,0},{128,64},{192,128},{1,193},{65,1},{129,65},{193,129... | collective-permute-start | bytes 294920 | tf_op jit(solution)/shard_map/ppermute | solution.py:598
  51.3 0.0 collective-permute-done.13.last
  51.4 0.0 collective-permute-done.14.main
  51.4 5.1 %shard_map.65 = (f32[2,256,256]{2,1,0:T(8,128)}, f32[3,288,128]{2,1,0:T(8,128)S(1)}, f32[3,288,128]{2,1,0:T(8,128)S(1)}, f32[144,128]{1,0:T(8,128)S(1)}) custom-call(f32[256,256]{1,0:T(8,128)S(1)} %collective-permute-done.13.last, f32[808,128]{1,0:T(8,128)S(1)} %collective-permute-done.14.main, f32[11,3,288,128]{3,2,1,0:T(8,128)S(1)} %get-tuple-element.60.ext, ...), custom_call_target="tpu_custom_call" | custom-call | flops 30000000 | bytes 1000 | tf_op jit(solution)/shard_map/pallas_call | solution.py:642
  56.5 0.0 collective-permute-done.11.two
  56.5 0.0 collective-permute-done.12.three
  56.5 0.0 collective-permute-done.10.one
  56.5 5.6 %shard_map.66 = f32[8,256,256]{2,1,0:T(8,128)} custom-call(f32[360,128]{1,0:T(8,128)S(1)} %collective-permute-done.10.one, f32[192,128]{1,0:T(8,128)S(1)} %collective-permute-done.11.two, f32[192,128]{1,0:T(8,128)S(1)} %collective-permute-done.12.three, f32[2,160,128]{2,1,0:T(8,128)S(1)} %get-tuple-element.57.four, ...), custom_call_target="tpu_custom_call" | custom-call | bytes 1000 | tf_op jit(solution)/shard_map/pallas_call | solution.py:650
Async XLA Ops:
  0.6 1.0 %copy-start = (f32[256,256]{1,0:T(8,128)S(1)}, f32[256,256]{1,0:T(8,128)}, u32[]{:S(2)}) copy-start(f32[256,256]{1,0:T(8,128)} %start.1) | copy-start | bytes 786436
  1.6 0.9 %copy-start.1 = (f32[256,256]{1,0:T(8,128)S(1)}, f32[256,256]{1,0:T(8,128)}, u32[]{:S(2)}) copy-start(f32[256,256]{1,0:T(8,128)} %conduct.1) | copy-start | bytes 786436
  4.3 6.1 %collective-permute-start = (f32[11,16,256]{2,1,0:T(8,128)S(1)}, f32[11,16,256]{2,1,0:T(8,128)S(1)}, u32[]{:S(2)}, u32[]{:S(2)}) collective-permute-start(f32[11,16,256]{2,1,0:T(8,128)S(1)} %get-tuple-element.40), channel_id=1, source_target_pairs={{0,8},{8,16},{16,24},{24,32},{32,40},{40,48},{48,56},{56,0},{1,9},... | collective-permute-start | bytes 540680 | tf_op jit(solution)/shard_map/ppermute | solution.py:598
  4.3 6.1 %collective-permute-start.1 = (f32[11,16,256]{2,1,0:T(8,128)S(1)}, f32[11,16,256]{2,1,0:T(8,128)S(1)}, u32[]{:S(2)}, u32[]{:S(2)}) collective-permute-start(f32[11,16,256]{2,1,0:T(8,128)S(1)} %get-tuple-element.41), channel_id=1, source_target_pairs={{0,56},{8,0},{16,8},{24,16},{32,24},{40,32},{48,40},{56,48},{1,57}... | collective-permute-start | bytes 540680 | tf_op jit(solution)/shard_map/ppermute | solution.py:598
  8.0 5.7 %collective-permute-start.2 = (f32[2,176,128]{2,1,0:T(8,128)S(1)}, f32[2,176,128]{2,1,0:T(8,128)S(1)}, u32[]{:S(2)}, u32[]{:S(2)}) collective-permute-start(f32[2,176,128]{2,1,0:T(8,128)S(1)} %get-tuple-element.43), channel_id=1, source_target_pairs={{0,1},{1,2},{2,3},{3,4},{4,5},{5,6},{6,7},{7,0},{8,9},{9,10},{10,1... | collective-permute-start | bytes 540680 | tf_op jit(solution)/shard_map/ppermute | solution.py:598
  10.0 6.6 %collective-permute-start.3 = (f32[2,176,128]{2,1,0:T(8,128)S(1)}, f32[2,176,128]{2,1,0:T(8,128)S(1)}, u32[]{:S(2)}, u32[]{:S(2)}) collective-permute-start(f32[2,176,128]{2,1,0:T(8,128)S(1)} %get-tuple-element.44), channel_id=1, source_target_pairs={{0,7},{1,0},{2,1},{3,2},{4,3},{5,4},{6,5},{7,6},{8,15},{9,8},{10,9... | collective-permute-start | bytes 540680 | tf_op jit(solution)/shard_map/ppermute | solution.py:598
  10.9 5.7 %collective-permute-start.4 = (f32[48,128]{1,0:T(8,128)S(1)}, f32[48,128]{1,0:T(8,128)S(1)}, u32[]{:S(2)}, u32[]{:S(2)}) collective-permute-start(f32[48,128]{1,0:T(8,128)S(1)} %get-tuple-element.45), channel_id=1, source_target_pairs={{0,1},{1,2},{2,3},{3,4},{4,5},{5,6},{6,7},{7,0},{8,9},{9,10},{10,1... | collective-permute-start | bytes 73736 | tf_op jit(solution)/shard_map/ppermute | solution.py:598
  13.8 5.0 %collective-permute-start.5 = (f32[48,128]{1,0:T(8,128)S(1)}, f32[48,128]{1,0:T(8,128)S(1)}, u32[]{:S(2)}, u32[]{:S(2)}) collective-permute-start(f32[48,128]{1,0:T(8,128)S(1)} %get-tuple-element.46), channel_id=1, source_target_pairs={{0,7},{1,0},{2,1},{3,2},{4,3},{5,4},{6,5},{7,6},{8,15},{9,8},{10,9... | collective-permute-start | bytes 73736 | tf_op jit(solution)/shard_map/ppermute | solution.py:598
  29.4 22.0 %collective-permute-start.14 = (f32[808,128]{1,0:T(8,128)S(1)}, f32[808,128]{1,0:T(8,128)S(1)}, u32[]{:S(2)}, u32[]{:S(2)}) collective-permute-start(f32[808,128]{1,0:T(8,128)S(1)} %get-tuple-element.59), channel_id=1, source_target_pairs={{0,64},{64,128},{128,192},{192,0},{1,65},{65,129},{129,193},{193,1... | collective-permute-start | bytes 1241096 | tf_op jit(solution)/shard_map/ppermute | solution.py:598
  31.0 4.6 %collective-permute-start.6 = (f32[4,16,128]{2,1,0:T(8,128)S(1)}, f32[4,16,128]{2,1,0:T(8,128)S(1)}, u32[]{:S(2)}, u32[]{:S(2)}) collective-permute-start(f32[4,16,128]{2,1,0:T(8,128)S(1)} %get-tuple-element.48), channel_id=1, source_target_pairs={{0,8},{8,16},{16,24},{24,32},{32,40},{40,48},{48,56},{56,0},{1,9},... | collective-permute-start | bytes 98312 | tf_op jit(solution)/shard_map/ppermute | solution.py:598
  31.0 4.6 %collective-permute-start.7 = (f32[4,16,128]{2,1,0:T(8,128)S(1)}, f32[4,16,128]{2,1,0:T(8,128)S(1)}, u32[]{:S(2)}, u32[]{:S(2)}) collective-permute-start(f32[4,16,128]{2,1,0:T(8,128)S(1)} %get-tuple-element.49), channel_id=1, source_target_pairs={{0,56},{8,0},{16,8},{24,16},{32,24},{40,32},{48,40},{56,48},{1,57}... | collective-permute-start | bytes 98312 | tf_op jit(solution)/shard_map/ppermute | solution.py:598
  35.7 5.4 %collective-permute-start.8 = (f32[160,128]{1,0:T(8,128)S(1)}, f32[160,128]{1,0:T(8,128)S(1)}, u32[]{:S(2)}, u32[]{:S(2)}) collective-permute-start(f32[160,128]{1,0:T(8,128)S(1)} %get-tuple-element.52), channel_id=1, source_target_pairs={{0,1},{1,2},{2,3},{3,4},{4,5},{5,6},{6,7},{7,0},{8,9},{9,10},{10,1... | collective-permute-start | bytes 245768 | tf_op jit(solution)/shard_map/ppermute | solution.py:598
  39.0 4.4 %collective-permute-start.9 = (f32[160,128]{1,0:T(8,128)S(1)}, f32[160,128]{1,0:T(8,128)S(1)}, u32[]{:S(2)}, u32[]{:S(2)}) collective-permute-start(f32[160,128]{1,0:T(8,128)S(1)} %get-tuple-element.53), channel_id=1, source_target_pairs={{0,7},{1,0},{2,1},{3,2},{4,3},{5,4},{6,5},{7,6},{8,15},{9,8},{10,9... | collective-permute-start | bytes 245768 | tf_op jit(solution)/shard_map/ppermute | solution.py:598
  39.0 12.4 %collective-permute-start.13 = (f32[256,256]{1,0:T(8,128)S(1)}, f32[256,256]{1,0:T(8,128)S(1)}, u32[]{:S(2)}, u32[]{:S(2)}) collective-permute-start(f32[256,256]{1,0:T(8,128)S(1)} %get-tuple-element.37.last), channel_id=1, source_target_pairs={{0,64},{64,128},{128,192},{192,0},{1,65},{65,129},{129,193},{193,1... | collective-permute-start | bytes 786440 | tf_op jit(solution)/shard_map/ppermute | solution.py:598
  45.6 10.8 %collective-permute-start.10 = (f32[360,128]{1,0:T(8,128)S(1)}, f32[360,128]{1,0:T(8,128)S(1)}, u32[]{:S(2)}, u32[]{:S(2)}) collective-permute-start(f32[360,128]{1,0:T(8,128)S(1)} %get-tuple-element.54), channel_id=1, source_target_pairs={{0,64},{64,128},{128,192},{192,0},{1,65},{65,129},{129,193},{193,1... | collective-permute-start | bytes 552968 | tf_op jit(solution)/shard_map/ppermute | solution.py:598
  47.5 9.0 %collective-permute-start.11 = (f32[192,128]{1,0:T(8,128)S(1)}, f32[192,128]{1,0:T(8,128)S(1)}, u32[]{:S(2)}, u32[]{:S(2)}) collective-permute-start(f32[192,128]{1,0:T(8,128)S(1)} %get-tuple-element.55), channel_id=1, source_target_pairs={{0,128},{64,192},{128,0},{192,64},{1,129},{65,193},{129,1},{193,65... | collective-permute-start | bytes 294920 | tf_op jit(solution)/shard_map/ppermute | solution.py:598
  49.0 7.5 %collective-permute-start.12 = (f32[192,128]{1,0:T(8,128)S(1)}, f32[192,128]{1,0:T(8,128)S(1)}, u32[]{:S(2)}, u32[]{:S(2)}) collective-permute-start(f32[192,128]{1,0:T(8,128)S(1)} %get-tuple-element.56), channel_id=1, source_target_pairs={{0,192},{64,0},{128,64},{192,128},{1,193},{65,1},{129,65},{193,129... | collective-permute-start | bytes 294920 | tf_op jit(solution)/shard_map/ppermute | solution.py:598

commit v5 on v4

--- a/solution.py
+++ b/solution.py
@@ -165,18 +165,19 @@
         for b in range(3):
             got = jnp.concatenate([turned[b, pl.ds(j, LIVE, stride=3), :], pad], axis=0).T
             if b < 2:
-                line[HALO + 128 * b : HALO + 128 * b + 128, :] = got
+                line[j, HALO + 128 * b : HALO + 128 * b + 128, :] = got
             else:
-                line[HALO + N : EXT, :] = got[0:HALO, :]
-                line[0:HALO, :] = got[128 - HALO : 128, :]
-        mix(dst.at[j], natural(line, V), V)
+                line[j, HALO + N : EXT, :] = got[0:HALO, :]
+                line[j, 0:HALO, :] = got[128 - HALO : 128, :]
+    for j in range(3):
+        mix(dst.at[j], natural(line.at[j], V), V)
 
 
 def unlay(write, read, line, turned):
     for j in range(3):
-        unmix(line, lambda v: read(j, v), V)
+        unmix(line.at[j], lambda v: read(j, v), V)
         for b in range(2):
-            got = line[HALO + 128 * b : HALO + 128 * b + 128, :].T
+            got = line[j, HALO + 128 * b : HALO + 128 * b + 128, :].T
             turned[b, pl.ds(j, LIVE, stride=3), :] = got[0:LIVE, :]
     for b in range(2):
         for h in range(2):
@@ -353,10 +354,12 @@
             x = roll(corner[HALO * (f % 3) : HALO * (f % 3) + HALO, :], -HALO - 2 * HALO * (f // 3))
             turned[f, 2, base : base + HALO, :] = jnp.where(ends, x * present, 0.0)
 
-    def lay_field(f):
-        lay(ext.at[f], turned.at[f], line)
-
-    repeat(FIELDS, lay_field)
+    def lay_fields(k):
+        for i in range(2):
+            lay(ext.at[2 * k + i], turned.at[2 * k + i], line.at[i])
+
+    repeat(FIELDS // 2, lay_fields)
+    lay(ext.at[FIELDS - 1], turned.at[FIELDS - 1], line.at[0])
     for v in range(V):
         for j in range(3):
             c = ext[COEF, j, vec(v), :]
@@ -405,9 +408,9 @@
 
     repeat(FACTOR + 1, free_step)
     for k, (ref, f) in enumerate(((rhs, 1), (rhs, 0), (rhs, 2), (ext, COEF))):
-        pair[:, 0:128] = restrict(ref, f, pair)
-        unmix(rows_c, lambda v: pair[vec(v), 0:128], HV)
-        coarse[k] = rows_c[8 : 8 + C, :]
+        got = restrict(ref, f, pair.at[k])
+        unmix(rows_c.at[k], lambda v: got[vec(v), :], HV)
+        coarse[k] = rows_c[k, 8 : 8 + C, :]
     for k in range(4):
         up[k] = coarse[k, 0:HALO, :]
         down[k] = coarse[k, C - HALO : C, :]
@@ -574,7 +577,7 @@
             def put(b, h, block, f=f):
                 stage[4 * f + at, 128 * b : 128 * b + 128, 128 * h : 128 * h + 128] = block
 
-            unlay(put, lambda j, v, f=f: scaled[f, j, vec(v), :], line, turned)
+            unlay(put, lambda j, v, f=f: scaled[f, j, vec(v), :], line.at[f], turned.at[f])
             send(f, at).start()
 
     give(FACTOR - 1)
@@ -625,7 +628,7 @@
             (4, HALO, 128), (4, HALO, 128), (C, 128), (C, 128), (4, C, 128),
         ],
         7,
-        [vmem(3, 3, EXT, 128)] * 3 + [vmem(EXT, 128), vmem(HALF, 384), vmem(HALF, 128)] + [vmem(3, 2, EXT, 128)] * 2,
+        [vmem(3, 3, EXT, 128)] * 3 + [vmem(2, 3, EXT, 128), vmem(4, HALF, 384), vmem(4, HALF, 128)] + [vmem(3, 2, EXT, 128)] * 2,
         {0: 0}, 50_000_000,
     )(turned, above, below, before, after, before_c, after_c)
     c_above, c_below = ring(c_down, "sx", 1), ring(c_up, "sx", -1)
@@ -644,7 +647,7 @@
         [(2, N, N), (3, EXT, 128), (3, EXT, 128), (HALF, 128)],
         5,
         [vmem(2, 3, EXT, 128)] * 3
-        + [vmem(3, EXT, 128), vmem(HALO, N), vmem(HALO, N), vmem(128, 128), vmem(EXT, 128), vmem(HALF, 384)],
+        + [vmem(3, EXT, 128), vmem(HALO, N), vmem(HALO, N), vmem(128, 128), vmem(3, EXT, 128), vmem(HALF, 384)],
         flops=30_000_000,
     )(last_in, main_in, ext, coefs, forced)
     (updated,) = call(
@@ -652,7 +655,7 @@
         [(8, N, N)],
         11,
         [vmem(1, 2, CEXT, 128)] * 3 + [vmem(4, CEXT, 128), vmem(3, 3, HALF, 128)] + [vmem(2, 3, EXT, 128)] * 3
-        + [vmem(2, EXT, 128), vmem(EXT, 128), vmem(HALF, 256), vmem(CEXT, 128), vmem(8, N, N)]
+        + [vmem(2, 2, EXT, 128), vmem(2, 3, EXT, 128), vmem(HALF, 256), vmem(CEXT, 128), vmem(8, N, N)]
         + [pltpu.SemaphoreType.DMA((8,))],
         out_specs=[HB],
     )(one, two, three, four, ccoefs, coarse_mid, ext, coefs, new_start, new_mid, own_new)

time: 62.4 us -> 61.1 us (0.979)
  Pallas kernels: 26.6 us -> 25.4 us
    pallas_call x1, Pallas kernels: 10.5 us -> 9.45 us  [shards(): call(local_body, [(FIELDS, 3, EXT, 128), (FIELDS, 3, EXT, 128), (2, 3, EX...]
where the time goes in v5:
time: 61.1 us; the launch traced here: 60.9 us
  Pallas kernels  25.4 us (42%)
  starting transfers between devices  22.9 us (37%)
  waiting for transfers between devices  9.76 us (16%)
  local copies, waits for them, and re-layouts  1.89 us (3%)
  between operations  0.87 us (1%)
    ppermute x15, starting transfers between devices, ring(): return lax.ppermute(x, axis, [(i, (i + by) % count) for i in range(count)])  22.9 us
    ppermute x15, waiting for transfers between devices, ring(): return lax.ppermute(x, axis, [(i, (i + by) % count) for i in range(count)])  9.76 us
    pallas_call x1, Pallas kernels, shards(): call(local_body, [(FIELDS, 3, EXT, 128), (FIELDS, 3, EXT, 128), (2, 3, EX...  9.45 us
    pallas_call x1, Pallas kernels, shards(): call(final_body, [(8, N, N)], 11, [vmem(1, 2, CEXT, 128)] * 3 + [vmem(4,...  5.56 us
    pallas_call x1, Pallas kernels, shards(): call(arrive_body, [(2, N, N), (3, EXT, 128), (3, EXT, 128), (HALF, 128)],...  5.1 us
    pallas_call x1, Pallas kernels, shards(): call(coarse_body, [(ONE, 128), (TWO, 128), (TWO, 128), (2, CEXT, 128), (2...  2.2 us
    unnamed x4, local copies, waits for them, and re-layouts  1.89 us
    pallas_call x1, Pallas kernels, shards(): call(load_body, [(FIELDS, HALO, N)] * 2 + [(8, N, N)] + [(N, N)] * 3, [HB...  1.72 us
  transfers between devices with their start and end apart: 15, of which 6 were waited for; matrix products, arithmetic and copies ran while one was open for 0% of the time, Pallas kernels for 14%

profile of v5, /device:TPU:64, one launch (start us, length us, event | category | flops | bytes accessed | tf_op | source)
XLA Modules:
  0.0 60.9 jit_solution(14390638479552998920)
XLA Ops:
  0.6 0.0 copy-start
  0.6 0.9 %copy-done = f32[256,256]{1,0:T(8,128)S(1)} copy-done((f32[256,256]{1,0:T(8,128)S(1)}, f32[256,256]{1,0:T(8,128)}, u32[]{:S(2)}) %copy-start) | copy-done | bytes 262168
  1.6 0.0 copy-start.1
  1.6 0.9 %copy-done.1 = f32[256,256]{1,0:T(8,128)S(1)} copy-done((f32[256,256]{1,0:T(8,128)S(1)}, f32[256,256]{1,0:T(8,128)}, u32[]{:S(2)}) %copy-start.1) | copy-done | bytes 262168
  2.5 1.7 %shard_map.59 = (f32[11,16,256]{2,1,0:T(8,128)S(1)}, f32[11,16,256]{2,1,0:T(8,128)S(1)}, f32[8,256,256]{2,1,0:T(8,128)S(1)}, f32[256,256]{1,0:T(8,128)S(1)}, f32...) custom-call(f32[8,256,256]{2,1,0:T(8,128)} %source.1, f32[8,256,256]{2,1,0:T(8,128)} %iterate.1, f32[256,256]{1,0:T(8,128)S(1)} %copy-done, ...), custom_call_target="tpu_custom_call" | custom-call | bytes 1000 | tf_op jit(solution)/shard_map/pallas_call | solution.py:609
  4.3 0.0 collective-permute-start
  4.3 2.9 %collective-permute-start.1 = (f32[11,16,256]{2,1,0:T(8,128)S(1)}, f32[11,16,256]{2,1,0:T(8,128)S(1)}, u32[]{:S(2)}, u32[]{:S(2)}) collective-permute-start(f32[11,16,256]{2,1,0:T(8,128)S(1)} %get-tuple-element.41), channel_id=1, source_target_pairs={{0,56},{8,0},{16,8},{24,16},{32,24},{40,32},{48,40},{56,48},{1,57}... | collective-permute-start | bytes 540680 | tf_op jit(solution)/shard_map/ppermute | solution.py:601
  7.2 0.8 %shard_map.60 = (f32[11,3,288,128]{3,2,1,0:T(8,128)S(1)}, f32[2,176,128]{2,1,0:T(8,128)S(1)}, f32[2,176,128]{2,1,0:T(8,128)S(1)}) custom-call(f32[8,256,256]{2,1,0:T(8,128)S(1)} %get-tuple-element.35.src, f32[256,256]{1,0:T(8,128)S(1)} %get-tuple-element.36.middle, f32[256,256]{1,0:T(8,128)S(1)} %get-tuple-element.37.last, f32[256,256]{1,0:T(8,128)S(1)} %get-tuple-element.38.coef), custom_call_target="tpu_custom_call" | custom-call | flops 20000000 | bytes 1000 | tf_op jit(solution)/shard_map/pallas_call | solution.py:615
  8.0 2.0 %collective-permute-start.2 = (f32[2,176,128]{2,1,0:T(8,128)S(1)}, f32[2,176,128]{2,1,0:T(8,128)S(1)}, u32[]{:S(2)}, u32[]{:S(2)}) collective-permute-start(f32[2,176,128]{2,1,0:T(8,128)S(1)} %get-tuple-element.43), channel_id=1, source_target_pairs={{0,1},{1,2},{2,3},{3,4},{4,5},{5,6},{6,7},{7,0},{8,9},{9,10},{10,1... | collective-permute-start | bytes 540680 | tf_op jit(solution)/shard_map/ppermute | solution.py:601
  10.0 0.1 collective-permute-start.3
  10.1 0.3 collective-permute-done.above
  10.4 0.0 collective-permute-done.1.below
  10.4 0.5 shard_map.61
  10.9 2.9 %collective-permute-start.4 = (f32[48,128]{1,0:T(8,128)S(1)}, f32[48,128]{1,0:T(8,128)S(1)}, u32[]{:S(2)}, u32[]{:S(2)}) collective-permute-start(f32[48,128]{1,0:T(8,128)S(1)} %get-tuple-element.45), channel_id=1, source_target_pairs={{0,1},{1,2},{2,3},{3,4},{4,5},{5,6},{6,7},{7,0},{8,9},{9,10},{10,1... | collective-permute-start | bytes 73736 | tf_op jit(solution)/shard_map/ppermute | solution.py:601
  13.8 0.0 collective-permute-start.5
  13.8 0.0 collective-permute-done.2.before
  13.8 2.9 %collective-permute-done.3.after = f32[2,176,128]{2,1,0:T(8,128)S(1)} collective-permute-done((f32[2,176,128]{2,1,0:T(8,128)S(1)}, f32[2,176,128]{2,1,0:T(8,128)S(1)}, u32[]{:S(2)}, u32[]{:S(2)}) %collective-permute-start.3) | collective-permute-done | bytes 180256 | tf_op jit(solution)/shard_map/ppermute | solution.py:601
  16.6 0.0 collective-permute-done.4.before_c
  16.6 2.2 %collective-permute-done.5.after_c = f32[48,128]{1,0:T(8,128)S(1)} collective-permute-done((f32[48,128]{1,0:T(8,128)S(1)}, f32[48,128]{1,0:T(8,128)S(1)}, u32[]{:S(2)}, u32[]{:S(2)}) %collective-permute-start.5) | collective-permute-done | bytes 24608 | tf_op jit(solution)/shard_map/ppermute | solution.py:601
  18.8 9.5 %shard_map.62 = (f32[11,3,288,128]{3,2,1,0:T(8,128)S(1)}, f32[11,3,288,128]{3,2,1,0:T(8,128)S(1)}, f32[2,3,288,128]{3,2,1,0:T(8,128)S(1)}, f32[3,288,128]{2,1,0:...) custom-call(f32[11,3,288,128]{3,2,1,0:T(8,128)S(1)} %get-tuple-eleme, ...), custom_call_target="tpu_custom_call", output_to_operand_aliasing={{0}: (0, {})} | custom-call | flops 50000000 | bytes 1000 | tf_op jit(solution)/shard_map/pallas_call | solution.py:624
  28.3 1.7 %collective-permute-start.14 = (f32[808,128]{1,0:T(8,128)S(1)}, f32[808,128]{1,0:T(8,128)S(1)}, u32[]{:S(2)}, u32[]{:S(2)}) collective-permute-start(f32[808,128]{1,0:T(8,128)S(1)} %get-tuple-element.59), channel_id=1, source_target_pairs={{0,64},{64,128},{128,192},{192,0},{1,65},{65,129},{129,193},{193,1... | collective-permute-start | bytes 1241096 | tf_op jit(solution)/shard_map/ppermute | solution.py:601
  29.9 0.0 collective-permute-start.6
  29.9 3.0 %collective-permute-start.7 = (f32[4,16,128]{2,1,0:T(8,128)S(1)}, f32[4,16,128]{2,1,0:T(8,128)S(1)}, u32[]{:S(2)}, u32[]{:S(2)}) collective-permute-start(f32[4,16,128]{2,1,0:T(8,128)S(1)} %get-tuple-element.49), channel_id=1, source_target_pairs={{0,56},{8,0},{16,8},{24,16},{32,24},{40,32},{48,40},{56,48},{1,57}... | collective-permute-start | bytes 98312 | tf_op jit(solution)/shard_map/ppermute | solution.py:601
  32.9 1.6 %collective-permute-done.6.above = f32[4,16,128]{2,1,0:T(8,128)S(1)} collective-permute-done((f32[4,16,128]{2,1,0:T(8,128)S(1)}, f32[4,16,128]{2,1,0:T(8,128)S(1)}, u32[]{:S(2)}, u32[]{:S(2)}) %collective-permute-start.6) | collective-permute-done | bytes 32800 | tf_op jit(solution)/shard_map/ppermute | solution.py:601
  34.5 0.0 collective-permute-done.7.below
  34.5 0.1 shard_map.63
  34.6 3.3 %collective-permute-start.8 = (f32[160,128]{1,0:T(8,128)S(1)}, f32[160,128]{1,0:T(8,128)S(1)}, u32[]{:S(2)}, u32[]{:S(2)}) collective-permute-start(f32[160,128]{1,0:T(8,128)S(1)} %get-tuple-element.52), channel_id=1, source_target_pairs={{0,1},{1,2},{2,3},{3,4},{4,5},{5,6},{6,7},{7,0},{8,9},{9,10},{10,1... | collective-permute-start | bytes 245768 | tf_op jit(solution)/shard_map/ppermute | solution.py:601
  37.9 0.0 collective-permute-start.9
  37.9 1.6 %collective-permute-start.13 = (f32[256,256]{1,0:T(8,128)S(1)}, f32[256,256]{1,0:T(8,128)S(1)}, u32[]{:S(2)}, u32[]{:S(2)}) collective-permute-start(f32[256,256]{1,0:T(8,128)S(1)} %get-tuple-element.37.last), channel_id=1, source_target_pairs={{0,64},{64,128},{128,192},{192,0},{1,65},{65,129},{129,193},{193,1... | collective-permute-start | bytes 786440 | tf_op jit(solution)/shard_map/ppermute | solution.py:601
  39.5 0.5 collective-permute-done.8.before
  40.0 2.4 %collective-permute-done.9.after = f32[160,128]{1,0:T(8,128)S(1)} collective-permute-done((f32[160,128]{1,0:T(8,128)S(1)}, f32[160,128]{1,0:T(8,128)S(1)}, u32[]{:S(2)}, u32[]{:S(2)}) %collective-permute-start.9) | collective-permute-done | bytes 81952 | tf_op jit(solution)/shard_map/ppermute | solution.py:601
  42.3 2.2 %shard_map.64 = (f32[360,128]{1,0:T(8,128)S(1)}, f32[192,128]{1,0:T(8,128)S(1)}, f32[192,128]{1,0:T(8,128)S(1)}, f32[2,160,128]{2,1,0:T(8,128)S(1)}, f32[2,2,160,128]{3,2,1,0:T(8,128)S(1)}) custom-call(f32[4,128,128]{2,1,0:T(8,128)S(1)} %get-tuple-element.47.coarse, f32[4,16,128]{2,1,0:T(8,128)S(1)} %collective-permute-done.6.above, ...), custom_call_target="tpu_custom_call" | custom-call | bytes 1000 | tf_op jit(solution)/shard_map/pallas_call | solution.py:638
  44.5 1.6 %collective-permute-start.10 = (f32[360,128]{1,0:T(8,128)S(1)}, f32[360,128]{1,0:T(8,128)S(1)}, u32[]{:S(2)}, u32[]{:S(2)}) collective-permute-start(f32[360,128]{1,0:T(8,128)S(1)} %get-tuple-element.54), channel_id=1, source_target_pairs={{0,64},{64,128},{128,192},{192,0},{1,65},{65,129},{129,193},{193,1... | collective-permute-start | bytes 552968 | tf_op jit(solution)/shard_map/ppermute | solution.py:601
  46.2 1.6 %collective-permute-start.11 = (f32[192,128]{1,0:T(8,128)S(1)}, f32[192,128]{1,0:T(8,128)S(1)}, u32[]{:S(2)}, u32[]{:S(2)}) collective-permute-start(f32[192,128]{1,0:T(8,128)S(1)} %get-tuple-element.55), channel_id=1, source_target_pairs={{0,128},{64,192},{128,0},{192,64},{1,129},{65,193},{129,1},{193,65... | collective-permute-start | bytes 294920 | tf_op jit(solution)/shard_map/ppermute | solution.py:601
  47.7 2.3 %collective-permute-start.12 = (f32[192,128]{1,0:T(8,128)S(1)}, f32[192,128]{1,0:T(8,128)S(1)}, u32[]{:S(2)}, u32[]{:S(2)}) collective-permute-start(f32[192,128]{1,0:T(8,128)S(1)} %get-tuple-element.56), channel_id=1, source_target_pairs={{0,192},{64,0},{128,64},{192,128},{1,193},{65,1},{129,65},{193,129... | collective-permute-start | bytes 294920 | tf_op jit(solution)/shard_map/ppermute | solution.py:601
  50.1 0.0 collective-permute-done.13.last
  50.1 0.0 collective-permute-done.14.main
  50.1 5.1 %shard_map.65 = (f32[2,256,256]{2,1,0:T(8,128)}, f32[3,288,128]{2,1,0:T(8,128)S(1)}, f32[3,288,128]{2,1,0:T(8,128)S(1)}, f32[144,128]{1,0:T(8,128)S(1)}) custom-call(f32[256,256]{1,0:T(8,128)S(1)} %collective-permute-done.13.last, f32[808,128]{1,0:T(8,128)S(1)} %collective-permute-done.14.main, f32[11,3,288,128]{3,2,1,0:T(8,128)S(1)} %get-tuple-element.60.ext, ...), custom_call_target="tpu_custom_call" | custom-call | flops 30000000 | bytes 1000 | tf_op jit(solution)/shard_map/pallas_call | solution.py:645
  55.2 0.0 collective-permute-done.11.two
  55.2 0.0 collective-permute-done.12.three
  55.2 0.0 collective-permute-done.10.one
  55.2 5.6 %shard_map.66 = f32[8,256,256]{2,1,0:T(8,128)} custom-call(f32[360,128]{1,0:T(8,128)S(1)} %collective-permute-done.10.one, f32[192,128]{1,0:T(8,128)S(1)} %collective-permute-done.11.two, f32[192,128]{1,0:T(8,128)S(1)} %collective-permute-done.12.three, f32[2,160,128]{2,1,0:T(8,128)S(1)} %get-tuple-element.57.four, ...), custom_call_target="tpu_custom_call" | custom-call | bytes 1000 | tf_op jit(solution)/shard_map/pallas_call | solution.py:653
Async XLA Ops:
  0.6 1.0 %copy-start = (f32[256,256]{1,0:T(8,128)S(1)}, f32[256,256]{1,0:T(8,128)}, u32[]{:S(2)}) copy-start(f32[256,256]{1,0:T(8,128)} %start.1) | copy-start | bytes 786436
  1.6 0.9 %copy-start.1 = (f32[256,256]{1,0:T(8,128)S(1)}, f32[256,256]{1,0:T(8,128)}, u32[]{:S(2)}) copy-start(f32[256,256]{1,0:T(8,128)} %conduct.1) | copy-start | bytes 786436
  4.3 6.1 %collective-permute-start = (f32[11,16,256]{2,1,0:T(8,128)S(1)}, f32[11,16,256]{2,1,0:T(8,128)S(1)}, u32[]{:S(2)}, u32[]{:S(2)}) collective-permute-start(f32[11,16,256]{2,1,0:T(8,128)S(1)} %get-tuple-element.40), channel_id=1, source_target_pairs={{0,8},{8,16},{16,24},{24,32},{32,40},{40,48},{48,56},{56,0},{1,9},... | collective-permute-start | bytes 540680 | tf_op jit(solution)/shard_map/ppermute | solution.py:601
  4.3 6.1 %collective-permute-start.1 = (f32[11,16,256]{2,1,0:T(8,128)S(1)}, f32[11,16,256]{2,1,0:T(8,128)S(1)}, u32[]{:S(2)}, u32[]{:S(2)}) collective-permute-start(f32[11,16,256]{2,1,0:T(8,128)S(1)} %get-tuple-element.41), channel_id=1, source_target_pairs={{0,56},{8,0},{16,8},{24,16},{32,24},{40,32},{48,40},{56,48},{1,57}... | collective-permute-start | bytes 540680 | tf_op jit(solution)/shard_map/ppermute | solution.py:601
  8.0 5.7 %collective-permute-start.2 = (f32[2,176,128]{2,1,0:T(8,128)S(1)}, f32[2,176,128]{2,1,0:T(8,128)S(1)}, u32[]{:S(2)}, u32[]{:S(2)}) collective-permute-start(f32[2,176,128]{2,1,0:T(8,128)S(1)} %get-tuple-element.43), channel_id=1, source_target_pairs={{0,1},{1,2},{2,3},{3,4},{4,5},{5,6},{6,7},{7,0},{8,9},{9,10},{10,1... | collective-permute-start | bytes 540680 | tf_op jit(solution)/shard_map/ppermute | solution.py:601
  10.0 6.6 %collective-permute-start.3 = (f32[2,176,128]{2,1,0:T(8,128)S(1)}, f32[2,176,128]{2,1,0:T(8,128)S(1)}, u32[]{:S(2)}, u32[]{:S(2)}) collective-permute-start(f32[2,176,128]{2,1,0:T(8,128)S(1)} %get-tuple-element.44), channel_id=1, source_target_pairs={{0,7},{1,0},{2,1},{3,2},{4,3},{5,4},{6,5},{7,6},{8,15},{9,8},{10,9... | collective-permute-start | bytes 540680 | tf_op jit(solution)/shard_map/ppermute | solution.py:601
  10.9 5.7 %collective-permute-start.4 = (f32[48,128]{1,0:T(8,128)S(1)}, f32[48,128]{1,0:T(8,128)S(1)}, u32[]{:S(2)}, u32[]{:S(2)}) collective-permute-start(f32[48,128]{1,0:T(8,128)S(1)} %get-tuple-element.45), channel_id=1, source_target_pairs={{0,1},{1,2},{2,3},{3,4},{4,5},{5,6},{6,7},{7,0},{8,9},{9,10},{10,1... | collective-permute-start | bytes 73736 | tf_op jit(solution)/shard_map/ppermute | solution.py:601
  13.8 5.0 %collective-permute-start.5 = (f32[48,128]{1,0:T(8,128)S(1)}, f32[48,128]{1,0:T(8,128)S(1)}, u32[]{:S(2)}, u32[]{:S(2)}) collective-permute-start(f32[48,128]{1,0:T(8,128)S(1)} %get-tuple-element.46), channel_id=1, source_target_pairs={{0,7},{1,0},{2,1},{3,2},{4,3},{5,4},{6,5},{7,6},{8,15},{9,8},{10,9... | collective-permute-start | bytes 73736 | tf_op jit(solution)/shard_map/ppermute | solution.py:601
  28.3 21.8 %collective-permute-start.14 = (f32[808,128]{1,0:T(8,128)S(1)}, f32[808,128]{1,0:T(8,128)S(1)}, u32[]{:S(2)}, u32[]{:S(2)}) collective-permute-start(f32[808,128]{1,0:T(8,128)S(1)} %get-tuple-element.59), channel_id=1, source_target_pairs={{0,64},{64,128},{128,192},{192,0},{1,65},{65,129},{129,193},{193,1... | collective-permute-start | bytes 1241096 | tf_op jit(solution)/shard_map/ppermute | solution.py:601
  29.9 4.6 %collective-permute-start.6 = (f32[4,16,128]{2,1,0:T(8,128)S(1)}, f32[4,16,128]{2,1,0:T(8,128)S(1)}, u32[]{:S(2)}, u32[]{:S(2)}) collective-permute-start(f32[4,16,128]{2,1,0:T(8,128)S(1)} %get-tuple-element.48), channel_id=1, source_target_pairs={{0,8},{8,16},{16,24},{24,32},{32,40},{40,48},{48,56},{56,0},{1,9},... | collective-permute-start | bytes 98312 | tf_op jit(solution)/shard_map/ppermute | solution.py:601
  29.9 4.6 %collective-permute-start.7 = (f32[4,16,128]{2,1,0:T(8,128)S(1)}, f32[4,16,128]{2,1,0:T(8,128)S(1)}, u32[]{:S(2)}, u32[]{:S(2)}) collective-permute-start(f32[4,16,128]{2,1,0:T(8,128)S(1)} %get-tuple-element.49), channel_id=1, source_target_pairs={{0,56},{8,0},{16,8},{24,16},{32,24},{40,32},{48,40},{56,48},{1,57}... | collective-permute-start | bytes 98312 | tf_op jit(solution)/shard_map/ppermute | solution.py:601
  34.6 5.4 %collective-permute-start.8 = (f32[160,128]{1,0:T(8,128)S(1)}, f32[160,128]{1,0:T(8,128)S(1)}, u32[]{:S(2)}, u32[]{:S(2)}) collective-permute-start(f32[160,128]{1,0:T(8,128)S(1)} %get-tuple-element.52), channel_id=1, source_target_pairs={{0,1},{1,2},{2,3},{3,4},{4,5},{5,6},{6,7},{7,0},{8,9},{9,10},{10,1... | collective-permute-start | bytes 245768 | tf_op jit(solution)/shard_map/ppermute | solution.py:601
  37.9 4.4 %collective-permute-start.9 = (f32[160,128]{1,0:T(8,128)S(1)}, f32[160,128]{1,0:T(8,128)S(1)}, u32[]{:S(2)}, u32[]{:S(2)}) collective-permute-start(f32[160,128]{1,0:T(8,128)S(1)} %get-tuple-element.53), channel_id=1, source_target_pairs={{0,7},{1,0},{2,1},{3,2},{4,3},{5,4},{6,5},{7,6},{8,15},{9,8},{10,9... | collective-permute-start | bytes 245768 | tf_op jit(solution)/shard_map/ppermute | solution.py:601
  37.9 12.2 %collective-permute-start.13 = (f32[256,256]{1,0:T(8,128)S(1)}, f32[256,256]{1,0:T(8,128)S(1)}, u32[]{:S(2)}, u32[]{:S(2)}) collective-permute-start(f32[256,256]{1,0:T(8,128)S(1)} %get-tuple-element.37.last), channel_id=1, source_target_pairs={{0,64},{64,128},{128,192},{192,0},{1,65},{65,129},{129,193},{193,1... | collective-permute-start | bytes 786440 | tf_op jit(solution)/shard_map/ppermute | solution.py:601
  44.5 10.6 %collective-permute-start.10 = (f32[360,128]{1,0:T(8,128)S(1)}, f32[360,128]{1,0:T(8,128)S(1)}, u32[]{:S(2)}, u32[]{:S(2)}) collective-permute-start(f32[360,128]{1,0:T(8,128)S(1)} %get-tuple-element.54), channel_id=1, source_target_pairs={{0,64},{64,128},{128,192},{192,0},{1,65},{65,129},{129,193},{193,1... | collective-permute-start | bytes 552968 | tf_op jit(solution)/shard_map/ppermute | solution.py:601
  46.2 9.0 %collective-permute-start.11 = (f32[192,128]{1,0:T(8,128)S(1)}, f32[192,128]{1,0:T(8,128)S(1)}, u32[]{:S(2)}, u32[]{:S(2)}) collective-permute-start(f32[192,128]{1,0:T(8,128)S(1)} %get-tuple-element.55), channel_id=1, source_target_pairs={{0,128},{64,192},{128,0},{192,64},{1,129},{65,193},{129,1},{193,65... | collective-permute-start | bytes 294920 | tf_op jit(solution)/shard_map/ppermute | solution.py:601
  47.7 7.4 %collective-permute-start.12 = (f32[192,128]{1,0:T(8,128)S(1)}, f32[192,128]{1,0:T(8,128)S(1)}, u32[]{:S(2)}, u32[]{:S(2)}) collective-permute-start(f32[192,128]{1,0:T(8,128)S(1)} %get-tuple-element.56), channel_id=1, source_target_pairs={{0,192},{64,0},{128,64},{192,128},{1,193},{65,1},{129,65},{193,129... | collective-permute-start | bytes 294920 | tf_op jit(solution)/shard_map/ppermute | solution.py:601
